TPU v7x, 8 devices: a whole 2x2x1 slice. The times are simulated.
8 devices in a mesh: dp: 2 (over z, y), tp: 4 (over x, core).
Axes of the slice: x: 2, y: 2, z: 1, core: 2. Of those that a mesh axis runs over, the one named last changes fastest.
Arguments:
- hidden: bfloat16 [6, 192, 8192], P('dp', 'tp'), parts along dimension 0
- positions: int32 [6, 192], P('dp', 'tp'), parts along dimension 0
- doc_ids: int32 [6, 192], P('dp', 'tp'), parts along dimension 0
- norm_gain: bfloat16 [8192], replicated
- w_query: bfloat16 [8192, 8192], P(None, 'tp')
- w_key: bfloat16 [8192, 1024], P(None, 'tp')
- w_value: bfloat16 [8192, 1024], P(None, 'tp')
- w_out: bfloat16 [8192, 8192], P('tp')
- grad_out: bfloat16 [6, 192, 8192], P('dp', 'tp'), parts along dimension 0
Outputs:
- output 1: bfloat16 [6, 192, 8192], P('dp', 'tp'), parts along dimension 0
- output 2: bfloat16 [6, 192, 8192], P('dp', 'tp'), parts along dimension 0
- output 3: float32 [16384], P('dp'), parts along dimension 0
- output 4: float32 [16384, 8192], P('dp', 'tp'), parts along dimension 0
- output 5: float32 [16384, 1024], P('dp', 'tp'), parts along dimension 0
- output 6: float32 [16384, 1024], P('dp', 'tp'), parts along dimension 0
- output 7: float32 [16384, 8192], P(('dp', 'tp')), parts along dimension 0
There are 2 independent parts. A program takes and returns all parts, laid end to end along the dimension named above; an argument that names none is the same for every part.
All inputs are finite; a program needn't handle non-finite values.
Results may differ from a plain program's by a relative error of at most 0.0102642.
Values are sent between devices in bfloat16 or wider.
A program may use at most 1 GiB of HBM per device.

v0:
```python
import jax
import jax.numpy as jnp
from jax import lax
from jax.sharding import PartitionSpec as P

HEAD_DIM = 128
NORM_EPS = 1e-5
ROPE_BASE = 10000.0


def rope_tables(positions):
    inv_freq = ROPE_BASE ** (-jnp.arange(0, HEAD_DIM, 2, dtype=jnp.float32) / HEAD_DIM)
    angles = positions.astype(jnp.float32)[:, :, None] * inv_freq
    return jnp.cos(angles)[:, :, None, :], jnp.sin(angles)[:, :, None, :]


def rotate_pairs(values, cos_tab, sin_tab):
    pair_view = values.reshape(values.shape[:-1] + (HEAD_DIM // 2, 2))
    even_part = pair_view[..., 0]
    odd_part = pair_view[..., 1]
    turned = jnp.stack([even_part * cos_tab - odd_part * sin_tab, even_part * sin_tab + odd_part * cos_tab], axis=-1)
    return turned.reshape(values.shape)


def attend_mask(doc_full):
    seq_len = doc_full.shape[1]
    rows_iota = lax.broadcasted_iota(jnp.int32, (seq_len, seq_len), 0)
    cols_iota = lax.broadcasted_iota(jnp.int32, (seq_len, seq_len), 1)
    return (doc_full[:, :, None] == doc_full[:, None, :]) & (cols_iota <= rows_iota)[None]


def rms_norm(hidden, norm_gain):
    hidden_f = hidden.astype(jnp.float32)
    inv_rms = lax.rsqrt(jnp.mean(hidden_f * hidden_f, axis=-1, keepdims=True) + NORM_EPS)
    return (hidden_f * inv_rms * norm_gain.astype(jnp.float32)).astype(jnp.bfloat16), inv_rms


def norm_backward(hidden, norm_gain, inv_rms, grad_normed):
    hidden_f = hidden.astype(jnp.float32)
    gain_grad_in = grad_normed * norm_gain.astype(jnp.float32)
    grad_gain = jnp.sum(grad_normed * hidden_f * inv_rms, axis=(0, 1))
    mean_term = jnp.mean(gain_grad_in * hidden_f, axis=-1, keepdims=True)
    grad_hidden = inv_rms * gain_grad_in - hidden_f * (inv_rms * inv_rms * inv_rms) * mean_term
    return grad_hidden, grad_gain


def attention_forward(normed_full, w_query, w_key, w_value, cos_tab, sin_tab, allowed):
    batch_rows = normed_full.shape[0]
    seq_len = normed_full.shape[1]
    kv_heads = w_key.shape[1] // HEAD_DIM
    group_size = w_query.shape[1] // w_key.shape[1]
    query_raw = jnp.einsum('bsd,dn->bsn', normed_full, w_query, preferred_element_type=jnp.float32)
    key_raw = jnp.einsum('bsd,dn->bsn', normed_full, w_key, preferred_element_type=jnp.float32)
    value_raw = jnp.einsum('bsd,dn->bsn', normed_full, w_value, preferred_element_type=jnp.float32)
    query_rot = rotate_pairs(query_raw.reshape(batch_rows, seq_len, kv_heads * group_size, HEAD_DIM), cos_tab, sin_tab)
    query_rot = query_rot.astype(jnp.bfloat16).reshape(batch_rows, seq_len, kv_heads, group_size, HEAD_DIM)
    key_rot = rotate_pairs(key_raw.reshape(batch_rows, seq_len, kv_heads, HEAD_DIM), cos_tab, sin_tab).astype(jnp.bfloat16)
    value_rows = value_raw.astype(jnp.bfloat16).reshape(batch_rows, seq_len, kv_heads, HEAD_DIM)
    scores = jnp.einsum('bqhgd,bkhd->bhgqk', query_rot, key_rot, preferred_element_type=jnp.float32) * (HEAD_DIM ** -0.5)
    attn_probs = jax.nn.softmax(jnp.where(allowed[:, None, None], scores, -1e30), axis=-1)
    probs_low = attn_probs.astype(jnp.bfloat16)
    heads_out = jnp.einsum('bhgqk,bkhd->bqhgd', probs_low, value_rows, preferred_element_type=jnp.float32)
    heads_out = heads_out.astype(jnp.bfloat16).reshape(batch_rows, seq_len, kv_heads * group_size * HEAD_DIM)
    return heads_out, (query_rot, key_rot, value_rows, attn_probs, probs_low)


def attention_backward(normed_full, saved_fwd, grad_heads, w_query, w_key, w_value, cos_tab, sin_tab):
    query_rot, key_rot, value_rows, attn_probs, probs_low = saved_fwd
    batch_rows = query_rot.shape[0]
    seq_len = query_rot.shape[1]
    kv_heads = query_rot.shape[2]
    group_size = query_rot.shape[3]
    grad_o = grad_heads.reshape(batch_rows, seq_len, kv_heads, group_size, HEAD_DIM)
    grad_probs = jnp.einsum('bqhgd,bkhd->bhgqk', grad_o, value_rows, preferred_element_type=jnp.float32)
    grad_value = jnp.einsum('bhgqk,bqhgd->bkhd', probs_low, grad_o, preferred_element_type=jnp.float32)
    row_dot = jnp.sum(attn_probs * grad_probs, axis=-1, keepdims=True)
    grad_scores = (attn_probs * (grad_probs - row_dot) * (HEAD_DIM ** -0.5)).astype(jnp.bfloat16)
    grad_query = jnp.einsum('bhgqk,bkhd->bqhgd', grad_scores, key_rot, preferred_element_type=jnp.float32)
    grad_key = jnp.einsum('bhgqk,bqhgd->bkhd', grad_scores, query_rot, preferred_element_type=jnp.float32)
    grad_query = rotate_pairs(grad_query.reshape(batch_rows, seq_len, kv_heads * group_size, HEAD_DIM), cos_tab, -sin_tab)
    grad_query = grad_query.astype(jnp.bfloat16).reshape(batch_rows, seq_len, kv_heads * group_size * HEAD_DIM)
    grad_key = rotate_pairs(grad_key, cos_tab, -sin_tab).astype(jnp.bfloat16).reshape(batch_rows, seq_len, kv_heads * HEAD_DIM)
    grad_value = grad_value.astype(jnp.bfloat16).reshape(batch_rows, seq_len, kv_heads * HEAD_DIM)
    grad_wq = jnp.einsum('bsd,bsn->dn', normed_full, grad_query, preferred_element_type=jnp.float32)
    grad_wk = jnp.einsum('bsd,bsn->dn', normed_full, grad_key, preferred_element_type=jnp.float32)
    grad_wv = jnp.einsum('bsd,bsn->dn', normed_full, grad_value, preferred_element_type=jnp.float32)
    grad_normed = (jnp.einsum('bsn,dn->bsd', grad_query, w_query, preferred_element_type=jnp.float32)
                   + jnp.einsum('bsn,dn->bsd', grad_key, w_key, preferred_element_type=jnp.float32)
                   + jnp.einsum('bsn,dn->bsd', grad_value, w_value, preferred_element_type=jnp.float32))
    return grad_normed, grad_wq, grad_wk, grad_wv


def sum_scatter_rows(partial, tp_size):
    batch_rows = partial.shape[0]
    seq_len = partial.shape[1]
    pieces = partial.astype(jnp.bfloat16).reshape(batch_rows, tp_size, seq_len // tp_size, partial.shape[2])
    received = lax.all_to_all(pieces, 'tp', 1, 1, tiled=True)
    return jnp.sum(received, axis=1, dtype=jnp.float32)


def solution(mesh):
    tp_size = mesh.shape['tp']

    def device_step(hidden, positions, doc_ids, norm_gain, w_query, w_key, w_value, w_out, grad_out):
        normed, inv_rms = rms_norm(hidden, norm_gain)
        normed_full = lax.all_gather(normed, 'tp', axis=1, tiled=True)
        pos_full = lax.all_gather(positions, 'tp', axis=1, tiled=True)
        doc_full = lax.all_gather(doc_ids, 'tp', axis=1, tiled=True)
        cos_tab, sin_tab = rope_tables(pos_full)
        allowed = attend_mask(doc_full)
        heads_out, saved_fwd = attention_forward(normed_full, w_query, w_key, w_value, cos_tab, sin_tab, allowed)
        partial = jnp.einsum('bsn,nd->bsd', heads_out, w_out, preferred_element_type=jnp.float32)
        attn_rows = sum_scatter_rows(partial, tp_size).astype(jnp.bfloat16)
        attn_out = hidden + attn_rows
        grad_full = lax.all_gather(grad_out, 'tp', axis=1, tiled=True)
        grad_w_out = jnp.einsum('bsn,bsd->nd', heads_out, grad_full, preferred_element_type=jnp.float32)
        grad_heads = jnp.einsum('bsd,nd->bsn', grad_full, w_out, preferred_element_type=jnp.float32).astype(jnp.bfloat16)
        grad_normed_part, grad_wq, grad_wk, grad_wv = attention_backward(normed_full, saved_fwd, grad_heads, w_query, w_key, w_value, cos_tab, sin_tab)
        grad_normed = sum_scatter_rows(grad_normed_part, tp_size)
        grad_norm_in, gain_part = norm_backward(hidden, norm_gain, inv_rms, grad_normed)
        grad_gain = lax.psum(gain_part, 'tp')
        grad_hidden = (grad_out.astype(jnp.float32) + grad_norm_in).astype(jnp.bfloat16)
        return (attn_out, grad_hidden, grad_gain, grad_wq, grad_wk, grad_wv, grad_w_out)

    row_spec = P('dp', 'tp', None)
    tok_spec = P('dp', 'tp')
    col_spec = P(None, 'tp')
    return jax.shard_map(
        device_step, mesh=mesh,
        in_specs=(row_spec, tok_spec, tok_spec, P(), col_spec, col_spec, col_spec, P('tp', None), row_spec),
        out_specs=(row_spec, row_spec, P('dp'), P('dp', 'tp'), P('dp', 'tp'), P('dp', 'tp'), P(('dp', 'tp'), None)),
        check_vma=False)
```

profile of v0, /device:TPU:0, one launch (start us, length us, event | category | flops | bytes accessed | tf_op | source)
XLA Modules:
  0.0 635.6 jit_solution(4989669397849953598)
XLA Ops:
  7.2 2.2 fusion.17
  11.4 3.7 fusion.19
  15.9 9.8 %all-gather.1 = s32[4,48,3]{1,2,0:T(4,128)S(1)} all-gather(s32[1,48,3]{1,2,0:T(4,128)S(1)} %bitcast.171), channel_id=1, replica_groups=mesh['dp'=2,'tp'=4] {'tp'}, dimensions={0}, use_global_device_ids=true | all-gather | bytes 2880 | tf_op jit(solution)/shard_map/all_gather | solution.py:107
  25.8 6.6 %all-gather = s32[4,48,3]{1,2,0:T(4,128)S(1)} all-gather(s32[1,48,3]{1,2,0:T(4,128)S(1)} %bitcast.172), channel_id=1, replica_groups=mesh['dp'=2,'tp'=4] {'tp'}, dimensions={0}, use_global_device_ids=true | all-gather | bytes 2880 | tf_op jit(solution)/shard_map/all_gather | solution.py:108
  34.2 45.9 %all-gather.5.cloned.1.call-done = bf16[3,192,8192]{2,1,0:T(8,128)(2,1)} async-done(((bf16[3,48,8192]{2,1,0:T(8,128)(2,1)}), bf16[3,192,8192]{2,1,0:T(8,128)(2,1)}) %all-gather.5.cloned.1.call-update) | async-done | bytes 9437200 | tf_op jit(solution)/shard_map/all_gather | solution.py:106
  80.0 7.5 %fusion.52 = bf16[3,192,256]{2,1,0:T(8,128)(2,1)S(1)} fusion(bf16[3,192,8192]{2,1,0:T(8,128)(2,1)} %all-gather.5.cloned.1.call-done, bf16[8192,256]{1,0:T(8,128)(2,1)} %param.15), kind=kOutput, calls=%fused_computation.69 | convolution fusion | flops 2416066560 | bytes 13926400 | tf_op jit(solution)/shard_map/bsd,dn->bsn/dot_general | solution.py:54
  87.6 10.7 %fusion.32 = f32[3,192,256]{1,2,0:T(8,128)S(1)} fusion(bf16[3,192,8192]{2,1,0:T(8,128)(2,1)} %all-gather.5.cloned.1.call-done, bf16[8192,256]{1,0:T(8,128)(2,1)} %param.14), kind=kOutput, calls=%fused_computation.46 | convolution fusion | flops 2415919104 | bytes 14221312 | tf_op jit(solution)/shard_map/bsd,dn->bsn/dot_general | solution.py:53
  102.2 41.2 %all-gather.7.cloned.1.call-done = bf16[3,192,8192]{2,1,0:T(8,128)(2,1)} async-done(((bf16[3,48,8192]{2,1,0:T(8,128)(2,1)}), bf16[3,192,8192]{2,1,0:T(8,128)(2,1)}) %all-gather.7.cloned.1.call-update) | async-done | bytes 9437200 | tf_op jit(solution)/shard_map/all_gather | solution.py:115
  143.4 24.8 %fusion.40 = bf16[3,192,2048]{2,1,0:T(8,128)(2,1)S(1)} fusion(bf16[3,192,8192]{2,1,0:T(8,128)(2,1)} %all-gather.7.cloned.1.call-done, bf16[2048,8192]{1,0:T(8,128)(2,1)} %param.16), kind=kOutput, calls=%fused_computation.60 | convolution fusion | flops 19328532480 | bytes 45350912 | tf_op jit(solution)/shard_map/bsd,nd->bsn/dot_general | solution.py:117
  168.9 34.2 %fusion.8 = f32[3,192,2048]{1,2,0:T(8,128)} fusion(bf16[3,192,8192]{2,1,0:T(8,128)(2,1)} %all-gather.5.cloned.1.call-done, bf16[8192,2048]{1,0:T(8,128)(2,1)} %param.13), kind=kOutput, calls=%fused_computation.10 | convolution fusion | flops 19327352832 | bytes 47710208 | tf_op jit(solution)/shard_map/bsd,dn->bsn/dot_general | solution.py:52
  203.1 8.2 %reshape_reshape.10 = f32[3,192,16,64,2]{1,4,3,2,0:T(2,128)} reshape(f32[3,192,2048]{1,2,0:T(8,128)} %fusion.8) | data formatting | bytes 9437184 | tf_op jit(solution)/shard_map/reshape;reshape | solution.py:18
  211.3 10.3 %subtract_convert_fusion.1 = (bf16[3,192,16,64,1]{1,4,3,2,0:T(2,128)(2,1)S(1)}, bf16[3,192,16,64,1]{1,4,3,2,0:T(2,128)(2,1)S(1)}) fusion(f32[3,192,16,64,2]{1,4,3,2,0:T(2,128)} %reshape_reshape.10, f32[3,192,64]{1,2,0:T(8,128)S(1)} %get-tuple-element.22, f32[3,192,64]{1,2,0:T(8,128)S(1)} %get-tuple-element.23), kind=kLoop, calls=%fused_computation.59 | loop fusion | flops 4718592 | bytes 7372800 | tf_op jit(solution)/shard_map/convert.5
  221.5 8.2 %pad_maximum_fusion = bf16[3,192,16,64,2]{1,4,3,2,0:T(2,128)(2,1)S(1)} fusion(bf16[3,192,16,64,1]{1,4,3,2,0:T(2,128)(2,1)S(1)} %get-tuple-element.12, bf16[3,192,16,64,1]{1,4,3,2,0:T(2,128)(2,1)S(1)} %get-tuple-element.11), kind=kLoop, calls=%fused_computation.54 | loop fusion | flops 4718592 | bytes 4718592 | tf_op jit(solution)/shard_map/stack | solution.py:21
  229.8 5.1 copy.92
  234.8 4.7 copy.94
  239.6 9.0 %fusion.79 = (f32[3,2,8,192]{3,2,1,0:T(8,128)S(1)}, f32[3,2,8,192,192]{3,4,2,1,0:T(8,128)}) fusion(pred[3,192,192]{1,2,0:T(8,128)(4,1)S(1)} %compare_and_fusion, bf16[3,192,2,128,1]{3,1,4,2,0:T(8,128)(2,1)S(1)} %copy.120, bf16[3,192,2,8,128]{4,1,3,2,0:T(8,128)(2,1)} %copy.94), kind=kOutput, calls=%fused_computation.104 | convolution fusion | flops 460062912 | bytes 9879552 | tf_op jit(solution)/shard_map/sub | solution.py:60
  248.5 7.1 %fusion.76 = bf16[3,2,8,192,192]{3,4,2,1,0:T(8,128)(2,1)} fusion(f32[3,2,8,192,192]{3,4,2,1,0:T(8,128)} %get-tuple-element.27, f32[3,2,8,192]{3,2,1,0:T(8,128)S(1)} %get-tuple-element.26), kind=kLoop, calls=%fused_computation.101 | loop fusion | flops 3538944 | bytes 10653696 | tf_op jit(solution)/shard_map/convert_element_type | solution.py:61
  255.7 7.8 %copy.113 = bf16[3,2,8,192,192]{4,2,3,1,0:T(8,128)(2,1)} copy(bf16[3,2,8,192,192]{3,4,2,1,0:T(8,128)(2,1)} %fusion.76) | data formatting | bytes 7077888 | tf_op jit(solution)/shard_map/convert_element_type | solution.py:61
  263.4 5.6 convert_bitcast_fusion
  269.0 5.2 fusion.45
  274.2 14.1 %fusion.51 = f32[3,192,2,128]{3,1,2,0:T(8,128)S(1)} fusion(bf16[3,192,2,8,128]{4,1,3,2,0:T(8,128)(2,1)} %copy.94, f32[3,2,192,192,8]{3,2,4,1,0:T(8,128)} %fusion.45, f32[3,2,8,192,192]{3,4,2,1,0:T(8,128)} %get-tuple-element.27, f32[3,2,8,192]{3,2,1,0:T(8,128)S(1)} %get-tuple-element.26), kind=kOutput, calls=%fused_computation.68 | convolution fusion | flops 465380544 | bytes 17141760 | tf_op jit(solution)/shard_map/bhgqk,bqhgd->bkhd/dot_general | solution.py:79
  288.4 16.1 %fusion.47 = f32[3,192,2,8,128]{4,1,3,2,0:T(8,128)} fusion(bf16[3,192,2,128,1]{3,1,4,2,0:T(8,128)(2,1)} %copy-done.11, f32[3,2,192,192,8]{3,2,4,1,0:T(8,128)} %fusion.45, f32[3,2,8,192,192]{3,4,2,1,0:T(8,128)} %get-tuple-element.27, f32[3,2,8,192]{3,2,1,0:T(8,128)S(1)} %get-tuple-element.26), kind=kOutput, calls=%fused_computation.66 | convolution fusion | flops 465380544 | bytes 19206144 | tf_op jit(solution)/shard_map/bhgqk,bkhd->bqhgd/dot_general | solution.py:78
  304.5 4.7 fusion.58
  310.7 2.4 reshape.96
  316.6 6.6 %copy.103 = f32[3,192,2,8,128]{1,3,2,4,0:T(8,128)} copy(f32[3,192,2,8,128]{4,1,3,2,0:T(8,128)} %fusion.47) | data formatting | bytes 9437184 | tf_op jit(solution)/shard_map/bhgqk,bkhd->bqhgd/transpose | solution.py:78
  323.2 3.6 fusion.77
  326.8 6.7 %subtract_convert_fusion = (bf16[3,192,16,64,1]{1,4,3,2,0:T(2,128)(2,1)S(1)}, bf16[3,192,16,64,1]{1,4,3,2,0:T(2,128)(2,1)S(1)}) fusion(f32[3,192,16,64,1]{1,2,4,3,0:T(8,128)S(1)} %get-tuple-element.14, f32[3,192,16,64,1]{1,2,4,3,0:T(8,128)S(1)} %get-tuple-element.13, f32[3,192,64]{1,2,0:T(8,128)S(1)} %copy-done.7, f32[3,192,64]{1,2,0:T(8,128)S(1)} %get-tuple-element.23), kind=kLoop, calls=%fused_computation.57 | loop fusion | flops 4718592 | bytes 7372800 | tf_op jit(solution)/shard_map/convert.3
  333.5 7.8 %pad_maximum_fusion.1 = bf16[3,192,16,64,2]{1,4,3,2,0:T(2,128)(2,1)S(1)} fusion(bf16[3,192,16,64,1]{1,4,3,2,0:T(2,128)(2,1)S(1)} %get-tuple-element.10, bf16[3,192,16,64,1]{1,4,3,2,0:T(2,128)(2,1)S(1)} %get-tuple-element.9), kind=kLoop, calls=%fused_computation.55 | loop fusion | flops 4718592 | bytes 4718592 | tf_op jit(solution)/shard_map/stack | solution.py:21
  341.3 4.4 convert_element_type.88
  345.8 27.2 %fusion.10 = bf16[3,192,8192]{2,1,0:T(8,128)(2,1)} fusion(bf16[3,192,2048]{2,1,0:T(8,128)(2,1)} %reshape.96, bf16[2048,8192]{1,0:T(8,128)(2,1)} %param.16), kind=kOutput, calls=%fused_computation.14 | convolution fusion | flops 19332071424 | bytes 45350912 | tf_op jit(solution)/shard_map/bsn,nd->bsd/dot_general | solution.py:112
  372.9 8.4 %copy.98 = bf16[3,4,48,8192]{3,2,0,1:T(8,128)(2,1)} copy(bf16[3,4,48,8192]{3,2,1,0:T(8,128)(2,1)} %bitcast.163) | data formatting | bytes 18874368 | tf_op jit(solution)/shard_map/reshape | solution.py:96
  381.4 6.2 all-to-all-start
  387.6 12.8 %fusion.30 = f32[3,192,8192]{2,1,0:T(8,128)} fusion(bf16[3,192,256]{1,2,0:T(8,128)(2,1)S(1)} %convert_element_type.89, bf16[8192,256]{1,0:T(8,128)(2,1)} %param.14), kind=kOutput, calls=%fused_computation.44 | convolution fusion | flops 2415919104 | bytes 23363584 | tf_op jit(solution)/shard_map/bsn,dn->bsd/dot_general | solution.py:88
  400.5 33.6 %fusion.6 = f32[3,192,8192]{2,1,0:T(8,128)} fusion(bf16[3,192,2048]{1,2,0:T(8,128)(2,1)S(1)} %copy-done.4, bf16[8192,2048]{1,0:T(8,128)(2,1)} %param.13), kind=kOutput, calls=%fused_computation.8 | convolution fusion | flops 19327352832 | bytes 54788096 | tf_op jit(solution)/shard_map/bsn,dn->bsd/dot_general | solution.py:87
  434.1 17.7 %add_convert_fusion = bf16[3,192,8192]{2,1,0:T(8,128)(2,1)} fusion(f32[3,192,8192]{2,1,0:T(8,128)} %fusion.6, f32[3,192,8192]{2,1,0:T(8,128)} %fusion.30, bf16[8192,256]{1,0:T(8,128)(2,1)S(1)} %copy-done.3, bf16[3,2,24,8,128]{4,3,2,1,0:T(8,128)(2,1)S(1)} %copy-done.8), kind=kOutput, calls=%fused_computation.13 | convolution fusion | flops 2430074880 | bytes 51675136 | tf_op jit(solution)/shard_map/bsn,dn->bsd/dot_general | solution.py:89
  451.7 8.5 %copy.115 = bf16[3,4,48,8192]{3,2,0,1:T(8,128)(2,1)} copy(bf16[3,4,48,8192]{3,2,1,0:T(8,128)(2,1)} %bitcast.158) | data formatting | bytes 18874368 | tf_op jit(solution)/shard_map/reshape | solution.py:96
  460.2 10.6 %convolution_bitcast_fusion.2 = f32[8192,256]{1,0:T(8,128)} fusion(bf16[3,192,8192]{2,1,0:T(8,128)(2,1)} %all-gather.5.cloned.1.call-done, bf16[3,2,24,8,128]{4,3,2,1,0:T(8,128)(2,1)S(1)} %copy-done.8), kind=kOutput, calls=%fused_computation.15 | convolution fusion | flops 2415919104 | bytes 18120704 | tf_op jit(solution)/shard_map/bsd,bsn->dn/dot_general | solution.py:86
  470.8 20.8 %all-to-all-done = bf16[3,4,48,8192]{3,2,0,1:T(8,128)(2,1)} async-done(((bf16[3,4,48,8192]{3,2,0,1:T(8,128)(2,1)}), bf16[3,4,48,8192]{3,2,0,1:T(8,128)(2,1)}, u32[]{:S(2)}, u32[]{:S(2)}) %all-to-all-start) | async-done | bytes 9437216 | tf_op jit(solution)/shard_map/all_to_all | solution.py:97
  491.7 5.8 all-to-all-start.1
  497.5 10.8 %convolution_bitcast_fusion.3 = f32[8192,256]{1,0:T(8,128)} fusion(bf16[3,192,8192]{2,1,0:T(8,128)(2,1)} %all-gather.5.cloned.1.call-done, bf16[3,192,256]{1,2,0:T(8,128)(2,1)S(1)} %convert_element_type.89), kind=kOutput, calls=%fused_computation.16 | convolution fusion | flops 2415919104 | bytes 18120704 | tf_op jit(solution)/shard_map/bsd,bsn->dn/dot_general | solution.py:85
  508.2 35.1 %convolution_bitcast_fusion = f32[2048,8192]{1,0:T(8,128)} fusion(bf16[3,192,2048]{2,1,0:T(8,128)(2,1)S(1)} %copy-done.6, bf16[3,192,8192]{2,1,0:T(8,128)(2,1)} %all-gather.7.cloned.1.call-done), kind=kOutput, calls=%fused_computation.2 | convolution fusion | flops 19327352832 | bytes 78905344 | tf_op jit(solution)/shard_map/bsn,bsd->nd/dot_general | solution.py:116
  543.3 35.9 %convolution_bitcast_fusion.1 = f32[8192,2048]{1,0:T(8,128)} fusion(bf16[3,192,8192]{2,1,0:T(8,128)(2,1)} %all-gather.5.cloned.1.call-done, bf16[3,192,2048]{1,2,0:T(8,128)(2,1)S(1)} %copy-done.5), kind=kOutput, calls=%fused_computation.3 | convolution fusion | flops 19327352832 | bytes 78905344 | tf_op jit(solution)/shard_map/bsd,bsn->dn/dot_general | solution.py:84
  579.3 7.7 %reduce_sum.68 = bf16[3,48,8192]{2,1,0:T(8,128)(2,1)} reduce(bf16[3,4,48,8192]{3,2,0,1:T(8,128)(2,1)} %all-to-all-done, bf16[]{:T(256)} %constant.23.clone.1), dimensions={1}, to_apply=%region_3.4 | reduce | flops 3538944 | bytes 11796482 | tf_op jit(solution)/shard_map/reduce_sum | solution.py:98
  587.0 3.6 add.48
  590.6 10.9 %all-to-all-done.1 = bf16[3,4,48,8192]{3,2,0,1:T(8,128)(2,1)} async-done(((bf16[3,4,48,8192]{3,2,0,1:T(8,128)(2,1)}), bf16[3,4,48,8192]{3,2,0,1:T(8,128)(2,1)}, u32[]{:S(2)}, u32[]{:S(2)}) %all-to-all-start.1) | async-done | bytes 9437216 | tf_op jit(solution)/shard_map/all_to_all | solution.py:97
  601.5 6.1 convert_reduce_fusion
  611.6 10.9 %psum.7 = f32[8192]{0:T(1024)} all-reduce(f32[8192]{0:T(1024)S(1)} %get-tuple-element.7), channel_id=1, replica_groups=mesh['dp'=2,'tp'=4] {'tp'}, use_global_device_ids=true, to_apply=%region_8.9 | all-reduce | flops 8192 | bytes 65536 | tf_op jit(solution)/shard_map/psum | solution.py:121
  622.4 6.1 fusion.23
  (63 shorter events, 18.1 us)
Async XLA Ops:
  7.2 72.9 %all-gather.5.cloned.1.call-start = ((), (), s32[]{:S(2)}) async-start(), calls=%async_computation.2 | async-start | bytes 11796480 | tf_op jit(solution)/shard_map/all_gather | solution.py:106
  10.0 0.7 copy-start.12
  10.8 0.6 copy-start.9
  11.4 4.5 copy-start.15
  11.4 14.4 %copy-start.16 = (s32[3,48]{1,0:T(4,128)S(1)}, s32[3,48]{1,0:T(4,128)}, u32[]{:S(2)}) copy-start(s32[3,48]{1,0:T(4,128)} %param.11) | copy-start | bytes 1732
  15.2 128.2 %all-gather.7.cloned.1.call-start = ((), (), s32[]{:S(2)}) async-start(), calls=%async_computation.3 | async-start | bytes 11796480 | tf_op jit(solution)/shard_map/all_gather | solution.py:115
  102.2 137.4 %copy-start.11 = (bf16[3,192,2,128,1]{3,1,4,2,0:T(8,128)(2,1)}, bf16[3,192,2,128,1]{3,1,4,2,0:T(8,128)(2,1)S(1)}, u32[]{:S(2)}) copy-start(bf16[3,192,2,128,1]{3,1,4,2,0:T(8,128)(2,1)S(1)} %copy.120) | copy-start | bytes 884740
  304.5 4.7 copy-start.2
  310.7 3.6 copy-start.7
  381.4 110.3 %all-to-all-start = ((bf16[3,4,48,8192]{3,2,0,1:T(8,128)(2,1)}), bf16[3,4,48,8192]{3,2,0,1:T(8,128)(2,1)}, u32[]{:S(2)}, u32[]{:S(2)}) async-start(bf16[3,4,48,8192]{3,2,0,1:T(8,128)(2,1)} %copy.98), calls=%async_computation | async-start | bytes 18874368 | tf_op jit(solution)/shard_map/all_to_all | solution.py:97
  387.6 12.8 %copy-start.4 = (bf16[3,192,2048]{1,2,0:T(8,128)(2,1)S(1)}, bf16[3,192,2048]{1,2,0:T(8,128)(2,1)}, u32[]{:S(2)}) copy-start(bf16[3,192,2048]{1,2,0:T(8,128)(2,1)} %convert_element_type.88) | copy-start | bytes 7077892
  400.4 33.6 %copy-start.3 = (bf16[8192,256]{1,0:T(8,128)(2,1)S(1)}, bf16[8192,256]{1,0:T(8,128)(2,1)}, u32[]{:S(2)}) copy-start(bf16[8192,256]{1,0:T(8,128)(2,1)} %param.15) | copy-start | bytes 12582916
  400.5 33.6 %copy-start.8 = (bf16[3,2,24,8,128]{4,3,2,1,0:T(8,128)(2,1)S(1)}, bf16[3,2,24,8,128]{4,3,2,1,0:T(8,128)(2,1)}, u32[]{:S(2)}) copy-start(bf16[3,2,24,8,128]{4,3,2,1,0:T(8,128)(2,1)} %fusion.58) | copy-start | bytes 884740
  491.7 109.8 %all-to-all-start.1 = ((bf16[3,4,48,8192]{3,2,0,1:T(8,128)(2,1)}), bf16[3,4,48,8192]{3,2,0,1:T(8,128)(2,1)}, u32[]{:S(2)}, u32[]{:S(2)}) async-start(bf16[3,4,48,8192]{3,2,0,1:T(8,128)(2,1)} %copy.115), calls=%async_computation.1 | async-start | bytes 18874368 | tf_op jit(solution)/shard_map/all_to_all | solution.py:97
  497.4 10.8 %copy-start.6 = (bf16[3,192,2048]{2,1,0:T(8,128)(2,1)S(1)}, bf16[3,192,2048]{2,1,0:T(8,128)(2,1)}, u32[]{:S(2)}) copy-start(bf16[3,192,2048]{2,1,0:T(8,128)(2,1)} %reshape.96) | copy-start | bytes 7077892
  508.2 35.1 %copy-start.5 = (bf16[3,192,2048]{1,2,0:T(8,128)(2,1)S(1)}, bf16[3,192,2048]{1,2,0:T(8,128)(2,1)}, u32[]{:S(2)}) copy-start(bf16[3,192,2048]{1,2,0:T(8,128)(2,1)} %convert_element_type.88) | copy-start | bytes 7077892
  579.3 7.7 %copy-start = (bf16[3,48,8192]{2,1,0:T(8,128)(2,1)S(1)}, bf16[3,48,8192]{2,1,0:T(8,128)(2,1)}, u32[]{:S(2)}) copy-start(bf16[3,48,8192]{2,1,0:T(8,128)(2,1)} %param.9) | copy-start | bytes 7077892
  590.6 19.1 %copy-start.10 = (f32[8192]{0:T(1024)S(1)}, f32[8192]{0:T(1024)}, u32[]{:S(2)}) copy-start(f32[8192]{0:T(1024)} %copy-done.9) | copy-start | bytes 98308
  590.6 19.1 %copy-start.13 = (f32[3,48]{1,0:T(4,128)S(1)}, f32[3,48]{1,0:T(4,128)}, u32[]{:S(2)}) copy-start(f32[3,48]{1,0:T(4,128)} %copy-done.12) | copy-start | bytes 1732
  607.6 2.1 copy-start.1
  609.7 12.7 %copy-start.14 = (f32[3,48]{1,0:T(4,128)S(1)}, f32[3,48]{1,0:T(4,128)}, u32[]{:S(2)}) copy-start(f32[3,48]{1,0:T(4,128)} %get-tuple-element.24) | copy-start | bytes 1732
Sparse Core Ops, SparseCore 0:
  15.3 64.7 all-gather.4
  81.6 61.7 all-gather.6
where the time goes:
time: 641 us; the launch traced here: 636 us
  matrix products  316 us (49%)
  waiting for transfers between devices  120 us (19%)
  other arithmetic  78.3 us (12%)
  local copies, waits for them, and re-layouts  68.3 us (11%)
  blocking collectives  27.2 us (4%)
  between operations  14.6 us (2%)
  starting transfers between devices  12.1 us (2%)
    all_gather x1, waiting for transfers between devices, device_step(): normed_full = lax.all_gather(normed, 'tp', axis=1, tiled=True)  45.9 us
    all_gather x1, waiting for transfers between devices, device_step(): grad_full = lax.all_gather(grad_out, 'tp', axis=1, tiled=True)  41.2 us
    dot_general x1, matrix products, attention_backward(): jnp.einsum('bsd,bsn->dn', normed_full, grad_query, preferred_element_type...  35.9 us
    dot_general x1, matrix products, device_step(): jnp.einsum('bsn,bsd->nd', heads_out, grad_full, preferred_element_type=jn...  35.1 us
    dot_general x1, matrix products, attention_forward(): jnp.einsum('bsd,dn->bsn', normed_full, w_query, preferred_element_type=jn...  34.2 us
    dot_general x1, matrix products, attention_backward(): jnp.einsum('bsn,dn->bsd', grad_query, w_query, preferred_element_type=jnp...  33.6 us
    all_to_all x2, waiting for transfers between devices, sum_scatter_rows(): received = lax.all_to_all(pieces, 'tp', 1, 1, tiled=True)  31.7 us
    dot_general x1, matrix products, device_step(): jnp.einsum('bsn,nd->bsd', heads_out, w_out, preferred_element_type=jnp.fl...  27.2 us
  transfers between devices with their start and end apart: 4, of which 4 were waited for; matrix products, arithmetic and copies ran while one was open for 31% of the time, Pallas kernels for 0%

commit v1 on v0

v1 whole, which is shorter than its diff:
```python
import functools

import jax
import jax.numpy as jnp
from jax import lax
from jax.experimental import pallas as pl
from jax.experimental.pallas import tpu as pltpu
from jax.sharding import PartitionSpec as P


HEAD_DIM = 128
NORM_EPS = 1e-5
ROPE_BASE = 10000.0
BF16 = jnp.bfloat16
F32 = jnp.float32
ANY = pl.BlockSpec(memory_space=pl.ANY)
NN = (((1,), (0,)), ((), ()))
NT = (((1,), (1,)), ((), ()))
TN = (((0,), (0,)), ((), ()))


def dot(a, b, dims=NN):
    return lax.dot_general(a, b, dims, preferred_element_type=F32)


def const_spec(shape):
    return pl.BlockSpec(shape, lambda *_: (0,) * len(shape), pipeline_mode=pl.Buffered(1))


def params(mib, *semantics):
    return pltpu.CompilerParams(dimension_semantics=semantics or ("arbitrary",), vmem_limit_bytes=mib << 20)


def cost(flops, moved):
    return pl.CostEstimate(flops=int(flops), bytes_accessed=int(moved), transcendentals=0)


def swap_pairs(x):
    lane = lax.broadcasted_iota(jnp.int32, x.shape, x.ndim - 1)
    return jnp.where(lane % 2 == 0, pltpu.roll(x, x.shape[-1] - 1, x.ndim - 1), pltpu.roll(x, 1, x.ndim - 1))


def qkv_kernel(q_steps, ha, hb, gain, cos, sin, wq, wk, wv, n_out, inv_out, q_out, k_out, v_out, hs, ks, vs, sem):
    step = pl.program_id(0)
    half = ha.shape[0]

    @pl.when(step == 0)
    def _():
        loads = [pltpu.make_async_copy(ha, hs.at[pl.ds(0, half)], sem.at[0]),
                 pltpu.make_async_copy(hb, hs.at[pl.ds(half, half)], sem.at[1])]
        for c in loads:
            c.start()
        pltpu.make_async_copy(wk, ks, sem.at[2]).start()
        pltpu.make_async_copy(wv, vs, sem.at[3]).start()
        for c in loads:
            c.wait()

        def rows(i, _):
            at = pl.ds(pl.multiple_of(i * 16, 16), 16)
            x = hs[at, :].astype(F32)
            inv = lax.rsqrt(jnp.mean(x * x, axis=-1, keepdims=True) + NORM_EPS)
            n_out[at, :] = (x * inv * gain[...].astype(F32)).astype(BF16)
            inv_out[at, :] = jnp.broadcast_to(inv, (16, 128))
            return 0

        lax.fori_loop(0, 2 * half // 16, rows, 0)

    def rotated(raw):
        parts = []
        for j in range(raw.shape[1] // HEAD_DIM):
            x = raw[:, j * HEAD_DIM:(j + 1) * HEAD_DIM]
            parts.append((x * cos[...] + swap_pairs(x) * sin[...]).astype(BF16))
        return jnp.concatenate(parts, axis=1)

    @pl.when(step < q_steps)
    def _():
        q_out[...] = rotated(dot(n_out[...], wq[...]))

    @pl.when(step == q_steps)
    def _():
        pltpu.make_async_copy(wk, ks, sem.at[2]).wait()
        k_out[...] = rotated(dot(n_out[...], ks[...]))

    @pl.when(step == q_steps + 1)
    def _():
        pltpu.make_async_copy(wv, vs, sem.at[3]).wait()
        v_out[...] = dot(n_out[...], vs[...]).astype(BF16)


def qkv(ha, hb, gain, cos, sin, wq, wk, wv):
    half, width = ha.shape
    tok = 2 * half
    nq, nk = wq.shape[1], wk.shape[1]
    blk = 256
    q_steps = nq // blk
    return pl.pallas_call(
        functools.partial(qkv_kernel, q_steps), name="qkv", grid=(q_steps + 2,),
        in_specs=[ANY, ANY, const_spec((1, width)), const_spec((tok, HEAD_DIM)), const_spec((tok, HEAD_DIM)),
                  pl.BlockSpec((width, blk), lambda i: (0, jnp.minimum(i, q_steps - 1))), ANY, ANY],
        out_specs=[const_spec((tok, width)), const_spec((tok, 128)),
                   pl.BlockSpec((tok, blk), lambda i: (0, jnp.minimum(i, q_steps - 1))),
                   const_spec((tok, nk)), const_spec((tok, nk))],
        out_shape=[jax.ShapeDtypeStruct((tok, width), BF16), jax.ShapeDtypeStruct((tok, 128), F32),
                   jax.ShapeDtypeStruct((tok, nq), BF16), jax.ShapeDtypeStruct((tok, nk), BF16),
                   jax.ShapeDtypeStruct((tok, nk), BF16)],
        scratch_shapes=[pltpu.VMEM((tok, width), BF16), pltpu.VMEM((width, nk), BF16), pltpu.VMEM((width, nk), BF16),
                        pltpu.SemaphoreType.DMA((4,))],
        compiler_params=params(60), cost_estimate=cost(2 * tok * width * (nq + 2 * nk), 2 * width * (nq + 2 * nk)),
    )(ha, hb, gain, cos, sin, wq, wk, wv)


def heads_grad_kernel(ga, gb, w, out, gs, sem):
    half = ga.shape[0]

    @pl.when(pl.program_id(0) == 0)
    def _():
        loads = [pltpu.make_async_copy(ga, gs.at[pl.ds(0, half)], sem.at[0]),
                 pltpu.make_async_copy(gb, gs.at[pl.ds(half, half)], sem.at[1])]
        for c in loads:
            c.start()
        for c in loads:
            c.wait()

    out[...] = dot(gs[...], w[...], NT).astype(BF16)


def heads_grad(ga, gb, w_out):
    half, width = ga.shape
    tok = 2 * half
    n = w_out.shape[0]
    blk = 256
    return pl.pallas_call(
        heads_grad_kernel, name="heads_grad", grid=(n // blk,),
        in_specs=[ANY, ANY, pl.BlockSpec((blk, width), lambda i: (i, 0))],
        out_specs=pl.BlockSpec((tok, blk), lambda i: (0, i)),
        out_shape=jax.ShapeDtypeStruct((tok, n), BF16),
        scratch_shapes=[pltpu.VMEM((tok, width), BF16), pltpu.SemaphoreType.DMA((2,))],
        compiler_params=params(60), cost_estimate=cost(2 * tok * width * n, 2 * width * n),
    )(ga, gb, w_out)


def by_head(a_ref, b_ref, group):
    def flat(r):
        v = r[...]
        return v.reshape(v.shape[0] * v.shape[2], v.shape[3])

    full = jnp.concatenate([flat(a_ref), flat(b_ref)], axis=0)
    return jnp.concatenate([full[:, h * HEAD_DIM:(h + 1) * HEAD_DIM] for h in range(group)], axis=0)


def put(ref, value):
    ref[...] = value.reshape(ref.shape)


def attend_kernel(group, qa, qb, ka, kb, va, vb, mask, oa, ob):
    q = by_head(qa, qb, group)
    k = by_head(ka, kb, 1)
    v = by_head(va, vb, 1)
    seq = k.shape[0]
    scores = dot(q, k, NT) * (HEAD_DIM ** -0.5)
    scores = jnp.where((mask[...] > 0), scores.reshape(group, seq, seq), -1e30).reshape(group * seq, seq)
    top = jnp.max(scores, axis=-1, keepdims=True)
    e = jnp.exp(scores - top)
    probs = (e / jnp.sum(e, axis=-1, keepdims=True)).astype(BF16)
    o = dot(probs, v).astype(BF16)
    o = jnp.concatenate([o[h * seq:(h + 1) * seq] for h in range(group)], axis=1)
    put(oa, o[:seq // 2])
    put(ob, o[seq // 2:])


def head_specs(slots, rows, wide):
    return pl.BlockSpec((slots, 1, rows, wide), lambda r, h: (0, r, 0, h))


def attend(qa, qb, ka, kb, va, vb, mask):
    slots, batch, rows, nq = qa.shape
    kv = ka.shape[3] // HEAD_DIM
    group = nq // ka.shape[3]
    seq = 2 * slots * rows
    qs, ks = head_specs(slots, rows, group * HEAD_DIM), head_specs(slots, rows, HEAD_DIM)
    return pl.pallas_call(
        functools.partial(attend_kernel, group), name="attend", grid=(batch, kv),
        in_specs=[qs, qs, ks, ks, ks, ks, pl.BlockSpec((1, seq, seq), lambda r, h: (r, 0, 0))],
        out_specs=[qs, qs], out_shape=[jax.ShapeDtypeStruct(qa.shape, BF16)] * 2,
        compiler_params=params(60, "arbitrary", "arbitrary"),
        cost_estimate=cost(batch * kv * group * seq * seq * HEAD_DIM * 40, 4 * qa.size * 2),
    )(qa, qb, ka, kb, va, vb, mask)


def attend_back_kernel(group, qa, qb, ka, kb, va, vb, ga, gb, mask, ca, cb, sa, sb, dqa, dqb, dka, dkb, dva, dvb):
    q = by_head(qa, qb, group)
    g = by_head(ga, gb, group)
    k = by_head(ka, kb, 1)
    v = by_head(va, vb, 1)
    cos, sin = by_head(ca, cb, 1), by_head(sa, sb, 1)
    seq = k.shape[0]
    scale = HEAD_DIM ** -0.5
    scores = jnp.where(mask[0] > 0, dot(k, q, NT) * scale, -1e30)
    e = jnp.exp(scores - jnp.max(scores, axis=0, keepdims=True))
    probs = e / jnp.sum(e, axis=0, keepdims=True)
    gp = dot(v, g, NT)
    dots = jnp.sum(probs * gp, axis=0, keepdims=True)
    ds = (probs * (gp - dots) * scale).astype(BF16)
    dv = dot(probs.astype(BF16), g).astype(BF16)
    dk = dot(ds, q)
    dq = dot(ds, k, TN)

    def unrotated(x):
        return (x * cos - swap_pairs(x) * sin).astype(BF16)

    dq = jnp.concatenate([unrotated(dq[h * seq:(h + 1) * seq]) for h in range(group)], axis=1)
    dk = unrotated(dk)
    for lo, hi, value in ((dqa, dqb, dq), (dka, dkb, dk), (dva, dvb, dv)):
        put(lo, value[:seq // 2])
        put(hi, value[seq // 2:])


def attend_back(qa, qb, ka, kb, va, vb, ga, gb, mask, ca, cb, sa, sb):
    slots, batch, rows, nq = qa.shape
    kv = ka.shape[3] // HEAD_DIM
    group = nq // ka.shape[3]
    seq = 2 * slots * rows
    qs, ks = head_specs(slots, rows, group * HEAD_DIM), head_specs(slots, rows, HEAD_DIM)
    ts = pl.BlockSpec((slots, 1, rows, HEAD_DIM), lambda r, h: (0, r, 0, 0))
    return pl.pallas_call(
        functools.partial(attend_back_kernel, group), name="attend_back", grid=(batch, kv),
        in_specs=[qs, qs, ks, ks, ks, ks, qs, qs, pl.BlockSpec((1, seq, group * seq), lambda r, h: (r, 0, 0)), ts, ts, ts, ts],
        out_specs=[qs, qs, ks, ks, ks, ks],
        out_shape=[jax.ShapeDtypeStruct(x.shape, BF16) for x in (qa, qb, ka, kb, va, vb)],
        compiler_params=params(60, "arbitrary", "arbitrary"),
        cost_estimate=cost(batch * kv * group * seq * seq * HEAD_DIM * 60, 8 * qa.size * 2),
    )(qa, qb, ka, kb, va, vb, ga, gb, mask, ca, cb, sa, sb)


def out_share_kernel(o, w, first, second):
    r = dot(o[...], w[...])
    half = first.shape[0]
    first[...] = r[:half].astype(first.dtype)
    second[...] = r[half:].astype(second.dtype)


def out_share(o, w_out, types):
    tok, n = o.shape
    width = w_out.shape[1]
    blk = 1024
    spec = pl.BlockSpec((tok // 2, blk), lambda i: (0, i))
    return pl.pallas_call(
        out_share_kernel, name="out_share", grid=(width // blk,),
        in_specs=[const_spec((tok, n)), pl.BlockSpec((n, blk), lambda i: (0, i))],
        out_specs=[spec, spec], out_shape=[jax.ShapeDtypeStruct((tok // 2, width), t) for t in types],
        compiler_params=params(60), cost_estimate=cost(2 * tok * width * n, 2 * width * n),
    )(o, w_out)


def norm_share_kernel(dq, dk, dv, wq, wk, wv, ha, hb, inv, first, second, gain):
    r = dot(dq[...], wq[...], NT) + dot(dk[...], wk[...], NT) + dot(dv[...], wv[...], NT)
    half = first.shape[0]
    first[...] = r[:half].astype(first.dtype)
    second[...] = r[half:].astype(second.dtype)
    scaled = jnp.concatenate([ha[...], hb[...]], axis=0).astype(F32) * inv[:, :1]
    gain[...] = jnp.sum(r * scaled, axis=0, keepdims=True)


def norm_share(dq, dk, dv, wq, wk, wv, ha, hb, inv, types):
    tok, nq = dq.shape
    nk = dk.shape[1]
    width = wq.shape[0]
    blk = 512
    spec = pl.BlockSpec((tok // 2, blk), lambda i: (0, i))
    return pl.pallas_call(
        norm_share_kernel, name="norm_share", grid=(width // blk,),
        in_specs=[const_spec((tok, nq)), const_spec((tok, nk)), const_spec((tok, nk)),
                  pl.BlockSpec((blk, nq), lambda i: (i, 0)), pl.BlockSpec((blk, nk), lambda i: (i, 0)),
                  pl.BlockSpec((blk, nk), lambda i: (i, 0)), spec, spec, const_spec((tok, 128))],
        out_specs=[spec, spec, pl.BlockSpec((1, blk), lambda i: (0, i))],
        out_shape=[jax.ShapeDtypeStruct((tok // 2, width), t) for t in types] + [jax.ShapeDtypeStruct((1, width), F32)],
        compiler_params=params(60), cost_estimate=cost(2 * tok * width * (nq + 2 * nk), 2 * width * (nq + 2 * nk)),
    )(dq, dk, dv, wq, wk, wv, ha, hb, inv)


def grad_out_kernel(oa, ob, g0, g1, g2, g3, out, ot):
    @pl.when(pl.program_id(0) == 0)
    def _():
        n = oa.shape[1]
        for c in range(0, n, 256):
            ot[c:c + 256, :] = jnp.concatenate([oa[:, c:c + 256], ob[:, c:c + 256]], axis=0).T

    g = jnp.concatenate([g0[...], g1[...], g2[...], g3[...]], axis=0)
    out[...] = dot(ot[...], g)


def grad_w_out(oa, ob, g):
    tok, n = oa.shape
    width = g[0].shape[1]
    blk = 512
    return pl.pallas_call(
        grad_out_kernel, name="grad_w_out", grid=(width // blk,),
        in_specs=[const_spec((tok, n))] * 2 + [pl.BlockSpec((tok // 2, blk), lambda i: (0, i))] * 4,
        out_specs=pl.BlockSpec((n, blk), lambda i: (0, i)), out_shape=jax.ShapeDtypeStruct((n, width), F32),
        scratch_shapes=[pltpu.VMEM((n, 2 * tok), BF16)],
        compiler_params=params(60), cost_estimate=cost(4 * tok * width * n, 4 * width * n),
    )(oa, ob, *g)


def grad_qkv_kernel(na, nb, dqa, dqb, dka, dkb, dva, dvb, gq, gk, gv):
    nt = jnp.concatenate([na[...], nb[...]], axis=0).T
    for lo, hi, out in ((dqa, dqb, gq), (dka, dkb, gk), (dva, dvb, gv)):
        out[...] = dot(nt, jnp.concatenate([lo[...], hi[...]], axis=0))


def grad_w_qkv(na, nb, dqa, dqb, dka, dkb, dva, dvb):
    tok, width = na.shape
    nq, nk = dqa.shape[1], dka.shape[1]
    blk = 512
    return pl.pallas_call(
        grad_qkv_kernel, name="grad_w_qkv", grid=(width // blk,),
        in_specs=[pl.BlockSpec((tok, blk), lambda i: (0, i))] * 2 + [const_spec((tok, nq))] * 2 + [const_spec((tok, nk))] * 4,
        out_specs=[pl.BlockSpec((blk, n), lambda i: (i, 0)) for n in (nq, nk, nk)],
        out_shape=[jax.ShapeDtypeStruct((width, n), F32) for n in (nq, nk, nk)],
        compiler_params=params(60), cost_estimate=cost(4 * tok * width * (nq + 2 * nk), 4 * width * (nq + 2 * nk)),
    )(na, nb, dqa, dqb, dka, dkb, dva, dvb)


def norm_back_kernel(p0, p1, p2, h, g, gain, inv, out):
    dn = p0[...].astype(F32) + p1[...].astype(F32) + p2[...].astype(F32)
    hf = h[...].astype(F32)
    s = inv[:, :1]
    dg = dn * gain[...].astype(F32)
    mean = jnp.mean(dg * hf, axis=-1, keepdims=True)
    out[...] = (g[...].astype(F32) + (s * dg - hf * (s * s * s) * mean)).astype(BF16)


def norm_back(p0, p1, p2, h, g, gain, inv):
    tok, width = h.shape
    blk = 16
    spec = pl.BlockSpec((blk, width), lambda i: (i, 0))
    return pl.pallas_call(
        norm_back_kernel, name="norm_back", grid=(tok // blk,),
        in_specs=[spec] * 5 + [const_spec((1, width)), pl.BlockSpec((blk, 128), lambda i: (i, 0))],
        out_specs=spec, out_shape=jax.ShapeDtypeStruct((tok, width), BF16),
        compiler_params=params(60), cost_estimate=cost(20 * tok * width, 12 * tok * width),
    )(p0, p1, p2, h, g, gain, inv)


def solution(mesh):
    tp_size = mesh.shape['tp']
    beside = [(i, i ^ 1) for i in range(tp_size)]
    across = [(i, i ^ 2) for i in range(tp_size)]
    diagonal = [(i, i ^ 3) for i in range(tp_size)]

    def send(x, pairs):
        return lax.ppermute(x, 'tp', pairs)

    def after(x, *others):
        return lax.optimization_barrier((x,) + others)[0]

    def step(hidden, positions, doc_ids, norm_gain, w_query, w_key, w_value, w_out, grad_out):
        batch, rows, width = hidden.shape
        tok = batch * rows
        nq, nk = w_query.shape[1], w_key.shape[1]
        group = nq // nk
        gain = norm_gain.reshape(1, width)

        ints = jnp.stack([positions, doc_ids])
        ints = jnp.stack([ints, send(ints, beside), send(ints, across), send(ints, diagonal)])
        h0 = hidden.reshape(tok, width)
        g0 = grad_out.reshape(tok, width)
        h2 = send(after(h0, ints), across)
        h1 = send(after(h0, ints), beside)
        g1 = send(after(g0, h1), beside)
        g2 = send(after(g0, h1), across)
        h3 = send(h2, beside)

        pos, doc = ints[:, 0], ints[:, 1]
        lane = jnp.arange(HEAD_DIM)
        inv_freq = ROPE_BASE ** (-(lane // 2 * 2).astype(F32) / HEAD_DIM)
        angles = pos.astype(F32)[..., None] * inv_freq
        cos, sin = jnp.cos(angles), jnp.sin(angles) * jnp.where(lane % 2 == 0, -1.0, 1.0)
        pos_r = jnp.swapaxes(pos, 0, 1).reshape(batch, 4 * rows)
        doc_r = jnp.swapaxes(doc, 0, 1).reshape(batch, 4 * rows)
        allowed = ((doc_r[:, :, None] == doc_r[:, None, :]) & (pos_r[:, None, :] <= pos_r[:, :, None])).astype(F32)
        allowed_t = jnp.tile(jnp.swapaxes(allowed, 1, 2), (1, 1, group)).astype(BF16)

        def heads(x):
            return x.reshape(2, batch, rows, x.shape[1])

        def flat(x):
            return x.reshape(2 * tok, x.shape[3])

        ca, cb, sa, sb = cos[:2], cos[2:], sin[:2], sin[2:]
        na, inv_a, qa, ka, va = qkv(h0, h1, gain, ca.reshape(2 * tok, HEAD_DIM), sa.reshape(2 * tok, HEAD_DIM), w_query, w_key, w_value)
        dha = heads_grad(after(g0, ka), g1, w_out)
        nb, inv_b, qb, kb, vb = qkv(after(h2, dha), h3, gain, cb.reshape(2 * tok, HEAD_DIM), sb.reshape(2 * tok, HEAD_DIM), w_query, w_key, w_value)
        saved = [heads(x) for x in (qa, qb, ka, kb, va, vb)]
        oa, ob = [flat(x) for x in attend(*saved, allowed)]

        p2, p3 = out_share(ob, w_out, (F32, F32))
        p3 = send(p3, beside)
        p0, p1 = out_share(after(oa, p2), w_out, (F32, BF16))
        s2 = (p2 + after(p3, p0)).astype(BF16)
        p1, s2, g2 = lax.optimization_barrier((p1, s2, g2))
        p1 = send(p1, beside)
        s2 = send(s2, across)
        g3 = send(g2, beside)

        dhb = heads_grad(g2, g3, w_out)
        grads = attend_back(*saved, heads(dha), heads(dhb), allowed_t, ca, cb, sa, sb)
        dqa, dqb, dka, dkb, dva, dvb = [flat(x) for x in grads]
        d2, d3, gain_b = norm_share(dqb, dkb, dvb, w_query, w_key, w_value, h2, h3, inv_b, (F32, BF16))
        d3 = send(d3, beside)
        d0, d1, gain_a = norm_share(after(dqa, d2), dka, dva, w_query, w_key, w_value, h0, h1, inv_a, (F32, BF16))
        t2 = (d2 + after(d3, d0).astype(F32)).astype(BF16)
        d1, t2, gg, p1, s2 = lax.optimization_barrier((d1, t2, gain_a + gain_b, p1, s2))
        t2 = send(t2, across)
        d1 = send(d1, beside)
        gg = gg + send(gg, beside)
        attn_rows = (p0 + p1.astype(F32) + s2.astype(F32)).astype(BF16)
        attn_out = (h0 + attn_rows).reshape(hidden.shape)

        g_out = grad_w_out(after(oa, attn_out), ob, (g0, g1, g2, g3))
        gq, gk, gv = grad_w_qkv(after(na, g_out), nb, dqa, dqb, dka, dkb, dva, dvb)
        gg = gg + send(gg, across)
        grad_gain = gg.reshape(width)
        grad_hidden = norm_back(after(d0, gk), d1, t2, h0, g0, gain, inv_a[:tok]).reshape(hidden.shape)
        return (attn_out, grad_hidden, grad_gain, gq, gk, gv, g_out)

    row_spec = P('dp', 'tp', None)
    tok_spec = P('dp', 'tp')
    col_spec = P(None, 'tp')

    return jax.shard_map(
        step, mesh=mesh,
        in_specs=(row_spec, tok_spec, tok_spec, P(), col_spec, col_spec, col_spec, P('tp', None), row_spec),
        out_specs=(row_spec, row_spec, P('dp'), P('dp', 'tp'), P('dp', 'tp'), P('dp', 'tp'), P(('dp', 'tp'), None)),
        check_vma=False)
```

time: 641 us -> 450 us (0.70)
  matrix products: 316 us -> 0 us
  Pallas kernels: 0 us -> 299 us
  other arithmetic: 78.3 us -> 21.6 us
  local copies, waits for them, and re-layouts: 68.3 us -> 16.3 us
  blocking collectives: 27.2 us -> 0 us
  waiting for transfers between devices: 120 us -> 100 us
  between operations: 14.6 us -> 0.78 us
    dot_general x17 -> x0, matrix products: 307 us -> none  [the longest x1 35.9 us: attention_backward(): jnp.einsum('bsd,bsn->dn', normed_full, grad_query, preferred_element_type...]
    pallas_call x0 -> x13, Pallas kernels: none -> 299 us  [the longest x2 59.3 us: qkv(): pl.pallas_call(functools.partial(qkv_kernel, q_steps), name='qkv', grid=(...]
    ppermute x0 -> x17, waiting for transfers between devices: none -> 100 us  [send(): return lax.ppermute(x, 'tp', pairs)]
    all_gather x2 -> x0, waiting for transfers between devices: 87.1 us -> none  [the longest x1 45.9 us: device_step(): normed_full = lax.all_gather(normed, 'tp', axis=1, tiled=True)]
    another operation x8 -> x2, other arithmetic: 36.9 us -> 0.71 us  [step(): jnp.stack([ints, send(ints, beside), send(ints, across), send(ints, diago...]
    all_to_all x2 -> x0, waiting for transfers between devices: 31.7 us -> none  [sum_scatter_rows(): received = lax.all_to_all(pieces, 'tp', 1, 1, tiled=True)]
    reshape x4 -> x1, local copies, waits for them, and re-layouts: 19.4 us -> 1.34 us  [step(): gain = norm_gain.reshape(1, width)]
    reduce_sum x4 -> x0, other arithmetic: 17.8 us -> none  [the longest x2 13.7 us: sum_scatter_rows(): return jnp.sum(received, axis=1, dtype=jnp.float32)]
  transfers between devices with their start and end apart: 4 -> 17, of which waited for: 4 -> 6; matrix products, arithmetic and copies ran while one was open for 31% -> 5% of each run, Pallas kernels for 0% -> 38%
where the time goes in v1:
time: 450 us; the launch traced here: 447 us
  Pallas kernels  299 us (66%)
  waiting for transfers between devices  100 us (22%)
  other arithmetic  21.6 us (5%)
  local copies, waits for them, and re-layouts  16.3 us (4%)
  starting transfers between devices  9.21 us (2%)
    ppermute x17, waiting for transfers between devices, send(): return lax.ppermute(x, 'tp', pairs)  100 us
    pallas_call x2, Pallas kernels, qkv(): pl.pallas_call(functools.partial(qkv_kernel, q_steps), name='qkv', grid=(...  59.3 us
    pallas_call x2, Pallas kernels, norm_share(): pl.pallas_call(norm_share_kernel, name='norm_share', grid=(width // blk,)...  52.6 us
    pallas_call x2, Pallas kernels, heads_grad(): pl.pallas_call(heads_grad_kernel, name='heads_grad', grid=(n // blk,), in...  40.1 us
    pallas_call x1, Pallas kernels, grad_w_qkv(): pl.pallas_call(grad_qkv_kernel, name='grad_w_qkv', grid=(width // blk,),...  40 us
    pallas_call x2, Pallas kernels, out_share(): pl.pallas_call(out_share_kernel, name='out_share', grid=(width // blk,),...  38.4 us
    pallas_call x1, Pallas kernels, grad_w_out(): pl.pallas_call(grad_out_kernel, name='grad_w_out', grid=(width // blk,),...  35.1 us
    pallas_call x1, Pallas kernels, attend_back(): pl.pallas_call(functools.partial(attend_back_kernel, group), name='attend...  13.7 us
  transfers between devices with their start and end apart: 17, of which 6 were waited for; matrix products, arithmetic and copies ran while one was open for 5% of the time, Pallas kernels for 38%

profile of v1, /device:TPU:0, one launch (start us, length us, event | category | flops | bytes accessed | tf_op | source)
XLA Modules:
  0.0 446.9 jit_solution(1109896293646002502)
XLA Ops:
  0.6 0.7 fusion.7
  1.3 3.3 collective-permute-start.1
  4.8 1.5 collective-permute-done.1
  6.2 1.4 collective-permute-done.2
  7.7 0.5 collective-permute-start.3
  8.2 0.2 collective-permute-start.4
  8.4 4.2 collective-permute-done.3.hb
  12.6 1.4 copy-done.3
  14.0 0.4 collective-permute-start.5
  14.3 1.3 reshape.139.gain
  15.7 1.1 fusion.1
  16.8 44.9 %collective-permute-done.4.ha = bf16[144,8192]{1,0:T(8,128)(2,1)} collective-permute-done((bf16[144,8192]{1,0:T(8,128)(2,1)}, bf16[144,8192]{1,0:T(8,128)(2,1)}, u32[]{:S(2)}, u32[]{:S(2)}) %collective-permute-start.4) | collective-permute-done | bytes 2359328 | tf_op jit(solution)/shard_map/ppermute | solution.py:352
  61.7 0.8 fusion.8
  62.7 1.1 convert_convert_fusion
  63.8 29.6 %qkv.2 = (bf16[288,8192]{1,0:T(8,128)(2,1)}, f32[288,128]{1,0:T(8,128)}, bf16[288,2048]{1,0:T(8,128)(2,1)}, bf16[288,256]{1,0:T(8,128)(2,1)}, bf16[288,256]{1,0:T(8,128)(2,1)}) custom-call(bf16[144,8192]{1,0:T(8,128)(2,1)} %bitcast.46, bf16[144,8192]{1,0:T(8,128)(2,1)} %copy-done.3, bf16[1,8192]{1,0:T(2,128)(2,1)} %reshape.139.gain, f32[288,128]{1,0:T(8,128)} %bitcast.68, ...), custom_call_target="tpu_custom_call" | custom-call | flops 12079595520 | bytes 41943040 | tf_op jit(solution)/shard_map/qkv/pallas_call | solution.py:96
  93.3 1.4 copy-done.2
  94.7 20.1 %heads_grad.2 = bf16[288,2048]{1,0:T(8,128)(2,1)} custom-call(bf16[144,8192]{1,0:T(8,128)(2,1)} %bitcast.50, bf16[144,8192]{1,0:T(8,128)(2,1)} %copy-done.2, bf16[2048,8192]{1,0:T(8,128)(2,1)} %w.7), custom_call_target="tpu_custom_call" | custom-call | flops 9663676416 | bytes 33554432 | tf_op jit(solution)/shard_map/heads_grad/pallas_call | solution.py:132
  114.9 29.7 %qkv.3 = (bf16[288,8192]{1,0:T(8,128)(2,1)}, f32[288,128]{1,0:T(8,128)}, bf16[288,2048]{1,0:T(8,128)(2,1)}, bf16[288,256]{1,0:T(8,128)(2,1)}, bf16[288,256]{1,0:T(8,128)(2,1)}) custom-call(bf16[144,8192]{1,0:T(8,128)(2,1)} %collective-permute-done.4.ha, bf16[144,8192]{1,0:T(8,128)(2,1)} %collective-permute-done.6.hb, bf16[1,8192]{1,0:T(2,128)(2,1)} %reshape.139.gain, ...), custom_call_target="tpu_custom_call" | custom-call | flops 12079595520 | bytes 41943040 | tf_op jit(solution)/shard_map/qkv/pallas_call | solution.py:96
  144.6 9.6 %attend.1 = (bf16[2,3,48,2048]{3,2,1,0:T(8,128)(2,1)}, bf16[2,3,48,2048]{3,2,1,0:T(8,128)(2,1)}) custom-call(bf16[2,3,48,2048]{3,2,1,0:T(8,128)(2,1)} %bitcast.84, bf16[2,3,48,2048]{3,2,1,0:T(8,128)(2,1)} %bitcast.86, bf16[2,3,48,256]{3,2,1,0:T(8,128)(2,1)} %bitcast.88, bf16[2,3,48,256]{3,2,1,0:T(8,128)(2,1)} %bitcast.92, bf16[2,3,48,256]{3,2,1,0:T(8,128)(2,1)} %bitcast.90, ...), custom_call_target="tpu_custom_call" | custom-call | flops 9059696640 | bytes 4718592 | tf_op jit(solution)/shard_map/attend/pallas_call | solution.py:181
  154.1 19.7 %out_share.2 = (f32[144,8192]{1,0:T(8,128)}, f32[144,8192]{1,0:T(8,128)}) custom-call(bf16[288,2048]{1,0:T(8,128)(2,1)} %bitcast.64, bf16[2048,8192]{1,0:T(8,128)(2,1)} %w.7), custom_call_target="tpu_custom_call" | custom-call | flops 9663676416 | bytes 33554432 | tf_op jit(solution)/shard_map/out_share/pallas_call | solution.py:247
  173.9 0.5 collective-permute-start.7
  174.4 0.6 collective-permute-start.8
  174.9 18.7 %out_share.3 = (f32[144,8192]{1,0:T(8,128)}, bf16[144,8192]{1,0:T(8,128)(2,1)}) custom-call(bf16[288,2048]{1,0:T(8,128)(2,1)} %bitcast.62, bf16[2048,8192]{1,0:T(8,128)(2,1)} %w.7), custom_call_target="tpu_custom_call" | custom-call | flops 9663676416 | bytes 33554432 | tf_op jit(solution)/shard_map/out_share/pallas_call | solution.py:247
  193.7 5.7 %add_convert_fusion.2 = bf16[144,8192]{1,0:T(8,128)(2,1)} fusion(f32[144,8192]{1,0:T(8,128)} %get-tuple-element.69, f32[144,8192]{1,0:T(8,128)} %collective-permute-done.7), kind=kLoop, calls=%fused_computation.2 | loop fusion | flops 2359296 | bytes 11796480 | tf_op jit(solution)/shard_map/convert_element_type | solution.py:400
  199.3 28.3 %collective-permute-done.8.ga.g2 = bf16[144,8192]{1,0:T(8,128)(2,1)} collective-permute-done((bf16[144,8192]{1,0:T(8,128)(2,1)S(1)}, bf16[144,8192]{1,0:T(8,128)(2,1)}, u32[]{:S(2)}, u32[]{:S(2)}) %collective-permute-start.8) | collective-permute-done | bytes 2359328 | tf_op jit(solution)/shard_map/ppermute | solution.py:352
  227.7 1.7 tile.2
  229.4 4.6 %convert_element_type.48.mask = bf16[3,192,1536]{2,1,0:T(8,128)(2,1)} reshape(bf16[3,192,8,192]{3,2,1,0:T(8,128)(2,1)} %tile.2) | data formatting | bytes 3538944 | tf_op jit(solution)/shard_map/convert_element_type | solution.py:382
  234.0 1.4 copy-done.4
  235.4 20.1 %heads_grad.3 = bf16[288,2048]{1,0:T(8,128)(2,1)} custom-call(bf16[144,8192]{1,0:T(8,128)(2,1)} %collective-permute-done.8.ga.g2, bf16[144,8192]{1,0:T(8,128)(2,1)} %copy-done.4, bf16[2048,8192]{1,0:T(8,128)(2,1)} %w.7), custom_call_target="tpu_custom_call" | custom-call | flops 9663676416 | bytes 33554432 | tf_op jit(solution)/shard_map/heads_grad/pallas_call | solution.py:132
  255.4 13.7 %attend_back.1 = (bf16[2,3,48,2048]{3,2,1,0:T(8,128)(2,1)}, bf16[2,3,48,2048]{3,2,1,0:T(8,128)(2,1)}, bf16[2,3,48,256]{3,2,1,0:T(8,128)(2,1)}, bf16[2,3,48,256]{...) custom-call(bf16[2,3,48,2048]{3,2,1,0:T(8,128)(2,1)} %bitcast.85, ...), custom_call_target="tpu_custom_call" | custom-call | flops 13589544960 | bytes 9437184 | tf_op jit(solution)/shard_map/attend_back/pallas_call | solution.py:225
  269.1 26.3 %norm_share.2 = (f32[144,8192]{1,0:T(8,128)}, bf16[144,8192]{1,0:T(8,128)(2,1)}, f32[1,8192]{1,0:T(1,128)}) custom-call(bf16[288,2048]{1,0:T(8,128)(2,1)} %bitcast.58, bf16[288,256]{1,0:T(8,128)(2,1)} %bitcast.72, bf16[288,256]{1,0:T(8,128)(2,1)} %bitcast.76, bf16[8192,2048]{1,0:T(8,128)(2,1)} %wq.7, bf16[8192,256]{1,0:T(8,128)(2,1)} %wk.7, ...), custom_call_target="tpu_custom_call" | custom-call | flops 12079595520 | bytes 41943040 | tf_op jit(solution)/shard_map/norm_share/pallas_call | solution.py:270
  295.4 0.5 collective-permute-start.10
  295.9 0.6 slice.27.inv
  296.5 0.6 collective-permute-start.12
  297.1 26.3 %norm_share.3 = (f32[144,8192]{1,0:T(8,128)}, bf16[144,8192]{1,0:T(8,128)(2,1)}, f32[1,8192]{1,0:T(1,128)}) custom-call(bf16[288,2048]{1,0:T(8,128)(2,1)} %bitcast.56, bf16[288,256]{1,0:T(8,128)(2,1)} %bitcast.70, bf16[288,256]{1,0:T(8,128)(2,1)} %bitcast.74, bf16[8192,2048]{1,0:T(8,128)(2,1)} %wq.7, bf16[8192,256]{1,0:T(8,128)(2,1)} %wk.7, ...), custom_call_target="tpu_custom_call" | custom-call | flops 12079595520 | bytes 41943040 | tf_op jit(solution)/shard_map/norm_share/pallas_call | solution.py:270
  323.5 0.8 add.42
  324.3 1.4 copy-done.6
  325.7 5.1 %add_convert_fusion.1 = bf16[144,8192]{1,0:T(8,128)(2,1)} fusion(f32[144,8192]{1,0:T(8,128)} %get-tuple-element.81, bf16[144,8192]{1,0:T(8,128)(2,1)} %copy-done.6), kind=kLoop, calls=%fused_computation.1 | loop fusion | flops 3538944 | bytes 9437184 | tf_op jit(solution)/shard_map/convert_element_type | solution.py:412
  330.8 19.7 %collective-permute-done.12 = bf16[144,8192]{1,0:T(8,128)(2,1)} collective-permute-done((bf16[144,8192]{1,0:T(8,128)(2,1)}, bf16[144,8192]{1,0:T(8,128)(2,1)}, u32[]{:S(2)}, u32[]{:S(2)}) %collective-permute-start.12) | collective-permute-done | bytes 2359328 | tf_op jit(solution)/shard_map/ppermute | solution.py:352
  350.5 6.5 %fusion = bf16[144,8192]{1,0:T(8,128)(2,1)} fusion(bf16[144,8192]{1,0:T(8,128)(2,1)} %collective-permute-done.12, f32[144,8192]{1,0:T(8,128)} %get-tuple-element.71, bf16[144,8192]{1,0:T(8,128)(2,1)} %collective-permute-done.11, bf16[3,48,8192]{2,1,0:T(8,128)(2,1)S(1)} %copy-done), kind=kLoop, calls=%fused_computation.3 | loop fusion | flops 7077888 | bytes 14155776 | tf_op jit(solution)/shard_map/add | solution.py:418
  357.0 0.5 collective-permute-start.13
  357.5 0.6 collective-permute-start.14
  358.1 35.1 %grad_w_out.1 = f32[2048,8192]{1,0:T(8,128)} custom-call(bf16[288,2048]{1,0:T(8,128)(2,1)} %bitcast.63, bf16[288,2048]{1,0:T(8,128)(2,1)} %bitcast.65, bf16[144,8192]{1,0:T(8,128)(2,1)} %bitcast.51, bf16[144,8192]{1,0:T(8,128)(2,1)} %copy-done.2, bf16[144,8192]{1,0:T(8,128)(2,1)} %collective-permute-done.8.ga.g2, bf16[144,8192]{1,0:T(8,128)(2,1)} %copy-done.4), custom_call_target="tpu_custom_call" | custom-call | flops 19327352832 | bytes 67108864 | tf_op jit(solution)/shard_map/grad_w_out/pallas_call | solution.py:296
  393.2 1.5 collective-permute-start.16
  394.7 40.0 %grad_w_qkv.1 = (f32[8192,2048]{1,0:T(8,128)}, f32[8192,256]{1,0:T(8,128)}, f32[8192,256]{1,0:T(8,128)}) custom-call(bf16[288,8192]{1,0:T(8,128)(2,1)} %get-tuple-element.98.na, bf16[288,8192]{1,0:T(8,128)(2,1)} %get-tuple-element.99.nb, bf16[288,2048]{1,0:T(8,128)(2,1)} %bitcast.57, bf16[288,2048]{1,0:T(8,128)(2,1)} %bitcast.59, bf16[288,256]{1,0:T(8,128)(2,1)} %bitcast.71, ...), custom_call_target="tpu_custom_call" | custom-call | flops 24159191040 | bytes 83886080 | tf_op jit(solution)/shard_map/grad_w_qkv/pallas_call | solution.py:315
  434.6 0.7 add.47
  435.3 1.4 copy-done.5
  436.7 10.2 %norm_back.1 = bf16[144,8192]{1,0:T(8,128)(2,1)} custom-call(f32[144,8192]{1,0:T(8,128)} %get-tuple-element.101.p0, bf16[144,8192]{1,0:T(8,128)(2,1)} %copy-done.5, bf16[144,8192]{1,0:T(8,128)(2,1)} %collective-permute-done.14.p2, bf16[144,8192]{1,0:T(8,128)(2,1)} %bitcast.48, bf16[144,8192]{1,0:T(8,128)(2,1)} %bitcast.52, bf16[1,8192]{1,0:T(2,128)(2,1)} %reshape.139.gain, ...), custom_call_target="tpu_custom_call" | custom-call | flops 23592960 | bytes 14155776 | tf_op jit(solution)/shard_map/norm_back/pallas_call | solution.py:337
  (39 shorter events, 0.4 us)
Async XLA Ops:
  1.3 4.9 %collective-permute-start.1 = (s32[2,3,48]{2,1,0:T(4,128)S(1)}, s32[2,3,48]{2,1,0:T(4,128)S(1)}, u32[]{:S(2)}, u32[]{:S(2)}) collective-permute-start(s32[2,3,48]{2,1,0:T(4,128)S(1)} %get-tuple-element.119), channel_id=1, source_target_pairs={{0,2},{1,3},{2,0},{3,1},{4,6},{5,7},{6,4},{7,5}} | collective-permute-start | bytes 3464 | tf_op jit(solution)/shard_map/ppermute | solution.py:352
  4.6 1.6 collective-permute-start
  4.6 3.0 collective-permute-start.2
  7.7 4.9 %collective-permute-start.3 = (bf16[144,8192]{1,0:T(8,128)(2,1)}, bf16[144,8192]{1,0:T(8,128)(2,1)S(1)}, u32[]{:S(2)}, u32[]{:S(2)}) collective-permute-start(bf16[144,8192]{1,0:T(8,128)(2,1)} %bitcast.44), channel_id=1, source_target_pairs={{0,1},{1,0},{2,3},{3,2},{4,5},{5,4},{6,7},{7,6}} | collective-permute-start | bytes 7077896 | tf_op jit(solution)/shard_map/ppermute | solution.py:352
  8.2 53.5 %collective-permute-start.4 = (bf16[144,8192]{1,0:T(8,128)(2,1)}, bf16[144,8192]{1,0:T(8,128)(2,1)}, u32[]{:S(2)}, u32[]{:S(2)}) collective-permute-start(bf16[144,8192]{1,0:T(8,128)(2,1)} %bitcast.45), channel_id=1, source_target_pairs={{0,2},{1,3},{2,0},{3,1},{4,6},{5,7},{6,4},{7,5}} | collective-permute-start | bytes 7077896 | tf_op jit(solution)/shard_map/ppermute | solution.py:352
  12.6 1.4 copy-start.3
  14.0 79.4 %collective-permute-start.5 = (bf16[144,8192]{1,0:T(8,128)(2,1)}, bf16[144,8192]{1,0:T(8,128)(2,1)S(1)}, u32[]{:S(2)}, u32[]{:S(2)}) collective-permute-start(bf16[144,8192]{1,0:T(8,128)(2,1)} %bitcast.49), channel_id=1, source_target_pairs={{0,1},{1,0},{2,3},{3,2},{4,5},{5,4},{6,7},{7,6}} | collective-permute-start | bytes 7077896 | tf_op jit(solution)/shard_map/ppermute | solution.py:352
  61.7 53.1 %collective-permute-start.6 = (bf16[144,8192]{1,0:T(8,128)(2,1)}, bf16[144,8192]{1,0:T(8,128)(2,1)}, u32[]{:S(2)}, u32[]{:S(2)}) collective-permute-start(bf16[144,8192]{1,0:T(8,128)(2,1)} %collective-permute-done.4.ha), channel_id=1, source_target_pairs={{0,1},{1,0},{2,3},{3,2},{4,5},{5,4},{6,7},{7,6}} | collective-permute-start | bytes 7077896 | tf_op jit(solution)/shard_map/ppermute | solution.py:352
  93.3 1.4 copy-start.2
  154.1 20.2 %copy-start.1 = (bf16[3,48,8192]{2,1,0:T(8,128)(2,1)S(1)}, bf16[3,48,8192]{2,1,0:T(8,128)(2,1)}, u32[]{:S(2)}) copy-start(bf16[3,48,8192]{2,1,0:T(8,128)(2,1)} %param.17) | copy-start | bytes 7077892
  173.9 19.8 %collective-permute-start.7 = (f32[144,8192]{1,0:T(8,128)}, f32[144,8192]{1,0:T(8,128)}, u32[]{:S(2)}, u32[]{:S(2)}) collective-permute-start(f32[144,8192]{1,0:T(8,128)} %get-tuple-element.73), channel_id=1, source_target_pairs={{0,1},{1,0},{2,3},{3,2},{4,5},{5,4},{6,7},{7,6}} | collective-permute-start | bytes 14155784 | tf_op jit(solution)/shard_map/ppermute | solution.py:352
  174.4 53.3 %collective-permute-start.8 = (bf16[144,8192]{1,0:T(8,128)(2,1)S(1)}, bf16[144,8192]{1,0:T(8,128)(2,1)}, u32[]{:S(2)}, u32[]{:S(2)}) collective-permute-start(bf16[144,8192]{1,0:T(8,128)(2,1)S(1)} %bitcast.53), channel_id=1, source_target_pairs={{0,2},{1,3},{2,0},{3,1},{4,6},{5,7},{6,4},{7,5}} | collective-permute-start | bytes 7077896 | tf_op jit(solution)/shard_map/ppermute | solution.py:352
  227.7 6.3 %collective-permute-start.9 = (bf16[144,8192]{1,0:T(8,128)(2,1)}, bf16[144,8192]{1,0:T(8,128)(2,1)S(1)}, u32[]{:S(2)}, u32[]{:S(2)}) collective-permute-start(bf16[144,8192]{1,0:T(8,128)(2,1)} %collective-permute-done.8.ga.g2), channel_id=1, source_target_pairs={{0,1},{1,0},{2,3},{3,2},{4,5},{5,4},{6,7},{7,6}} | collective-permute-start | bytes 7077896 | tf_op jit(solution)/shard_map/ppermute | solution.py:352
  234.0 1.4 copy-start.4
  269.1 26.8 %copy-start.7 = (f32[288,128]{1,0:T(8,128)S(1)}, f32[288,128]{1,0:T(8,128)}, u32[]{:S(2)}) copy-start(f32[288,128]{1,0:T(8,128)} %get-tuple-element.85.inv) | copy-start | bytes 442372
  295.4 28.9 %collective-permute-start.10 = (bf16[144,8192]{1,0:T(8,128)(2,1)}, bf16[144,8192]{1,0:T(8,128)(2,1)S(1)}, u32[]{:S(2)}, u32[]{:S(2)}) collective-permute-start(bf16[144,8192]{1,0:T(8,128)(2,1)} %get-tuple-element.87), channel_id=1, source_target_pairs={{0,1},{1,0},{2,3},{3,2},{4,5},{5,4},{6,7},{7,6}} | collective-permute-start | bytes 7077896 | tf_op jit(solution)/shard_map/ppermute | solution.py:352
  296.5 34.3 %collective-permute-start.11 = (bf16[144,8192]{1,0:T(8,128)(2,1)}, bf16[144,8192]{1,0:T(8,128)(2,1)}, u32[]{:S(2)}, u32[]{:S(2)}) collective-permute-start(bf16[144,8192]{1,0:T(8,128)(2,1)} %get-tuple-element.92), channel_id=1, source_target_pairs={{0,1},{1,0},{2,3},{3,2},{4,5},{5,4},{6,7},{7,6}} | collective-permute-start | bytes 7077896 | tf_op jit(solution)/shard_map/ppermute | solution.py:352
  296.5 54.0 %collective-permute-start.12 = (bf16[144,8192]{1,0:T(8,128)(2,1)}, bf16[144,8192]{1,0:T(8,128)(2,1)}, u32[]{:S(2)}, u32[]{:S(2)}) collective-permute-start(bf16[144,8192]{1,0:T(8,128)(2,1)} %add_convert_fusion.2), channel_id=1, source_target_pairs={{0,2},{1,3},{2,0},{3,1},{4,6},{5,7},{6,4},{7,5}} | collective-permute-start | bytes 7077896 | tf_op jit(solution)/shard_map/ppermute | solution.py:352
  297.1 26.3 %copy-start.8 = (f32[1,8192]{1,0:T(1,128)S(1)}, f32[1,8192]{1,0:T(1,128)}, u32[]{:S(2)}) copy-start(f32[1,8192]{1,0:T(1,128)} %get-tuple-element.91) | copy-start | bytes 98308
  324.3 1.4 copy-start.6
  325.7 24.8 %copy-start = (bf16[3,48,8192]{2,1,0:T(8,128)(2,1)S(1)}, bf16[3,48,8192]{2,1,0:T(8,128)(2,1)}, u32[]{:S(2)}) copy-start(bf16[3,48,8192]{2,1,0:T(8,128)(2,1)} %param.9) | copy-start | bytes 7077892
  357.0 36.2 %collective-permute-start.15 = (f32[1,8192]{1,0:T(1,128)S(1)}, f32[1,8192]{1,0:T(1,128)S(1)}, u32[]{:S(2)}, u32[]{:S(2)}) collective-permute-start(f32[1,8192]{1,0:T(1,128)S(1)} %add.42), channel_id=1, source_target_pairs={{0,1},{1,0},{2,3},{3,2},{4,5},{5,4},{6,7},{7,6}} | collective-permute-start | bytes 98312 | tf_op jit(solution)/shard_map/ppermute | solution.py:352
  357.0 78.3 %collective-permute-start.13 = (bf16[144,8192]{1,0:T(8,128)(2,1)}, bf16[144,8192]{1,0:T(8,128)(2,1)S(1)}, u32[]{:S(2)}, u32[]{:S(2)}) collective-permute-start(bf16[144,8192]{1,0:T(8,128)(2,1)} %get-tuple-element.102), channel_id=1, source_target_pairs={{0,1},{1,0},{2,3},{3,2},{4,5},{5,4},{6,7},{7,6}} | collective-permute-start | bytes 7077896 | tf_op jit(solution)/shard_map/ppermute | solution.py:352
  357.5 77.8 %collective-permute-start.14 = (bf16[144,8192]{1,0:T(8,128)(2,1)}, bf16[144,8192]{1,0:T(8,128)(2,1)}, u32[]{:S(2)}, u32[]{:S(2)}) collective-permute-start(bf16[144,8192]{1,0:T(8,128)(2,1)} %add_convert_fusion.1), channel_id=1, source_target_pairs={{0,2},{1,3},{2,0},{3,1},{4,6},{5,7},{6,4},{7,5}} | collective-permute-start | bytes 7077896 | tf_op jit(solution)/shard_map/ppermute | solution.py:352
  393.2 41.4 %collective-permute-start.16 = (f32[1,8192]{1,0:T(1,128)S(1)}, f32[1,8192]{1,0:T(1,128)S(1)}, u32[]{:S(2)}, u32[]{:S(2)}) collective-permute-start(f32[1,8192]{1,0:T(1,128)S(1)} %add.46), channel_id=1, source_target_pairs={{0,2},{1,3},{2,0},{3,1},{4,6},{5,7},{6,4},{7,5}} | collective-permute-start | bytes 98312 | tf_op jit(solution)/shard_map/ppermute | solution.py:352
  435.3 1.4 copy-start.5

commit v2 on v1

v2 whole, which is shorter than its diff:
```python
import functools

import jax
import jax.numpy as jnp
from jax import lax
from jax.experimental import pallas as pl
from jax.experimental.pallas import tpu as pltpu
from jax.sharding import PartitionSpec as P


HEAD_DIM = 128
NORM_EPS = 1e-5
ROPE_BASE = 10000.0
LOG2_E = 1.4426950408889634
BF16 = jnp.bfloat16
F32 = jnp.float32
ANY = pl.BlockSpec(memory_space=pl.ANY)
NN = (((1,), (0,)), ((), ()))
NT = (((1,), (1,)), ((), ()))
TN = (((0,), (0,)), ((), ()))


def dot(a, b, dims=NN):
    return lax.dot_general(a, b, dims, preferred_element_type=F32)


def const_spec(shape):
    return pl.BlockSpec(shape, lambda *_: (0,) * len(shape), pipeline_mode=pl.Buffered(1))


def params(mib, *semantics):
    return pltpu.CompilerParams(dimension_semantics=semantics or ("arbitrary",), vmem_limit_bytes=mib << 20)


def cost(flops, moved):
    return pl.CostEstimate(flops=int(flops), bytes_accessed=int(moved), transcendentals=0)


def swap_pairs(x):
    lane = lax.broadcasted_iota(jnp.int32, x.shape, x.ndim - 1)
    return jnp.where(lane % 2 == 0, pltpu.roll(x, x.shape[-1] - 1, x.ndim - 1), pltpu.roll(x, 1, x.ndim - 1))


def qkv_kernel(q_steps, ha, hb, gain, cos, sin, wq, wk, wv, n_out, inv_out, q_out, k_out, v_out, ns, ws, sem, wsem):
    step = pl.program_id(0)
    half, width = ha.shape
    nk = wk.shape[1]
    blk = ws.shape[2]
    slots = ws.shape[0]
    save_n = pltpu.make_async_copy(ns, n_out, sem.at[4])
    load_kv = [pltpu.make_async_copy(w, ws.at[q_steps % slots, :, pl.ds(i * nk, nk)], sem.at[2 + i]) for i, w in enumerate((wk, wv))]

    def load_q(i):
        return pltpu.make_async_copy(wq.at[:, pl.ds(pl.multiple_of(i * blk, blk), blk)], ws.at[i % slots], wsem.at[i % slots])

    @pl.when(step == 0)
    def _():
        loads = [pltpu.make_async_copy(ha, ns.at[pl.ds(0, half)], sem.at[0]),
                 pltpu.make_async_copy(hb, ns.at[pl.ds(half, half)], sem.at[1])]
        for c in loads:
            c.start()
        for c in loads:
            c.wait()
        load_q(0).start()
        wide = 512

        def rows(i, _):
            at = pl.ds(pl.multiple_of(i * 48, 48), 48)
            total = jnp.zeros((48, wide), F32)
            for c in range(0, width, wide):
                x = ns[at, c:c + wide].astype(F32)
                total = total + x * x
            inv = lax.rsqrt(jnp.sum(total, axis=-1, keepdims=True) / width + NORM_EPS)
            for c in range(0, width, wide):
                x = ns[at, c:c + wide].astype(F32)
                ns[at, c:c + wide] = (x * inv * gain[:, c:c + wide]).astype(BF16)
            inv_out[at, :] = jnp.broadcast_to(inv, (48, 128))
            return 0

        chunks = 2 * half // 48
        lax.fori_loop(0, chunks // 2, rows, 0)
        load_q(1).start()
        lax.fori_loop(chunks // 2, chunks, rows, 0)
        load_q(2).start()

    @pl.when((step > 0) & (step + slots - 1 < q_steps))
    def _():
        load_q(step + slots - 1).start()

    @pl.when(step + slots - 1 == q_steps)
    def _():
        for c in load_kv:
            c.start()
        save_n.start()

    def rotated(raw):
        parts = []
        for j in range(raw.shape[1] // HEAD_DIM):
            x = raw[:, j * HEAD_DIM:(j + 1) * HEAD_DIM]
            parts.append((x * cos[...] + swap_pairs(x) * sin[...]).astype(BF16))
        return jnp.concatenate(parts, axis=1)

    @pl.when(step < q_steps)
    def _():
        load_q(step).wait()
        q_out[...] = rotated(dot(ns[...], ws[step % slots]))

    @pl.when(step == q_steps)
    def _():
        for c in load_kv:
            c.wait()
        r = dot(ns[...], ws[q_steps % slots])
        k_out[...] = rotated(r[:, :nk])
        v_out[...] = r[:, nk:].astype(BF16)
        save_n.wait()


def qkv(ha, hb, gain, cos, sin, wq, wk, wv):
    half, width = ha.shape
    tok = 2 * half
    nq, nk = wq.shape[1], wk.shape[1]
    blk = 2 * nk
    q_steps = nq // blk
    return pl.pallas_call(
        functools.partial(qkv_kernel, q_steps), name="qkv", grid=(q_steps + 1,),
        in_specs=[ANY, ANY, const_spec((1, width)), const_spec((tok, HEAD_DIM)), const_spec((tok, HEAD_DIM)), ANY, ANY, ANY],
        out_specs=[ANY, const_spec((tok, 128)),
                   pl.BlockSpec((tok, blk), lambda i: (0, jnp.minimum(i, q_steps - 1))),
                   const_spec((tok, nk)), const_spec((tok, nk))],
        out_shape=[jax.ShapeDtypeStruct((tok, width), BF16), jax.ShapeDtypeStruct((tok, 128), F32),
                   jax.ShapeDtypeStruct((tok, nq), BF16), jax.ShapeDtypeStruct((tok, nk), BF16),
                   jax.ShapeDtypeStruct((tok, nk), BF16)],
        scratch_shapes=[pltpu.VMEM((tok, width), BF16), pltpu.VMEM((3, width, blk), BF16), pltpu.SemaphoreType.DMA((5,)),
                        pltpu.SemaphoreType.DMA((3,))],
        compiler_params=params(62), cost_estimate=cost(2 * tok * width * (nq + 2 * nk), 2 * width * (nq + 2 * nk)),
    )(ha, hb, gain, cos, sin, wq, wk, wv)


def heads_grad_kernel(steps, ga, gb, w, *refs):
    out, gs, ws, sem, wsem = refs[-5:]
    step = pl.program_id(0)
    half = ga.shape[0]
    slots, blk = ws.shape[:2]

    def load(i):
        return pltpu.make_async_copy(w.at[pl.ds(pl.multiple_of(i * blk, blk), blk)], ws.at[i % slots], wsem.at[i % slots])

    @pl.when(step == 0)
    def _():
        loads = [pltpu.make_async_copy(ga, gs.at[pl.ds(0, half)], sem.at[0]),
                 pltpu.make_async_copy(gb, gs.at[pl.ds(half, half)], sem.at[1])]
        for c in loads:
            c.start()
        load(0).start()
        for c in loads:
            c.wait()
        for i in range(1, slots):
            load(i).start()

    @pl.when((step > 0) & (step + slots - 1 < steps))
    def _():
        load(step + slots - 1).start()

    load(step).wait()
    out[...] = dot(gs[...], ws[step % slots], NT).astype(BF16)


def heads_grad(ga, gb, w_out, *before):
    half, width = ga.shape
    tok = 2 * half
    n = w_out.shape[0]
    blk = 256
    steps = n // blk
    return pl.pallas_call(
        functools.partial(heads_grad_kernel, steps), name="heads_grad", grid=(steps,),
        in_specs=[ANY] * (3 + len(before)), out_specs=pl.BlockSpec((tok, blk), lambda i: (0, i)),
        out_shape=jax.ShapeDtypeStruct((tok, n), BF16),
        scratch_shapes=[pltpu.VMEM((tok, width), BF16), pltpu.VMEM((4, blk, width), BF16), pltpu.SemaphoreType.DMA((2,)),
                        pltpu.SemaphoreType.DMA((4,))],
        compiler_params=params(62), cost_estimate=cost(2 * tok * width * n, 2 * width * n),
    )(ga, gb, w_out, *before)


def by_head(a_ref, b_ref, group):
    def flat(r):
        v = r[...]
        return v.reshape(v.shape[0] * v.shape[2], v.shape[3])

    full = jnp.concatenate([flat(a_ref), flat(b_ref)], axis=0)
    return jnp.concatenate([full[:, h * HEAD_DIM:(h + 1) * HEAD_DIM] for h in range(group)], axis=0)


def put(ref, value):
    ref[...] = value.reshape(ref.shape)


def soft_weights(k, q, down, across):
    allowed = (down[0][:, 0:1] == across[0][0:1, :]) & (down[0][:, 1:2] <= across[0][1:2, :])
    scores = jnp.where(allowed, dot(k, q, NT), -1e30)
    e = jnp.exp2((scores - jnp.max(scores, axis=0, keepdims=True)) * (HEAD_DIM ** -0.5 * LOG2_E))
    return e, 1.0 / jnp.sum(e, axis=0, keepdims=True)


def attend_kernel(group, qa, qb, ka, kb, va, vb, down, across, out):
    q = by_head(qa, qb, group)
    k = by_head(ka, kb, 1)
    v = by_head(va, vb, 1)
    seq = k.shape[0]
    e, scale = soft_weights(k, q, down, across)
    o = dot((e * scale).astype(BF16), v, TN).astype(BF16)
    o = jnp.concatenate([o[h * seq:(h + 1) * seq] for h in range(group)], axis=1)
    put(out, o)


def head_specs(slots, rows, wide):
    return pl.BlockSpec((slots, 1, rows, wide), lambda r, h: (0, r, 0, h))


def mask_specs(seq, group):
    return [pl.BlockSpec((1, seq, 2), lambda r, h: (r, 0, 0)), pl.BlockSpec((1, 2, group * seq), lambda r, h: (r, 0, 0))]


def attend(qa, qb, ka, kb, va, vb, down, across):
    slots, batch, rows, nq = qa.shape
    kv = ka.shape[3] // HEAD_DIM
    group = nq // ka.shape[3]
    seq = 2 * slots * rows
    qs, ks = head_specs(slots, rows, group * HEAD_DIM), head_specs(slots, rows, HEAD_DIM)
    return pl.pallas_call(
        functools.partial(attend_kernel, group), name="attend", grid=(batch, kv),
        in_specs=[qs, qs, ks, ks, ks, ks] + mask_specs(seq, group),
        out_specs=head_specs(2 * slots, rows, group * HEAD_DIM),
        out_shape=jax.ShapeDtypeStruct((2 * slots,) + qa.shape[1:], BF16),
        compiler_params=params(62, "arbitrary", "arbitrary"),
        cost_estimate=cost(batch * kv * group * seq * seq * HEAD_DIM * 40, 4 * qa.size * 2),
    )(qa, qb, ka, kb, va, vb, down, across)


def attend_back_kernel(group, qa, qb, ka, kb, va, vb, ga, gb, down, across, ca, cb, sa, sb, dq_out, dk_out, dv_out):
    q = by_head(qa, qb, group)
    g = by_head(ga, gb, group)
    k = by_head(ka, kb, 1)
    v = by_head(va, vb, 1)
    cos, sin = by_head(ca, cb, 1) * HEAD_DIM ** -0.5, by_head(sa, sb, 1) * HEAD_DIM ** -0.5
    seq = k.shape[0]
    e, scale = soft_weights(k, q, down, across)
    probs = e * scale
    gp = dot(v, g, NT)
    dots = jnp.sum(probs * gp, axis=0, keepdims=True)
    ds = (probs * (gp - dots)).astype(BF16)
    dv = dot(probs.astype(BF16), g).astype(BF16)
    dk = dot(ds, q)
    dq = dot(ds, k, TN)

    def unrotated(x):
        return (x * cos - swap_pairs(x) * sin).astype(BF16)

    dq = jnp.concatenate([unrotated(dq[h * seq:(h + 1) * seq]) for h in range(group)], axis=1)
    dk = unrotated(dk)
    put(dq_out, dq)
    put(dk_out, dk)
    put(dv_out, dv)


def attend_back(qa, qb, ka, kb, va, vb, ga, gb, down, across, ca, cb, sa, sb):
    slots, batch, rows, nq = qa.shape
    kv = ka.shape[3] // HEAD_DIM
    group = nq // ka.shape[3]
    seq = 2 * slots * rows
    qs, ks = head_specs(slots, rows, group * HEAD_DIM), head_specs(slots, rows, HEAD_DIM)
    ts = pl.BlockSpec((slots, 1, rows, HEAD_DIM), lambda r, h: (0, r, 0, 0))
    return pl.pallas_call(
        functools.partial(attend_back_kernel, group), name="attend_back", grid=(batch, kv),
        in_specs=[qs, qs, ks, ks, ks, ks, qs, qs] + mask_specs(seq, group) + [ts, ts, ts, ts],
        out_specs=[head_specs(2 * slots, rows, wide) for wide in (group * HEAD_DIM, HEAD_DIM, HEAD_DIM)],
        out_shape=[jax.ShapeDtypeStruct((2 * slots,) + x.shape[1:], BF16) for x in (qa, ka, va)],
        compiler_params=params(62, "arbitrary", "arbitrary"),
        cost_estimate=cost(batch * kv * group * seq * seq * HEAD_DIM * 60, 8 * qa.size * 2),
    )(qa, qb, ka, kb, va, vb, ga, gb, down, across, ca, cb, sa, sb)


def out_share_kernel(o, w, *outs):
    r = dot(o[...], w[...])
    rows = outs[0].shape[0]
    for i, out in enumerate(outs):
        out[...] = r[i * rows:(i + 1) * rows].astype(out.dtype)


def out_share(o, w_out, types):
    tok, n = o.shape
    width = w_out.shape[1]
    blk = 1024
    rows = tok // len(types)
    return pl.pallas_call(
        out_share_kernel, name="out_share", grid=(width // blk,),
        in_specs=[const_spec((tok, n)), pl.BlockSpec((n, blk), lambda i: (0, i))],
        out_specs=[pl.BlockSpec((rows, blk), lambda i: (0, i))] * len(types),
        out_shape=[jax.ShapeDtypeStruct((rows, width), t) for t in types],
        compiler_params=params(62), cost_estimate=cost(2 * tok * width * n, 2 * width * n),
    )(o, w_out)


def norm_share_kernel(dq, dk, dv, wq, wk, wv, h0, h1, h2, h3, inv_a, inv_b, d0, d1, d2, d3, gain):
    r = dot(dq[...], wq[...], NT) + dot(dk[...], wk[...], NT) + dot(dv[...], wv[...], NT)
    rows = d0.shape[0]
    total = 0.0
    for i, (h, d) in enumerate(((h0, d0), (h1, d1), (h2, d2), (h3, d3))):
        part = r[i * rows:(i + 1) * rows]
        d[...] = part.astype(d.dtype)
        inv = (inv_a, inv_b)[i // 2][(i % 2) * rows:(i % 2 + 1) * rows, :1]
        total = total + jnp.sum(part * (h[...].astype(F32) * inv), axis=0, keepdims=True)
    gain[...] = total


def norm_share(dq, dk, dv, wq, wk, wv, h, inv_a, inv_b):
    tok, nq = dq.shape
    nk = dk.shape[1]
    width = wq.shape[0]
    blk = 1024
    spec = pl.BlockSpec((tok // 4, blk), lambda i: (0, i))
    return pl.pallas_call(
        norm_share_kernel, name="norm_share", grid=(width // blk,),
        in_specs=[const_spec((tok, nq)), const_spec((tok, nk)), const_spec((tok, nk)),
                  pl.BlockSpec((blk, nq), lambda i: (i, 0)), pl.BlockSpec((blk, nk), lambda i: (i, 0)),
                  pl.BlockSpec((blk, nk), lambda i: (i, 0)), spec, spec, spec, spec,
                  const_spec((tok // 2, 128)), const_spec((tok // 2, 128))],
        out_specs=[spec] * 4 + [pl.BlockSpec((1, blk), lambda i: (0, i))],
        out_shape=[jax.ShapeDtypeStruct((tok // 4, width), BF16)] * 4 + [jax.ShapeDtypeStruct((1, width), F32)],
        compiler_params=params(62), cost_estimate=cost(2 * tok * width * (nq + 2 * nk), 2 * width * (nq + 2 * nk)),
    )(dq, dk, dv, wq, wk, wv, *h, inv_a, inv_b)


def weight_grads_kernel(steps, na, nb, dq, dk, dv, o, g0, g1, g2, g3, p0, p1, p2, h, gq, gk, gv, g_out, out, ot):
    step = pl.program_id(0)

    @pl.when(step < steps)
    def _():
        n = jnp.concatenate([na[...], nb[...]], axis=0).T
        for d, grad in ((dq, gq), (dk, gk), (dv, gv)):
            grad[...] = dot(n, d[...])

    @pl.when(step == steps)
    def _():
        for c in range(0, o.shape[1], 256):
            ot[c:c + 256, :] = o[:, c:c + 256].T

    @pl.when(step >= steps)
    def _():
        g_out[...] = dot(ot[...], jnp.concatenate([g0[...], g1[...], g2[...], g3[...]], axis=0))
        share = sum(x[...].astype(F32) for x in (p0, p1, p2))
        out[...] = (h[...].astype(F32) + share.astype(BF16).astype(F32)).astype(BF16)


def weight_grads(na, nb, dq, dk, dv, o, g, p, h):
    tok, nq = dq.shape
    nk = dk.shape[1]
    width = na.shape[1]
    blk = 1024
    steps = width // blk

    def early(i):
        return jnp.minimum(i, steps - 1)

    def late(i):
        return jnp.maximum(i - steps, 0)

    rows = pl.BlockSpec((tok // 4, blk), lambda i: (0, late(i)))
    return pl.pallas_call(
        functools.partial(weight_grads_kernel, steps), name="weight_grads", grid=(2 * steps,),
        in_specs=[pl.BlockSpec((tok // 2, blk), lambda i: (0, early(i)))] * 2 + [const_spec((tok, nq))] + [const_spec((tok, nk))] * 2
        + [const_spec((tok, nq))] + [rows] * 8,
        out_specs=[pl.BlockSpec((blk, n), lambda i: (early(i), 0)) for n in (nq, nk, nk)] + [pl.BlockSpec((nq, blk), lambda i: (0, late(i))), rows],
        out_shape=[jax.ShapeDtypeStruct((width, n), F32) for n in (nq, nk, nk)]
        + [jax.ShapeDtypeStruct((nq, width), F32), jax.ShapeDtypeStruct(h.shape, BF16)],
        scratch_shapes=[pltpu.VMEM((nq, tok), BF16)],
        compiler_params=params(62), cost_estimate=cost(4 * tok * width * (nq + nk), 8 * width * (nq + nk)),
    )(na, nb, dq, dk, dv, o, *g, *p, h)


def norm_back_kernel(d0, d1, d2, h, g, inv, gain, grad, dg):
    rows, width = h.shape
    wide = 1024
    total = jnp.zeros((rows, wide), F32)
    for c in range(0, width, wide):
        at = slice(c, c + wide)
        x = sum(d[:, at].astype(F32) for d in (d0, d1, d2)) * gain[:, at]
        dg[:, at] = x
        total = total + x * h[:, at].astype(F32)
    s = inv[:, :1]
    back = (s * s * s) * (jnp.sum(total, axis=-1, keepdims=True) / width)
    s = jnp.broadcast_to(s, (rows, wide))
    back = jnp.broadcast_to(back, (rows, wide))
    for c in range(0, width, wide):
        at = slice(c, c + wide)
        grad[:, at] = (g[:, at].astype(F32) + (s * dg[:, at] - h[:, at].astype(F32) * back)).astype(BF16)


def norm_back(d, h, g, inv, gain):
    tok, width = h.shape
    blk = 48
    spec = pl.BlockSpec((blk, width), lambda i: (i, 0))
    return pl.pallas_call(
        norm_back_kernel, name="norm_back", grid=(tok // blk,),
        in_specs=[spec] * 5 + [pl.BlockSpec((blk, 128), lambda i: (i, 0)), const_spec((1, width))],
        out_specs=spec, out_shape=jax.ShapeDtypeStruct((tok, width), BF16), scratch_shapes=[pltpu.VMEM((blk, width), F32)],
        compiler_params=params(62), cost_estimate=cost(20 * tok * width, 12 * tok * width),
    )(*d, h, g, inv, gain)


def solution(mesh):
    tp_size = mesh.shape['tp']
    beside = [(i, i ^ 1) for i in range(tp_size)]
    across = [(i, i ^ 2) for i in range(tp_size)]
    diagonal = [(i, i ^ 3) for i in range(tp_size)]

    def send(x, pairs):
        return lax.ppermute(x, 'tp', pairs)

    def after(x, *others):
        return lax.optimization_barrier((x,) + others)[0]

    def step(hidden, positions, doc_ids, norm_gain, w_query, w_key, w_value, w_out, grad_out):
        batch, rows, width = hidden.shape
        tok = batch * rows
        nq, nk = w_query.shape[1], w_key.shape[1]
        group = nq // nk
        gain = norm_gain.astype(F32).reshape(1, width)

        pos1, doc1 = send(positions, beside), send(doc_ids, beside)
        pos2, doc2 = send(positions, across), send(doc_ids, across)
        h0 = hidden.reshape(tok, width)
        g0 = grad_out.reshape(tok, width)
        h2 = send(h0, across)
        h1 = send(h0, beside)
        g1 = send(g0, beside)
        g2 = send(g0, across)
        h3 = send(h2, beside)

        lane = jnp.arange(HEAD_DIM)
        inv_freq = ROPE_BASE ** (-(lane // 2 * 2).astype(F32) / HEAD_DIM)
        sign = jnp.where(lane % 2 == 0, -1.0, 1.0)

        def tables(*pos):
            angles = jnp.stack(pos).astype(F32)[..., None] * inv_freq
            return jnp.cos(angles), jnp.sin(angles) * sign

        def heads(x):
            return x.reshape(2, batch, rows, x.shape[1])

        def flat(x):
            return x.reshape(x.shape[0] * tok, x.shape[3])

        ca, sa = tables(positions, pos1)
        na, inv_a, qa, ka, va = qkv(h0, h1, gain, ca.reshape(2 * tok, HEAD_DIM), sa.reshape(2 * tok, HEAD_DIM), w_query, w_key, w_value)
        pos2, doc2, ka = lax.optimization_barrier((pos2, doc2, ka))
        pos3, doc3 = send(pos2, beside), send(doc2, beside)
        cb, sb = tables(pos2, pos3)
        both = jnp.stack([jnp.concatenate([doc_ids, doc1, doc2, doc3], axis=1), jnp.concatenate([positions, pos1, pos2, pos3], axis=1)], axis=1)
        down, over = jnp.swapaxes(both, 1, 2), jnp.tile(both, (1, 1, group))
        dha = heads_grad(g0, g1, w_out, ka, cb, sb, down, over)
        nb, inv_b, qb, kb, vb = qkv(h2, h3, gain, cb.reshape(2 * tok, HEAD_DIM), sb.reshape(2 * tok, HEAD_DIM), w_query, w_key, w_value)
        saved = [heads(x) for x in (qa, qb, ka, kb, va, vb)]
        o = flat(attend(*saved, down, over))

        p0, p1, p2, p3 = out_share(o, w_out, (BF16, BF16, F32, BF16))
        g3 = send(after(g2, p2), beside)
        p3 = send(p3, beside)
        p1 = send(p1, beside)
        dhb = heads_grad(g2, g3, w_out)
        s2 = (p2 + after(p3, dhb).astype(F32)).astype(BF16)
        s2, dhb = lax.optimization_barrier((s2, dhb))
        s2 = send(s2, across)
        grads = attend_back(*saved, heads(dha), heads(dhb), down, over, ca, cb, sa, sb)
        dq, dk, dv = [flat(x) for x in grads]
        d0, d1, d2, d3, gg = norm_share(dq, dk, dv, w_query, w_key, w_value, (h0, h1, h2, h3), inv_a, inv_b)
        d3 = send(d3, beside)
        d1 = send(d1, beside)
        t2 = (d2.astype(F32) + d3.astype(F32)).astype(BF16)
        t2, gg, dq = lax.optimization_barrier((t2, gg, dq))
        t2 = send(t2, across)
        gg1, gg2, gg3 = send(gg, beside), send(gg, across), send(gg, diagonal)
        gq, gk, gv, g_out, attn_out = weight_grads(na, nb, dq, dk, dv, o, (g0, g1, g2, g3), (p0, p1, s2), h0)
        grad_hidden = norm_back((after(d0, gk), d1, t2), h0, g0, inv_a, gain)
        grad_gain = ((gg + gg1) + (gg2 + gg3)).reshape(width)
        attn_out, grad_hidden = attn_out.reshape(hidden.shape), grad_hidden.reshape(hidden.shape)
        return (attn_out, grad_hidden, grad_gain, gq, gk, gv, g_out)

    row_spec = P('dp', 'tp', None)
    tok_spec = P('dp', 'tp')
    col_spec = P(None, 'tp')

    return jax.shard_map(
        step, mesh=mesh,
        in_specs=(row_spec, tok_spec, tok_spec, P(), col_spec, col_spec, col_spec, P('tp', None), row_spec),
        out_specs=(row_spec, row_spec, P('dp'), P('dp', 'tp'), P('dp', 'tp'), P('dp', 'tp'), P(('dp', 'tp'), None)),
        check_vma=False)
```

time: 450 us -> 374 us (0.83)
  Pallas kernels: 299 us -> 240 us
  local copies, waits for them, and re-layouts: 16.3 us -> 1.4 us
  other arithmetic: 21.6 us -> 17.1 us
    pallas_call x2 -> x1, Pallas kernels: 52.6 us -> 32 us  [norm_share(): pl.pallas_call(norm_share_kernel, name='norm_share', grid=(width // blk,)...]
    pallas_call x2, Pallas kernels: 59.3 us -> 44.7 us  [qkv(): pl.pallas_call(functools.partial(qkv_kernel, q_steps), name='qkv', grid=(...]
    pallas_call x2 -> x1, Pallas kernels: 38.4 us -> 25 us  [out_share(): pl.pallas_call(out_share_kernel, name='out_share', grid=(width // blk,),...]
    add x4 -> x1, other arithmetic: 7.96 us -> 0.68 us  [step(): grad_gain = (gg + gg1 + (gg2 + gg3)).reshape(width)]
    unnamed x18 -> x6, local copies, waits for them, and re-layouts: 7.02 us -> 0.01 us
    pallas_call x4 -> x3, Pallas kernels: 115 us -> 109 us  [the longest x1 76.8 us: weight_grads(): pl.pallas_call(functools.partial(weight_grads_kernel, steps), name='weigh...]
    ppermute x17 -> x21, starting transfers between devices: 9.21 us -> 11.9 us  [send(): return lax.ppermute(x, 'tp', pairs)]
    convert_element_type x3 -> x6, other arithmetic: 11.8 us -> 9.35 us  [the longest x1 4.97 us: step(): s2 = (p2 + after(p3, dhb).astype(F32)).astype(BF16)]
  transfers between devices with their start and end apart: 17 -> 21, of which waited for: 6 -> 4; matrix products, arithmetic and copies ran while one was open for 5% -> 4% of each run, Pallas kernels for 38% -> 50%
where the time goes in v2:
time: 374 us; the launch traced here: 373 us
  Pallas kernels  240 us (64%)
  waiting for transfers between devices  102 us (27%)
  other arithmetic  17.1 us (5%)
  starting transfers between devices  11.9 us (3%)
    ppermute x21, waiting for transfers between devices, send(): return lax.ppermute(x, 'tp', pairs)  102 us
    pallas_call x1, Pallas kernels, weight_grads(): pl.pallas_call(functools.partial(weight_grads_kernel, steps), name='weigh...  76.8 us
    pallas_call x2, Pallas kernels, qkv(): pl.pallas_call(functools.partial(qkv_kernel, q_steps), name='qkv', grid=(...  44.7 us
    pallas_call x1, Pallas kernels, norm_share(): pl.pallas_call(norm_share_kernel, name='norm_share', grid=(width // blk,)...  32 us
    pallas_call x2, Pallas kernels, heads_grad(): pl.pallas_call(functools.partial(heads_grad_kernel, steps), name='heads_g...  31.8 us
    pallas_call x1, Pallas kernels, out_share(): pl.pallas_call(out_share_kernel, name='out_share', grid=(width // blk,),...  25 us
    pallas_call x1, Pallas kernels, attend_back(): pl.pallas_call(functools.partial(attend_back_kernel, group), name='attend...  13 us
    ppermute x21, starting transfers between devices, send(): return lax.ppermute(x, 'tp', pairs)  11.9 us
  transfers between devices with their start and end apart: 21, of which 4 were waited for; matrix products, arithmetic and copies ran while one was open for 4% of the time, Pallas kernels for 50%

profile of v2, /device:TPU:0, one launch (start us, length us, event | category | flops | bytes accessed | tf_op | source)
XLA Modules:
  0.0 373.0 jit_solution(15424921839958572003)
XLA Ops:
  0.6 3.3 collective-permute-start.2
  4.0 0.1 collective-permute-start.4
  4.0 0.4 collective-permute-start.1
  4.5 1.7 collective-permute-start.5
  6.2 49.4 %collective-permute-done.2.ha.h2 = bf16[144,8192]{1,0:T(8,128)(2,1)} collective-permute-done((bf16[144,8192]{1,0:T(8,128)(2,1)}, bf16[144,8192]{1,0:T(8,128)(2,1)}, u32[]{:S(2)}, u32[]{:S(2)}) %collective-permute-start.2) | collective-permute-done | bytes 2359328 | tf_op jit(solution)/shard_map/ppermute | solution.py:417
  55.6 1.3 reshape.172
  56.9 0.7 add_convert_fusion.2
  57.6 0.1 convert_element_type.56
  57.7 1.3 fusion
  59.0 22.4 %qkv.2 = (bf16[288,8192]{1,0:T(8,128)(2,1)}, f32[288,128]{1,0:T(8,128)}, bf16[288,2048]{1,0:T(8,128)(2,1)}, bf16[288,256]{1,0:T(8,128)(2,1)}, bf16[288,256]{1,0:T(8,128)(2,1)}) custom-call(bf16[144,8192]{1,0:T(8,128)(2,1)} %bitcast.40, bf16[144,8192]{1,0:T(8,128)(2,1)} %collective-permute-done.hb.h1, f32[1,8192]{1,0:T(1,128)} %bitcast.52, ...), custom_call_target="tpu_custom_call" | custom-call | flops 12079595520 | bytes 41943040 | tf_op jit(solution)/shard_map/qkv/pallas_call | solution.py:124
  81.4 0.5 collective-permute-start.6
  82.0 1.7 collective-permute-start.11
  83.7 0.2 collective-permute-start.7
  83.9 0.3 collective-permute-start.9
  84.2 0.1 add_bitcast_fusion.1
  84.3 0.1 convert_element_type.59
  84.4 0.2 copy.24
  84.6 4.0 %collective-permute-done.9 = s32[3,48]{1,0:T(4,128)S(1)} collective-permute-done((s32[3,48]{1,0:T(4,128)S(1)}, s32[3,48]{1,0:T(4,128)S(1)}, u32[]{:S(2)}, u32[]{:S(2)}) %collective-permute-start.9) | collective-permute-done | bytes 608 | tf_op jit(solution)/shard_map/ppermute | solution.py:417
  88.6 0.1 add_bitcast_fusion
  88.7 0.2 copy.23
  88.8 0.1 pad_add_fusion
  89.0 0.1 copy.25
  89.2 0.7 tile.10.refs_4_.across
  89.9 0.9 fusion.9.refs_3_.down
  90.8 1.3 fusion.1
  92.1 22.3 %qkv.3 = (bf16[288,8192]{1,0:T(8,128)(2,1)}, f32[288,128]{1,0:T(8,128)}, bf16[288,2048]{1,0:T(8,128)(2,1)}, bf16[288,256]{1,0:T(8,128)(2,1)}, bf16[288,256]{1,0:T(8,128)(2,1)}) custom-call(bf16[144,8192]{1,0:T(8,128)(2,1)} %collective-permute-done.2.ha.h2, bf16[144,8192]{1,0:T(8,128)(2,1)} %collective-permute-done.3.hb.h3, f32[1,8192]{1,0:T(1,128)} %bitcast.53, ...), custom_call_target="tpu_custom_call" | custom-call | flops 12079595520 | bytes 41943040 | tf_op jit(solution)/shard_map/qkv/pallas_call | solution.py:124
  114.4 8.4 %attend.1 = bf16[4,3,48,2048]{3,2,1,0:T(8,128)(2,1)} custom-call(bf16[2,3,48,2048]{3,2,1,0:T(8,128)(2,1)} %bitcast.66, bf16[2,3,48,2048]{3,2,1,0:T(8,128)(2,1)} %bitcast.68, bf16[2,3,48,256]{3,2,1,0:T(8,128)(2,1)} %bitcast.55, bf16[2,3,48,256]{3,2,1,0:T(8,128)(2,1)} %bitcast.72, bf16[2,3,48,256]{3,2,1,0:T(8,128)(2,1)} %bitcast.70, ...), custom_call_target="tpu_custom_call" | custom-call | flops 9059696640 | bytes 4718592 | tf_op jit(solution)/shard_map/attend/pallas_call | solution.py:229
  122.9 25.0 %out_share.1 = (bf16[144,8192]{1,0:T(8,128)(2,1)}, bf16[144,8192]{1,0:T(8,128)(2,1)}, f32[144,8192]{1,0:T(8,128)}, bf16[144,8192]{1,0:T(8,128)(2,1)}) custom-call(bf16[576,2048]{1,0:T(8,128)(2,1)} %bitcast.76, bf16[2048,8192]{1,0:T(8,128)(2,1)} %w.5), custom_call_target="tpu_custom_call" | custom-call | flops 19327352832 | bytes 33554432 | tf_op jit(solution)/shard_map/out_share/pallas_call | solution.py:294
  147.9 0.2 collective-permute-start.12
  148.1 0.3 collective-permute-start.10
  148.4 2.0 fusion.3
  150.4 15.9 %heads_grad.2 = bf16[288,2048]{1,0:T(8,128)(2,1)} custom-call(bf16[144,8192]{1,0:T(8,128)(2,1)} %bitcast.46, bf16[144,8192]{1,0:T(8,128)(2,1)} %collective-permute-done.7.gb.g1, bf16[2048,8192]{1,0:T(8,128)(2,1)} %w.5, bf16[288,256]{1,0:T(8,128)(2,1)} %get-tuple-element.51.refs_0_, f32[2,3,48,128]{3,2,1,0:T(8,128)} %get-tuple-element.91.refs_1_.cb, ...), custom_call_target="tpu_custom_call" | custom-call | flops 9663676416 | bytes 33554432 | tf_op jit(solution)/shard_map/heads_grad/pallas_call | solution.py:174
  166.2 15.9 %heads_grad.3 = bf16[288,2048]{1,0:T(8,128)(2,1)} custom-call(bf16[144,8192]{1,0:T(8,128)(2,1)} %collective-permute-done.11.ga.g2, bf16[144,8192]{1,0:T(8,128)(2,1)} %collective-permute-done.12.gb.g3, bf16[2048,8192]{1,0:T(8,128)(2,1)} %w.5), custom_call_target="tpu_custom_call" | custom-call | flops 9663676416 | bytes 33554432 | tf_op jit(solution)/shard_map/heads_grad/pallas_call | solution.py:174
  182.2 5.0 %add_convert_fusion.1 = bf16[144,8192]{1,0:T(8,128)(2,1)} fusion(f32[144,8192]{1,0:T(8,128)} %get-tuple-element.56, bf16[144,8192]{1,0:T(8,128)(2,1)} %collective-permute-done.10), kind=kLoop, calls=%fused_computation.1 | loop fusion | flops 3538944 | bytes 9437184 | tf_op jit(solution)/shard_map/convert_element_type | solution.py:470
  187.1 13.0 %attend_back.1 = (bf16[4,3,48,2048]{3,2,1,0:T(8,128)(2,1)}, bf16[4,3,48,256]{3,2,1,0:T(8,128)(2,1)}, bf16[4,3,48,256]{3,2,1,0:T(8,128)(2,1)}) custom-call(bf16[2,3,48,2048]{3,2,1,0:T(8,128)(2,1)} %bitcast.67, bf16[2,3,48,2048]{3,2,1,0:T(8,128)(2,1)} %bitcast.69, bf16[2,3,48,256]{3,2,1,0:T(8,128)(2,1)} %bitcast.56, bf16[2,3,48,256]{3,2,1,0:T(8,128)(2,1)} %bitcast.73, ...), custom_call_target="tpu_custom_call" | custom-call | flops 13589544960 | bytes 9437184 | tf_op jit(solution)/shard_map/attend_back/pallas_call | solution.py:272
  200.2 32.0 %norm_share.1 = (bf16[144,8192]{1,0:T(8,128)(2,1)}, bf16[144,8192]{1,0:T(8,128)(2,1)}, bf16[144,8192]{1,0:T(8,128)(2,1)}, bf16[144,8192]{1,0:T(8,128)(2,1)}, f32[1,8192]{1,0:T(1,128)}) custom-call(bf16[576,2048]{1,0:T(8,128)(2,1)} %bitcast.78, bf16[576,256]{1,0:T(8,128)(2,1)} %bitcast.81, bf16[576,256]{1,0:T(8,128)(2,1)} %bitcast.83, bf16[8192,2048]{1,0:T(8,128)(2,1)} %wq.5, ...), custom_call_target="tpu_custom_call" | custom-call | flops 24159191040 | bytes 41943040 | tf_op jit(solution)/shard_map/norm_share/pallas_call | solution.py:321
  232.2 0.2 collective-permute-start.13
  232.4 0.3 collective-permute-start.14
  232.7 0.3 collective-permute-start.15
  233.0 3.9 %collective-permute-done.13 = bf16[144,8192]{1,0:T(8,128)(2,1)S(1)} collective-permute-done((bf16[144,8192]{1,0:T(8,128)(2,1)}, bf16[144,8192]{1,0:T(8,128)(2,1)S(1)}, u32[]{:S(2)}, u32[]{:S(2)}) %collective-permute-start.13) | collective-permute-done | bytes 2359328 | tf_op jit(solution)/shard_map/ppermute | solution.py:417
  237.0 3.7 add_convert_fusion
  240.6 0.1 collective-permute-start.20
  240.7 1.7 collective-permute-start.19
  242.5 44.6 %collective-permute-done.15.p2 = bf16[144,8192]{1,0:T(8,128)(2,1)} collective-permute-done((bf16[144,8192]{1,0:T(8,128)(2,1)}, bf16[144,8192]{1,0:T(8,128)(2,1)}, u32[]{:S(2)}, u32[]{:S(2)}) %collective-permute-start.15) | collective-permute-done | bytes 2359328 | tf_op jit(solution)/shard_map/ppermute | solution.py:417
  287.1 0.3 collective-permute-start.17
  287.4 76.8 %weight_grads.1 = (f32[8192,2048]{1,0:T(8,128)}, f32[8192,256]{1,0:T(8,128)}, f32[8192,256]{1,0:T(8,128)}, f32[2048,8192]{1,0:T(8,128)}, bf16[144,8192]{1,0:T(8,128)(2,1)}) custom-call(bf16[288,8192]{1,0:T(8,128)(2,1)} %get-tuple-element.45.na, bf16[288,8192]{1,0:T(8,128)(2,1)} %get-tuple-element.48.nb, bf16[576,2048]{1,0:T(8,128)(2,1)} %bitcast.79, ...), custom_call_target="tpu_custom_call" | custom-call | flops 43486543872 | bytes 150994944 | tf_op jit(solution)/shard_map/weight_grads/pallas_call | solution.py:368
  364.2 0.7 add_add_fusion
  364.8 8.2 %norm_back.1 = bf16[144,8192]{1,0:T(8,128)(2,1)} custom-call(bf16[144,8192]{1,0:T(8,128)(2,1)} %get-tuple-element.76.d0, bf16[144,8192]{1,0:T(8,128)(2,1)} %collective-permute-done.16.d1, bf16[144,8192]{1,0:T(8,128)(2,1)} %collective-permute-done.17.d2, bf16[144,8192]{1,0:T(8,128)(2,1)} %bitcast.43, bf16[144,8192]{1,0:T(8,128)(2,1)} %bitcast.48, ...), custom_call_target="tpu_custom_call" | custom-call | flops 23592960 | bytes 14155776 | tf_op jit(solution)/shard_map/norm_back/pallas_call | solution.py:402
  (33 shorter events, 0.2 us)
Async XLA Ops:
  0.6 54.9 %collective-permute-start.2 = (bf16[144,8192]{1,0:T(8,128)(2,1)}, bf16[144,8192]{1,0:T(8,128)(2,1)}, u32[]{:S(2)}, u32[]{:S(2)}) collective-permute-start(bf16[144,8192]{1,0:T(8,128)(2,1)} %bitcast.38), channel_id=1, source_target_pairs={{0,2},{1,3},{2,0},{3,1},{4,6},{5,7},{6,4},{7,5}} | collective-permute-start | bytes 7077896 | tf_op jit(solution)/shard_map/ppermute | solution.py:417
  4.0 55.0 %collective-permute-start = (bf16[144,8192]{1,0:T(8,128)(2,1)}, bf16[144,8192]{1,0:T(8,128)(2,1)}, u32[]{:S(2)}, u32[]{:S(2)}) collective-permute-start(bf16[144,8192]{1,0:T(8,128)(2,1)} %bitcast.39), channel_id=1, source_target_pairs={{0,1},{1,0},{2,3},{3,2},{4,5},{5,4},{6,7},{7,6}} | collective-permute-start | bytes 7077896 | tf_op jit(solution)/shard_map/ppermute | solution.py:417
  4.0 77.4 %collective-permute-start.4 = (s32[3,48]{1,0:T(4,128)}, s32[3,48]{1,0:T(4,128)S(1)}, u32[]{:S(2)}, u32[]{:S(2)}) collective-permute-start(s32[3,48]{1,0:T(4,128)} %param.10), channel_id=1, source_target_pairs={{0,2},{1,3},{2,0},{3,1},{4,6},{5,7},{6,4},{7,5}} | collective-permute-start | bytes 1736 | tf_op jit(solution)/shard_map/ppermute | solution.py:417
  4.0 52.9 %collective-permute-start.1 = (s32[3,48]{1,0:T(4,128)}, s32[3,48]{1,0:T(4,128)S(1)}, u32[]{:S(2)}, u32[]{:S(2)}) collective-permute-start(s32[3,48]{1,0:T(4,128)} %param.10), channel_id=1, source_target_pairs={{0,1},{1,0},{2,3},{3,2},{4,5},{5,4},{6,7},{7,6}} | collective-permute-start | bytes 1736 | tf_op jit(solution)/shard_map/ppermute | solution.py:417
  4.5 76.9 %collective-permute-start.5 = (s32[3,48]{1,0:T(4,128)}, s32[3,48]{1,0:T(4,128)S(1)}, u32[]{:S(2)}, u32[]{:S(2)}) collective-permute-start(s32[3,48]{1,0:T(4,128)} %param.11), channel_id=1, source_target_pairs={{0,2},{1,3},{2,0},{3,1},{4,6},{5,7},{6,4},{7,5}} | collective-permute-start | bytes 1736 | tf_op jit(solution)/shard_map/ppermute | solution.py:417
  55.6 36.5 %collective-permute-start.3 = (bf16[144,8192]{1,0:T(8,128)(2,1)}, bf16[144,8192]{1,0:T(8,128)(2,1)}, u32[]{:S(2)}, u32[]{:S(2)}) collective-permute-start(bf16[144,8192]{1,0:T(8,128)(2,1)} %collective-permute-done.2.ha.h2), channel_id=1, source_target_pairs={{0,1},{1,0},{2,3},{3,2},{4,5},{5,4},{6,7},{7,6}} | collective-permute-start | bytes 7077896 | tf_op jit(solution)/shard_map/ppermute | solution.py:417
  59.0 22.9 %copy-start.2 = (s32[3,48]{1,0:T(4,128)S(1)}, s32[3,48]{1,0:T(4,128)}, u32[]{:S(2)}) copy-start(s32[3,48]{1,0:T(4,128)} %param.11) | copy-start | bytes 1732
  59.0 25.2 %copy-start.1 = (s32[3,48]{1,0:T(4,128)S(1)}, s32[3,48]{1,0:T(4,128)}, u32[]{:S(2)}) copy-start(s32[3,48]{1,0:T(4,128)} %param.10) | copy-start | bytes 1732
  81.4 2.5 collective-permute-start.6
  81.9 2.6 collective-permute-start.8
  82.0 65.9 %collective-permute-start.11 = (bf16[144,8192]{1,0:T(8,128)(2,1)}, bf16[144,8192]{1,0:T(8,128)(2,1)}, u32[]{:S(2)}, u32[]{:S(2)}) collective-permute-start(bf16[144,8192]{1,0:T(8,128)(2,1)} %bitcast.44), channel_id=1, source_target_pairs={{0,2},{1,3},{2,0},{3,1},{4,6},{5,7},{6,4},{7,5}} | collective-permute-start | bytes 7077896 | tf_op jit(solution)/shard_map/ppermute | solution.py:417
  83.7 66.6 %collective-permute-start.7 = (bf16[144,8192]{1,0:T(8,128)(2,1)}, bf16[144,8192]{1,0:T(8,128)(2,1)}, u32[]{:S(2)}, u32[]{:S(2)}) collective-permute-start(bf16[144,8192]{1,0:T(8,128)(2,1)} %bitcast.45), channel_id=1, source_target_pairs={{0,1},{1,0},{2,3},{3,2},{4,5},{5,4},{6,7},{7,6}} | collective-permute-start | bytes 7077896 | tf_op jit(solution)/shard_map/ppermute | solution.py:417
  83.9 4.7 %collective-permute-start.9 = (s32[3,48]{1,0:T(4,128)S(1)}, s32[3,48]{1,0:T(4,128)S(1)}, u32[]{:S(2)}, u32[]{:S(2)}) collective-permute-start(s32[3,48]{1,0:T(4,128)S(1)} %collective-permute-done.5), channel_id=1, source_target_pairs={{0,1},{1,0},{2,3},{3,2},{4,5},{5,4},{6,7},{7,6}} | collective-permute-start | bytes 1736 | tf_op jit(solution)/shard_map/ppermute | solution.py:417
  147.9 18.4 %collective-permute-start.12 = (bf16[144,8192]{1,0:T(8,128)(2,1)}, bf16[144,8192]{1,0:T(8,128)(2,1)}, u32[]{:S(2)}, u32[]{:S(2)}) collective-permute-start(bf16[144,8192]{1,0:T(8,128)(2,1)} %collective-permute-done.11.ga.g2), channel_id=1, source_target_pairs={{0,1},{1,0},{2,3},{3,2},{4,5},{5,4},{6,7},{7,6}} | collective-permute-start | bytes 7077896 | tf_op jit(solution)/shard_map/ppermute | solution.py:417
  148.1 34.1 %collective-permute-start.10 = (bf16[144,8192]{1,0:T(8,128)(2,1)}, bf16[144,8192]{1,0:T(8,128)(2,1)}, u32[]{:S(2)}, u32[]{:S(2)}) collective-permute-start(bf16[144,8192]{1,0:T(8,128)(2,1)} %get-tuple-element.57), channel_id=1, source_target_pairs={{0,1},{1,0},{2,3},{3,2},{4,5},{5,4},{6,7},{7,6}} | collective-permute-start | bytes 7077896 | tf_op jit(solution)/shard_map/ppermute | solution.py:417
  232.2 4.8 %collective-permute-start.13 = (bf16[144,8192]{1,0:T(8,128)(2,1)}, bf16[144,8192]{1,0:T(8,128)(2,1)S(1)}, u32[]{:S(2)}, u32[]{:S(2)}) collective-permute-start(bf16[144,8192]{1,0:T(8,128)(2,1)} %get-tuple-element.67), channel_id=1, source_target_pairs={{0,1},{1,0},{2,3},{3,2},{4,5},{5,4},{6,7},{7,6}} | collective-permute-start | bytes 7077896 | tf_op jit(solution)/shard_map/ppermute | solution.py:417
  232.4 10.1 %collective-permute-start.14 = (bf16[144,8192]{1,0:T(8,128)(2,1)}, bf16[144,8192]{1,0:T(8,128)(2,1)}, u32[]{:S(2)}, u32[]{:S(2)}) collective-permute-start(bf16[144,8192]{1,0:T(8,128)(2,1)} %get-tuple-element.71), channel_id=1, source_target_pairs={{0,1},{1,0},{2,3},{3,2},{4,5},{5,4},{6,7},{7,6}} | collective-permute-start | bytes 7077896 | tf_op jit(solution)/shard_map/ppermute | solution.py:417
  232.7 54.4 %collective-permute-start.15 = (bf16[144,8192]{1,0:T(8,128)(2,1)}, bf16[144,8192]{1,0:T(8,128)(2,1)}, u32[]{:S(2)}, u32[]{:S(2)}) collective-permute-start(bf16[144,8192]{1,0:T(8,128)(2,1)} %add_convert_fusion.1), channel_id=1, source_target_pairs={{0,2},{1,3},{2,0},{3,1},{4,6},{5,7},{6,4},{7,5}} | collective-permute-start | bytes 7077896 | tf_op jit(solution)/shard_map/ppermute | solution.py:417
  233.0 131.8 %collective-permute-start.16 = (bf16[144,8192]{1,0:T(8,128)(2,1)}, bf16[144,8192]{1,0:T(8,128)(2,1)}, u32[]{:S(2)}, u32[]{:S(2)}) collective-permute-start(bf16[144,8192]{1,0:T(8,128)(2,1)} %get-tuple-element.77), channel_id=1, source_target_pairs={{0,1},{1,0},{2,3},{3,2},{4,5},{5,4},{6,7},{7,6}} | collective-permute-start | bytes 7077896 | tf_op jit(solution)/shard_map/ppermute | solution.py:417
  237.0 3.7 copy-start
  240.6 123.5 %collective-permute-start.20 = (f32[1,8192]{1,0:T(1,128)S(1)}, f32[1,8192]{1,0:T(1,128)S(1)}, u32[]{:S(2)}, u32[]{:S(2)}) collective-permute-start(f32[1,8192]{1,0:T(1,128)S(1)} %copy-done), channel_id=1, source_target_pairs={{0,3},{1,2},{2,1},{3,0},{4,7},{5,6},{6,5},{7,4}} | collective-permute-start | bytes 98312 | tf_op jit(solution)/shard_map/ppermute | solution.py:417
  240.7 123.4 %collective-permute-start.19 = (f32[1,8192]{1,0:T(1,128)S(1)}, f32[1,8192]{1,0:T(1,128)S(1)}, u32[]{:S(2)}, u32[]{:S(2)}) collective-permute-start(f32[1,8192]{1,0:T(1,128)S(1)} %copy-done), channel_id=1, source_target_pairs={{0,2},{1,3},{2,0},{3,1},{4,6},{5,7},{6,4},{7,5}} | collective-permute-start | bytes 98312 | tf_op jit(solution)/shard_map/ppermute | solution.py:417
  242.5 121.7 %collective-permute-start.18 = (f32[1,8192]{1,0:T(1,128)S(1)}, f32[1,8192]{1,0:T(1,128)S(1)}, u32[]{:S(2)}, u32[]{:S(2)}) collective-permute-start(f32[1,8192]{1,0:T(1,128)S(1)} %copy-done), channel_id=1, source_target_pairs={{0,1},{1,0},{2,3},{3,2},{4,5},{5,4},{6,7},{7,6}} | collective-permute-start | bytes 98312 | tf_op jit(solution)/shard_map/ppermute | solution.py:417
  287.1 77.8 %collective-permute-start.17 = (bf16[144,8192]{1,0:T(8,128)(2,1)}, bf16[144,8192]{1,0:T(8,128)(2,1)}, u32[]{:S(2)}, u32[]{:S(2)}) collective-permute-start(bf16[144,8192]{1,0:T(8,128)(2,1)} %add_convert_fusion), channel_id=1, source_target_pairs={{0,2},{1,3},{2,0},{3,1},{4,6},{5,7},{6,4},{7,5}} | collective-permute-start | bytes 7077896 | tf_op jit(solution)/shard_map/ppermute | solution.py:417

commit v3 on v2

--- a/solution.py
+++ b/solution.py
@@ -41,12 +41,11 @@
     return jnp.where(lane % 2 == 0, pltpu.roll(x, x.shape[-1] - 1, x.ndim - 1), pltpu.roll(x, 1, x.ndim - 1))
 
 
-def qkv_kernel(q_steps, ha, hb, gain, cos, sin, wq, wk, wv, n_out, inv_out, q_out, k_out, v_out, ns, ws, sem, wsem):
-    step = pl.program_id(0)
+def project(step, ha, hb, gain, cos, sin, wq, wk, wv, n_out, inv_out, q_out, k_out, v_out, ns, ws, sem, wsem):
     half, width = ha.shape
     nk = wk.shape[1]
-    blk = ws.shape[2]
-    slots = ws.shape[0]
+    slots, _, blk = ws.shape
+    q_steps = wq.shape[1] // blk
     save_n = pltpu.make_async_copy(ns, n_out, sem.at[4])
     load_kv = [pltpu.make_async_copy(w, ws.at[q_steps % slots, :, pl.ds(i * nk, nk)], sem.at[2 + i]) for i, w in enumerate((wk, wv))]
 
@@ -103,7 +102,7 @@
     @pl.when(step < q_steps)
     def _():
         load_q(step).wait()
-        q_out[...] = rotated(dot(ns[...], ws[step % slots]))
+        q_out[:, pl.ds(pl.multiple_of(step * blk, blk), blk)] = rotated(dot(ns[...], ws[step % slots]))
 
     @pl.when(step == q_steps)
     def _():
@@ -115,23 +114,25 @@
         save_n.wait()
 
 
+def project_out(tok, width, nq, nk):
+    shapes = [jax.ShapeDtypeStruct((tok, 128), F32)] + [jax.ShapeDtypeStruct((tok, n), BF16) for n in (nq, nk, nk)]
+    return [ANY] + [const_spec(x.shape) for x in shapes], [jax.ShapeDtypeStruct((tok, width), BF16)] + shapes
+
+
+def project_scratch(tok, width, blk):
+    return [pltpu.VMEM((tok, width), BF16), pltpu.VMEM((3, width, blk), BF16), pltpu.SemaphoreType.DMA((5,)), pltpu.SemaphoreType.DMA((3,))]
+
+
 def qkv(ha, hb, gain, cos, sin, wq, wk, wv):
     half, width = ha.shape
     tok = 2 * half
     nq, nk = wq.shape[1], wk.shape[1]
     blk = 2 * nk
-    q_steps = nq // blk
+    specs, shapes = project_out(tok, width, nq, nk)
     return pl.pallas_call(
-        functools.partial(qkv_kernel, q_steps), name="qkv", grid=(q_steps + 1,),
+        lambda *refs: project(pl.program_id(0), *refs), name="qkv", grid=(nq // blk + 1,),
         in_specs=[ANY, ANY, const_spec((1, width)), const_spec((tok, HEAD_DIM)), const_spec((tok, HEAD_DIM)), ANY, ANY, ANY],
-        out_specs=[ANY, const_spec((tok, 128)),
-                   pl.BlockSpec((tok, blk), lambda i: (0, jnp.minimum(i, q_steps - 1))),
-                   const_spec((tok, nk)), const_spec((tok, nk))],
-        out_shape=[jax.ShapeDtypeStruct((tok, width), BF16), jax.ShapeDtypeStruct((tok, 128), F32),
-                   jax.ShapeDtypeStruct((tok, nq), BF16), jax.ShapeDtypeStruct((tok, nk), BF16),
-                   jax.ShapeDtypeStruct((tok, nk), BF16)],
-        scratch_shapes=[pltpu.VMEM((tok, width), BF16), pltpu.VMEM((3, width, blk), BF16), pltpu.SemaphoreType.DMA((5,)),
-                        pltpu.SemaphoreType.DMA((3,))],
+        out_specs=specs, out_shape=shapes, scratch_shapes=project_scratch(tok, width, blk),
         compiler_params=params(62), cost_estimate=cost(2 * tok * width * (nq + 2 * nk), 2 * width * (nq + 2 * nk)),
     )(ha, hb, gain, cos, sin, wq, wk, wv)
 
@@ -181,153 +182,267 @@
     )(ga, gb, w_out, *before)
 
 
-def by_head(a_ref, b_ref, group):
-    def flat(r):
-        v = r[...]
-        return v.reshape(v.shape[0] * v.shape[2], v.shape[3])
-
-    full = jnp.concatenate([flat(a_ref), flat(b_ref)], axis=0)
-    return jnp.concatenate([full[:, h * HEAD_DIM:(h + 1) * HEAD_DIM] for h in range(group)], axis=0)
-
-
-def put(ref, value):
-    ref[...] = value.reshape(ref.shape)
+def tokens_of(refs, row, rows, batch):
+    parts = []
+    for ref in refs:
+        for block in range(ref.shape[0] // (batch * rows)):
+            parts.append(ref[pl.ds(pl.multiple_of((block * batch + row) * rows, rows), rows), :])
+    return jnp.concatenate(parts, axis=0)
+
+
+def put_tokens(ref, row, rows, batch, lanes, value):
+    for block in range(ref.shape[0] // (batch * rows)):
+        ref[pl.ds(pl.multiple_of((block * batch + row) * rows, rows), rows), lanes] = value[block * rows:(block + 1) * rows]
+
+
+def heads_down(x):
+    return jnp.concatenate([x[:, c:c + HEAD_DIM] for c in range(0, x.shape[1], HEAD_DIM)], axis=0)
+
+
+def heads_across(x, seq):
+    return jnp.concatenate([x[c:c + seq] for c in range(0, x.shape[0], seq)], axis=1)
 
 
 def soft_weights(k, q, down, across):
-    allowed = (down[0][:, 0:1] == across[0][0:1, :]) & (down[0][:, 1:2] <= across[0][1:2, :])
+    allowed = (down[:, 0:1] == across[0:1, :]) & (down[:, 1:2] <= across[1:2, :])
     scores = jnp.where(allowed, dot(k, q, NT), -1e30)
     e = jnp.exp2((scores - jnp.max(scores, axis=0, keepdims=True)) * (HEAD_DIM ** -0.5 * LOG2_E))
     return e, 1.0 / jnp.sum(e, axis=0, keepdims=True)
 
 
-def attend_kernel(group, qa, qb, ka, kb, va, vb, down, across, out):
-    q = by_head(qa, qb, group)
-    k = by_head(ka, kb, 1)
-    v = by_head(va, vb, 1)
+def attend_row(row, rows, batch, q_refs, k_refs, v_refs, down, across, out):
+    q, k, v = (tokens_of(r, row, rows, batch) for r in (q_refs, k_refs, v_refs))
+    wide = HEAD_DIM * (q.shape[1] // k.shape[1])
+    for i in range(k.shape[1] // HEAD_DIM):
+        at, kv = slice(i * wide, (i + 1) * wide), slice(i * HEAD_DIM, (i + 1) * HEAD_DIM)
+        e, scale = soft_weights(k[:, kv], heads_down(q[:, at]), down[row], across[row])
+        o = dot((e * scale).astype(BF16), v[:, kv], TN).astype(BF16)
+        put_tokens(out, row, rows, batch, at, heads_across(o, k.shape[0]))
+
+
+def attend_back_row(row, rows, batch, q_refs, k_refs, v_refs, g_refs, down, across, cos_refs, sin_refs, dq_out, dk_out, dv_out):
+    q, k, v, g = (tokens_of(r, row, rows, batch) for r in (q_refs, k_refs, v_refs, g_refs))
+    cos, sin = (tokens_of(r, row, rows, batch) * HEAD_DIM ** -0.5 for r in (cos_refs, sin_refs))
     seq = k.shape[0]
-    e, scale = soft_weights(k, q, down, across)
-    o = dot((e * scale).astype(BF16), v, TN).astype(BF16)
-    o = jnp.concatenate([o[h * seq:(h + 1) * seq] for h in range(group)], axis=1)
-    put(out, o)
-
-
-def head_specs(slots, rows, wide):
-    return pl.BlockSpec((slots, 1, rows, wide), lambda r, h: (0, r, 0, h))
-
-
-def mask_specs(seq, group):
-    return [pl.BlockSpec((1, seq, 2), lambda r, h: (r, 0, 0)), pl.BlockSpec((1, 2, group * seq), lambda r, h: (r, 0, 0))]
-
-
-def attend(qa, qb, ka, kb, va, vb, down, across):
-    slots, batch, rows, nq = qa.shape
-    kv = ka.shape[3] // HEAD_DIM
-    group = nq // ka.shape[3]
-    seq = 2 * slots * rows
-    qs, ks = head_specs(slots, rows, group * HEAD_DIM), head_specs(slots, rows, HEAD_DIM)
-    return pl.pallas_call(
-        functools.partial(attend_kernel, group), name="attend", grid=(batch, kv),
-        in_specs=[qs, qs, ks, ks, ks, ks] + mask_specs(seq, group),
-        out_specs=head_specs(2 * slots, rows, group * HEAD_DIM),
-        out_shape=jax.ShapeDtypeStruct((2 * slots,) + qa.shape[1:], BF16),
-        compiler_params=params(62, "arbitrary", "arbitrary"),
-        cost_estimate=cost(batch * kv * group * seq * seq * HEAD_DIM * 40, 4 * qa.size * 2),
-    )(qa, qb, ka, kb, va, vb, down, across)
-
-
-def attend_back_kernel(group, qa, qb, ka, kb, va, vb, ga, gb, down, across, ca, cb, sa, sb, dq_out, dk_out, dv_out):
-    q = by_head(qa, qb, group)
-    g = by_head(ga, gb, group)
-    k = by_head(ka, kb, 1)
-    v = by_head(va, vb, 1)
-    cos, sin = by_head(ca, cb, 1) * HEAD_DIM ** -0.5, by_head(sa, sb, 1) * HEAD_DIM ** -0.5
-    seq = k.shape[0]
-    e, scale = soft_weights(k, q, down, across)
-    probs = e * scale
-    gp = dot(v, g, NT)
-    dots = jnp.sum(probs * gp, axis=0, keepdims=True)
-    ds = (probs * (gp - dots)).astype(BF16)
-    dv = dot(probs.astype(BF16), g).astype(BF16)
-    dk = dot(ds, q)
-    dq = dot(ds, k, TN)
+    wide = HEAD_DIM * (q.shape[1] // k.shape[1])
 
     def unrotated(x):
         return (x * cos - swap_pairs(x) * sin).astype(BF16)
 
-    dq = jnp.concatenate([unrotated(dq[h * seq:(h + 1) * seq]) for h in range(group)], axis=1)
-    dk = unrotated(dk)
-    put(dq_out, dq)
-    put(dk_out, dk)
-    put(dv_out, dv)
-
-
-def attend_back(qa, qb, ka, kb, va, vb, ga, gb, down, across, ca, cb, sa, sb):
-    slots, batch, rows, nq = qa.shape
-    kv = ka.shape[3] // HEAD_DIM
-    group = nq // ka.shape[3]
-    seq = 2 * slots * rows
-    qs, ks = head_specs(slots, rows, group * HEAD_DIM), head_specs(slots, rows, HEAD_DIM)
-    ts = pl.BlockSpec((slots, 1, rows, HEAD_DIM), lambda r, h: (0, r, 0, 0))
+    for i in range(k.shape[1] // HEAD_DIM):
+        at, kv = slice(i * wide, (i + 1) * wide), slice(i * HEAD_DIM, (i + 1) * HEAD_DIM)
+        qh, gh = heads_down(q[:, at]), heads_down(g[:, at])
+        e, scale = soft_weights(k[:, kv], qh, down[row], across[row])
+        probs = e * scale
+        gp = dot(v[:, kv], gh, NT)
+        ds = (probs * (gp - jnp.sum(probs * gp, axis=0, keepdims=True))).astype(BF16)
+        put_tokens(dv_out, row, rows, batch, kv, dot(probs.astype(BF16), gh).astype(BF16))
+        put_tokens(dk_out, row, rows, batch, kv, unrotated(dot(ds, qh)))
+        dq = dot(ds, k[:, kv], TN)
+        dq = jnp.concatenate([unrotated(dq[c:c + seq]) for c in range(0, dq.shape[0], seq)], axis=1)
+        put_tokens(dq_out, row, rows, batch, at, dq)
+
+
+def chip_sum(first, steps, share, out, keep, box, got, send_sem, recv_sem):
+    now = pl.program_id(0)
+    step = now - first
+    tp = lax.axis_index("tp")
+    neighbour = {"tp": tp + 1 - 2 * lax.rem(tp, 2)}
+
+    def copy(i):
+        return pltpu.make_async_remote_copy(box.at[i % 2], got.at[i % 2], send_sem.at[i % 2], recv_sem.at[i % 2],
+                                            device_id=neighbour, device_id_type=pl.DeviceIdType.MESH)
+
+    @pl.when(now == 0)
+    def _():
+        barrier = pltpu.get_barrier_semaphore()
+        pl.semaphore_signal(barrier, inc=1, device_id=neighbour, device_id_type=pl.DeviceIdType.MESH)
+        pl.semaphore_wait(barrier, 1)
+
+    @pl.when(step > 0)
+    def _():
+        copy(step - 1).start()
+
+    @pl.when((step >= 0) & (step < steps))
+    def _():
+        counterpart, diagonal = share()
+        keep[step % 2] = counterpart
+        box[step % 2] = diagonal
+
+    @pl.when(step > 0)
+    def _():
+        copy(step - 1).wait()
+        out[...] = (keep[(step - 1) % 2] + got[(step - 1) % 2]).astype(BF16)
+
+
+def chip_sum_scratch(rows, blk):
+    return [pltpu.VMEM((2, rows, blk), F32)] * 3 + [pltpu.SemaphoreType.DMA((2,))] * 2
+
+
+def clip(i, n):
+    return jnp.clip(i, 0, n - 1)
+
+
+def comm_params(number):
+    return pltpu.CompilerParams(dimension_semantics=("arbitrary",), vmem_limit_bytes=62 << 20, collective_id=number, has_side_effects=True)
+
+
+def forward_kernel(batch, first, steps, ha, hb, gain, cos, sin, wq, wk, wv, qa, ka, va, down, across, w_out,
+                   n_out, inv_out, qb, kb, vb, o, p0, p1, s2, ns, ws, sem, wsem, wo, osem, *chip):
+    step = pl.program_id(0)
+    slots, _, blk = wo.shape
+    attend_at = first - batch
+
+    def load(i):
+        return pltpu.make_async_copy(w_out.at[:, pl.ds(pl.multiple_of(i * blk, blk), blk)], wo.at[i % slots], osem.at[i % slots])
+
+    @pl.when(step < attend_at)
+    def _():
+        project(step, ha, hb, gain, cos, sin, wq, wk, wv, n_out, inv_out, qb, kb, vb, ns, ws, sem, wsem)
+
+    @pl.when(step == attend_at - 1)
+    def _():
+        for i in range(slots):
+            load(i).start()
+
+    @pl.when((step >= attend_at) & (step < first))
+    def _():
+        rows = qa.shape[0] // (2 * batch)
+        attend_row(step - attend_at, rows, batch, (qa, qb), (ka, kb), (va, vb), down, across, o)
+
+    @pl.when((step > first) & (step - first + slots - 1 < steps))
+    def _():
+        load(step - first + slots - 1).start()
+
+    def share():
+        load(step - first).wait()
+        r = dot(o[...], wo[(step - first) % slots])
+        rows = p0.shape[0]
+        p0[...] = r[:rows].astype(BF16)
+        p1[...] = r[rows:2 * rows].astype(BF16)
+        return r[2 * rows:3 * rows], r[3 * rows:]
+
+    chip_sum(first, steps, share, s2, *chip)
+
+
+def forward(batch, ha, hb, gain, cos, sin, wq, wk, wv, qa, ka, va, down, across, w_out):
+    half, width = ha.shape
+    tok = 2 * half
+    nq, nk = wq.shape[1], wk.shape[1]
+    wide, blk = 2 * nk, 1024
+    first, steps = nq // wide + 1 + batch, width // blk
+    specs, shapes = project_out(tok, width, nq, nk)
+    now = pl.BlockSpec((half, blk), lambda i: (0, clip(i - first, steps)))
+    late = pl.BlockSpec((half, blk), lambda i: (0, clip(i - first - 1, steps)))
     return pl.pallas_call(
-        functools.partial(attend_back_kernel, group), name="attend_back", grid=(batch, kv),
-        in_specs=[qs, qs, ks, ks, ks, ks, qs, qs] + mask_specs(seq, group) + [ts, ts, ts, ts],
-        out_specs=[head_specs(2 * slots, rows, wide) for wide in (group * HEAD_DIM, HEAD_DIM, HEAD_DIM)],
-        out_shape=[jax.ShapeDtypeStruct((2 * slots,) + x.shape[1:], BF16) for x in (qa, ka, va)],
-        compiler_params=params(62, "arbitrary", "arbitrary"),
-        cost_estimate=cost(batch * kv * group * seq * seq * HEAD_DIM * 60, 8 * qa.size * 2),
-    )(qa, qb, ka, kb, va, vb, ga, gb, down, across, ca, cb, sa, sb)
-
-
-def out_share_kernel(o, w, *outs):
-    r = dot(o[...], w[...])
-    rows = outs[0].shape[0]
-    for i, out in enumerate(outs):
-        out[...] = r[i * rows:(i + 1) * rows].astype(out.dtype)
-
-
-def out_share(o, w_out, types):
-    tok, n = o.shape
-    width = w_out.shape[1]
-    blk = 1024
-    rows = tok // len(types)
+        functools.partial(forward_kernel, batch, first, steps), name="forward", grid=(first + steps + 1,),
+        in_specs=[ANY, ANY] + [const_spec(x.shape) for x in (gain, cos, sin)] + [ANY] * 3
+        + [const_spec(x.shape) for x in (qa, ka, va, down, across)] + [ANY],
+        out_specs=specs + [const_spec((2 * tok, nq)), now, now, late],
+        out_shape=shapes + [jax.ShapeDtypeStruct((2 * tok, nq), BF16)] + [jax.ShapeDtypeStruct((half, width), BF16)] * 3,
+        scratch_shapes=project_scratch(tok, width, wide) + [pltpu.VMEM((3, nq, blk), BF16), pltpu.SemaphoreType.DMA((3,))]
+        + chip_sum_scratch(half, blk),
+        compiler_params=comm_params(0), cost_estimate=cost(2 * tok * width * (3 * nq + 2 * nk), 4 * width * nq),
+    )(ha, hb, gain, cos, sin, wq, wk, wv, qa, ka, va, down, across, w_out)
+
+
+def backward_kernel(batch, heads_steps, steps, ga, gb, w_out, gh_a, qa, qb, ka, kb, va, vb, down, across, ca, cb, sa, sb,
+                    wq, wk, wv, h0, h1, h2, h3, inv_a, inv_b,
+                    dq, dk, dv, d0, d1, t2, gain, gs, gh_b, wo, ws, wks, wvs, sem, osem, wsem, *chip):
+    step = pl.program_id(0)
+    half = ga.shape[0]
+    slots, blk = wo.shape[:2]
+    w_slots, wide = ws.shape[:2]
+    first = heads_steps + batch
+
+    def load(i):
+        return pltpu.make_async_copy(w_out.at[pl.ds(pl.multiple_of(i * blk, blk), blk)], wo.at[i % slots], osem.at[i % slots])
+
+    def load_w(i):
+        at = pl.ds(pl.multiple_of(i * wide, wide), wide)
+        return [pltpu.make_async_copy(w.at[at], buf.at[i % w_slots], wsem.at[j, i % w_slots])
+                for j, (w, buf) in enumerate(((wq, ws), (wk, wks), (wv, wvs)))]
+
+    def start_w(i):
+        for c in load_w(i):
+            c.start()
+
+    @pl.when(step == 0)
+    def _():
+        loads = [pltpu.make_async_copy(ga, gs.at[pl.ds(0, half)], sem.at[0]),
+                 pltpu.make_async_copy(gb, gs.at[pl.ds(half, half)], sem.at[1])]
+        for c in loads:
+            c.start()
+        load(0).start()
+        for c in loads:
+            c.wait()
+        for i in range(1, slots):
+            load(i).start()
+
+    @pl.when((step > 0) & (step + slots - 1 < heads_steps))
+    def _():
+        load(step + slots - 1).start()
+
+    @pl.when(step < heads_steps)
+    def _():
+        load(step).wait()
+        gh_b[:, pl.ds(pl.multiple_of(step * blk, blk), blk)] = dot(gs[...], wo[step % slots], NT).astype(BF16)
+
+    @pl.when(step == heads_steps - 1)
+    def _():
+        for i in range(w_slots):
+            start_w(i)
+
+    @pl.when((step >= heads_steps) & (step < first))
+    def _():
+        rows = qa.shape[0] // (2 * batch)
+        attend_back_row(step - heads_steps, rows, batch, (qa, qb), (ka, kb), (va, vb), (gh_a, gh_b), down, across, (ca, cb), (sa, sb), dq, dk, dv)
+
+    @pl.when((step > first) & (step - first + w_slots - 1 < steps))
+    def _():
+        start_w(step - first + w_slots - 1)
+
+    def share():
+        i = step - first
+        for c in load_w(i):
+            c.wait()
+        i = i % w_slots
+        r = dot(dq[...], ws[i], NT) + dot(dk[...], wks[i], NT) + dot(dv[...], wvs[i], NT)
+        parts = [r[j * half:(j + 1) * half] for j in range(4)]
+        d0[...] = parts[0].astype(BF16)
+        d1[...] = parts[1].astype(BF16)
+        total = 0.0
+        for j, (part, h) in enumerate(zip(parts, (h0, h1, h2, h3))):
+            inv = (inv_a, inv_b)[j // 2][(j % 2) * half:(j % 2 + 1) * half, :1]
+            total = total + jnp.sum(part * (h[...].astype(F32) * inv), axis=0, keepdims=True)
+        gain[...] = total
+        return parts[2], parts[3]
+
+    chip_sum(first, steps, share, t2, *chip)
+
+
+def backward(batch, ga, gb, w_out, gh_a, qa, qb, ka, kb, va, vb, down, across, ca, cb, sa, sb, wq, wk, wv, h, inv_a, inv_b):
+    half, width = ga.shape
+    tok = 4 * half
+    nq, nk = wq.shape[1], wk.shape[1]
+    blk, wide = 256, 1024
+    heads_steps, steps = nq // blk, width // wide
+    first = heads_steps + batch
+    now = pl.BlockSpec((half, wide), lambda i: (0, clip(i - first, steps)))
+    late = pl.BlockSpec((half, wide), lambda i: (0, clip(i - first - 1, steps)))
+    kept = (gh_a, qa, qb, ka, kb, va, vb, down, across, ca, cb, sa, sb)
     return pl.pallas_call(
-        out_share_kernel, name="out_share", grid=(width // blk,),
-        in_specs=[const_spec((tok, n)), pl.BlockSpec((n, blk), lambda i: (0, i))],
-        out_specs=[pl.BlockSpec((rows, blk), lambda i: (0, i))] * len(types),
-        out_shape=[jax.ShapeDtypeStruct((rows, width), t) for t in types],
-        compiler_params=params(62), cost_estimate=cost(2 * tok * width * n, 2 * width * n),
-    )(o, w_out)
-
-
-def norm_share_kernel(dq, dk, dv, wq, wk, wv, h0, h1, h2, h3, inv_a, inv_b, d0, d1, d2, d3, gain):
-    r = dot(dq[...], wq[...], NT) + dot(dk[...], wk[...], NT) + dot(dv[...], wv[...], NT)
-    rows = d0.shape[0]
-    total = 0.0
-    for i, (h, d) in enumerate(((h0, d0), (h1, d1), (h2, d2), (h3, d3))):
-        part = r[i * rows:(i + 1) * rows]
-        d[...] = part.astype(d.dtype)
-        inv = (inv_a, inv_b)[i // 2][(i % 2) * rows:(i % 2 + 1) * rows, :1]
-        total = total + jnp.sum(part * (h[...].astype(F32) * inv), axis=0, keepdims=True)
-    gain[...] = total
-
-
-def norm_share(dq, dk, dv, wq, wk, wv, h, inv_a, inv_b):
-    tok, nq = dq.shape
-    nk = dk.shape[1]
-    width = wq.shape[0]
-    blk = 1024
-    spec = pl.BlockSpec((tok // 4, blk), lambda i: (0, i))
-    return pl.pallas_call(
-        norm_share_kernel, name="norm_share", grid=(width // blk,),
-        in_specs=[const_spec((tok, nq)), const_spec((tok, nk)), const_spec((tok, nk)),
-                  pl.BlockSpec((blk, nq), lambda i: (i, 0)), pl.BlockSpec((blk, nk), lambda i: (i, 0)),
-                  pl.BlockSpec((blk, nk), lambda i: (i, 0)), spec, spec, spec, spec,
-                  const_spec((tok // 2, 128)), const_spec((tok // 2, 128))],
-        out_specs=[spec] * 4 + [pl.BlockSpec((1, blk), lambda i: (0, i))],
-        out_shape=[jax.ShapeDtypeStruct((tok // 4, width), BF16)] * 4 + [jax.ShapeDtypeStruct((1, width), F32)],
-        compiler_params=params(62), cost_estimate=cost(2 * tok * width * (nq + 2 * nk), 2 * width * (nq + 2 * nk)),
-    )(dq, dk, dv, wq, wk, wv, *h, inv_a, inv_b)
+        functools.partial(backward_kernel, batch, heads_steps, steps), name="backward", grid=(first + steps + 1,),
+        in_specs=[ANY] * 3 + [const_spec(x.shape) for x in kept] + [ANY] * 3 + [now] * 4 + [const_spec(x.shape) for x in (inv_a, inv_b)],
+        out_specs=[const_spec((tok, n)) for n in (nq, nk, nk)] + [now, now, late, pl.BlockSpec((1, wide), lambda i: (0, clip(i - first, steps)))],
+        out_shape=[jax.ShapeDtypeStruct((tok, n), BF16) for n in (nq, nk, nk)] + [jax.ShapeDtypeStruct((half, width), BF16)] * 3
+        + [jax.ShapeDtypeStruct((1, width), F32)],
+        scratch_shapes=[pltpu.VMEM((2 * half, width), BF16), pltpu.VMEM((2 * half, nq), BF16), pltpu.VMEM((4, blk, width), BF16),
+                        pltpu.VMEM((3, wide, nq), BF16), pltpu.VMEM((3, wide, nk), BF16), pltpu.VMEM((3, wide, nk), BF16),
+                        pltpu.SemaphoreType.DMA((2,)), pltpu.SemaphoreType.DMA((4,)), pltpu.SemaphoreType.DMA((3, 3))]
+        + chip_sum_scratch(half, wide),
+        compiler_params=comm_params(1), cost_estimate=cost(2 * tok * width * (2 * nq + 2 * nk), 4 * width * nq),
+    )(ga, gb, w_out, *kept, wq, wk, wv, *h, inv_a, inv_b)
 
 
 def weight_grads_kernel(steps, na, nb, dq, dk, dv, o, g0, g1, g2, g3, p0, p1, p2, h, gq, gk, gv, g_out, out, ot):
@@ -444,40 +559,25 @@
             angles = jnp.stack(pos).astype(F32)[..., None] * inv_freq
             return jnp.cos(angles), jnp.sin(angles) * sign
 
-        def heads(x):
-            return x.reshape(2, batch, rows, x.shape[1])
-
-        def flat(x):
-            return x.reshape(x.shape[0] * tok, x.shape[3])
-
-        ca, sa = tables(positions, pos1)
-        na, inv_a, qa, ka, va = qkv(h0, h1, gain, ca.reshape(2 * tok, HEAD_DIM), sa.reshape(2 * tok, HEAD_DIM), w_query, w_key, w_value)
+        ca, sa = [x.reshape(2 * tok, HEAD_DIM) for x in tables(positions, pos1)]
+        na, inv_a, qa, ka, va = qkv(h0, h1, gain, ca, sa, w_query, w_key, w_value)
         pos2, doc2, ka = lax.optimization_barrier((pos2, doc2, ka))
         pos3, doc3 = send(pos2, beside), send(doc2, beside)
-        cb, sb = tables(pos2, pos3)
+        cb, sb = [x.reshape(2 * tok, HEAD_DIM) for x in tables(pos2, pos3)]
         both = jnp.stack([jnp.concatenate([doc_ids, doc1, doc2, doc3], axis=1), jnp.concatenate([positions, pos1, pos2, pos3], axis=1)], axis=1)
         down, over = jnp.swapaxes(both, 1, 2), jnp.tile(both, (1, 1, group))
         dha = heads_grad(g0, g1, w_out, ka, cb, sb, down, over)
-        nb, inv_b, qb, kb, vb = qkv(h2, h3, gain, cb.reshape(2 * tok, HEAD_DIM), sb.reshape(2 * tok, HEAD_DIM), w_query, w_key, w_value)
-        saved = [heads(x) for x in (qa, qb, ka, kb, va, vb)]
-        o = flat(attend(*saved, down, over))
-
-        p0, p1, p2, p3 = out_share(o, w_out, (BF16, BF16, F32, BF16))
-        g3 = send(after(g2, p2), beside)
-        p3 = send(p3, beside)
+        nb, inv_b, qb, kb, vb, o, p0, p1, s2 = forward(
+            batch, h2, h3, gain, cb, sb, w_query, w_key, w_value, qa, ka, va, down, over, w_out)
+        s2 = send(s2, across)
+        g3 = send(after(g2, p0), beside)
         p1 = send(p1, beside)
-        dhb = heads_grad(g2, g3, w_out)
-        s2 = (p2 + after(p3, dhb).astype(F32)).astype(BF16)
-        s2, dhb = lax.optimization_barrier((s2, dhb))
-        s2 = send(s2, across)
-        grads = attend_back(*saved, heads(dha), heads(dhb), down, over, ca, cb, sa, sb)
-        dq, dk, dv = [flat(x) for x in grads]
-        d0, d1, d2, d3, gg = norm_share(dq, dk, dv, w_query, w_key, w_value, (h0, h1, h2, h3), inv_a, inv_b)
-        d3 = send(d3, beside)
+        dq, dk, dv, d0, d1, t2, gg = backward(
+            batch, g2, g3, w_out, dha, qa, qb, ka, kb, va, vb, down, over, ca, cb, sa, sb,
+            w_query, w_key, w_value, (h0, h1, h2, h3), inv_a, inv_b)
+        t2, d1, gg, dq = lax.optimization_barrier((t2, d1, gg, dq))
+        t2 = send(t2, across)
         d1 = send(d1, beside)
-        t2 = (d2.astype(F32) + d3.astype(F32)).astype(BF16)
-        t2, gg, dq = lax.optimization_barrier((t2, gg, dq))
-        t2 = send(t2, across)
         gg1, gg2, gg3 = send(gg, beside), send(gg, across), send(gg, diagonal)
         gq, gk, gv, g_out, attn_out = weight_grads(na, nb, dq, dk, dv, o, (g0, g1, g2, g3), (p0, p1, s2), h0)
         grad_hidden = norm_back((after(d0, gk), d1, t2), h0, g0, inv_a, gain)

time: 374 us -> 313 us (0.84)
  waiting for transfers between devices: 102 us -> 51.5 us
  other arithmetic: 17.1 us -> 6.54 us
    ppermute x21 -> x19, waiting for transfers between devices: 102 us -> 51.5 us  [send(): return lax.ppermute(x, 'tp', pairs)]
    pallas_call x2 -> x1, Pallas kernels: 31.8 us -> 15.9 us  [heads_grad(): pl.pallas_call(functools.partial(heads_grad_kernel, steps), name='heads_g...]
    pallas_call x6 -> x3, Pallas kernels: 123 us -> 138 us  [the longest x1 61.8 us: backward(): pl.pallas_call(functools.partial(backward_kernel, batch, heads_steps, ste...]
    convert_element_type x2 -> x0, other arithmetic: 8.65 us -> none  [the longest x1 4.97 us: step(): s2 = (p2 + after(p3, dhb).astype(F32)).astype(BF16)]
    ppermute x21 -> x19, starting transfers between devices: 11.9 us -> 13.6 us  [send(): return lax.ppermute(x, 'tp', pairs)]
  transfers between devices with their start and end apart: 21 -> 19, of which waited for: 4 -> 2; matrix products, arithmetic and copies ran while one was open for 4% -> 3% of each run, Pallas kernels for 50% -> 74%
where the time goes in v3:
time: 313 us
  Pallas kernels  239 us (76%)
  waiting for transfers between devices  51.5 us (16%)
  starting transfers between devices  13.6 us (4%)
  other arithmetic  6.54 us (2%)
    pallas_call x1, Pallas kernels, weight_grads(): pl.pallas_call(functools.partial(weight_grads_kernel, steps), name='weigh...  76.8 us
    pallas_call x1, Pallas kernels, backward(): pl.pallas_call(functools.partial(backward_kernel, batch, heads_steps, ste...  61.8 us
    pallas_call x1, Pallas kernels, forward(): pl.pallas_call(functools.partial(forward_kernel, batch, first, steps), na...  54 us
    ppermute x19, waiting for transfers between devices, send(): return lax.ppermute(x, 'tp', pairs)  51.5 us
    pallas_call x1, Pallas kernels, qkv(): pl.pallas_call(lambda *refs: project(pl.program_id(0), *refs), name='qkv'...  22.5 us
    pallas_call x1, Pallas kernels, heads_grad(): pl.pallas_call(functools.partial(heads_grad_kernel, steps), name='heads_g...  15.9 us
    ppermute x19, starting transfers between devices, send(): return lax.ppermute(x, 'tp', pairs)  13.6 us
    pallas_call x1, Pallas kernels, norm_back(): pl.pallas_call(norm_back_kernel, name='norm_back', grid=(tok // blk,), in...  8.14 us
  transfers between devices with their start and end apart: 19, of which 2 were waited for; matrix products, arithmetic and copies ran while one was open for 3% of the time, Pallas kernels for 74%

profile of v3, /device:TPU:0, one launch (start us, length us, event | category | flops | bytes accessed | tf_op | source)
XLA Modules:
  0.0 312.9 jit_solution(5042146508500971870)
XLA Ops:
  0.6 3.3 %collective-permute-start.2 = (bf16[144,8192]{1,0:T(8,128)(2,1)}, bf16[144,8192]{1,0:T(8,128)(2,1)}, u32[]{:S(2)}, u32[]{:S(2)}) collective-permute-start(bf16[144,8192]{1,0:T(8,128)(2,1)} %bitcast.22), channel_id=1, source_target_pairs={{0,2},{1,3},{2,0},{3,1},{4,6},{5,7},{6,4},{7,5}} | collective-permute-start | bytes 7077896 | tf_op jit(solution)/shard_map/ppermute | solution.py:532
  4.0 0.5 collective-permute-start.1
  4.5 0.0 collective-permute-start.4
  4.5 2.0 collective-permute-start.5
  6.5 49.1 %collective-permute-done.2.ha.h2 = bf16[144,8192]{1,0:T(8,128)(2,1)} collective-permute-done((bf16[144,8192]{1,0:T(8,128)(2,1)}, bf16[144,8192]{1,0:T(8,128)(2,1)}, u32[]{:S(2)}, u32[]{:S(2)}) %collective-permute-start.2) | collective-permute-done | bytes 2359328 | tf_op jit(solution)/shard_map/ppermute | solution.py:532
  55.6 1.3 reshape.116
  56.9 0.7 add_convert_fusion
  57.6 0.1 convert_element_type.31
  57.7 1.3 fusion
  59.0 0.0 collective-permute-done.refs_1_.h1
  59.0 22.5 %qkv.1 = (bf16[288,8192]{1,0:T(8,128)(2,1)}, f32[288,128]{1,0:T(8,128)}, bf16[288,2048]{1,0:T(8,128)(2,1)}, bf16[288,256]{1,0:T(8,128)(2,1)}, bf16[288,256]{1,0:T(8,128)(2,1)}) custom-call(bf16[144,8192]{1,0:T(8,128)(2,1)} %bitcast.24, bf16[144,8192]{1,0:T(8,128)(2,1)} %collective-permute-done.refs_1_.h1, f32[1,8192]{1,0:T(1,128)} %bitcast.34, ...), custom_call_target="tpu_custom_call" | custom-call | flops 12079595520 | bytes 41943040 | tf_op jit(solution)/shard_map/qkv/pallas_call | solution.py:132
  81.5 0.0 collective-permute-done.4
  81.5 0.5 collective-permute-start.6
  82.1 0.0 collective-permute-start.7
  82.1 0.5 collective-permute-start.11
  82.6 1.7 collective-permute-start.9
  84.3 0.1 add_bitcast_fusion.1
  84.4 0.1 convert_element_type.34
  84.5 0.2 copy.24
  84.7 0.0 collective-permute-done.7
  84.7 2.4 collective-permute-done.8
  87.1 0.1 add_bitcast_fusion
  87.1 0.2 copy.23
  87.3 0.1 pad_add_fusion
  87.5 0.1 copy.25
  87.6 0.7 tile.10.across.refs_4_
  88.4 0.9 fusion.7.down.refs_3_
  89.2 1.4 fusion.1
  90.6 54.0 %forward.1 = (bf16[288,8192]{1,0:T(8,128)(2,1)}, f32[288,128]{1,0:T(8,128)}, bf16[288,2048]{1,0:T(8,128)(2,1)}, bf16[288,256]{1,0:T(8,128)(2,1)}, bf16[288,256]{...) custom-call(bf16[144,8192]{1,0:T(8,128)(2,1)} %collective-permute-do, ...), custom_call_target="tpu_custom_call" | custom-call | flops 31406948352 | bytes 67108864 | tf_op jit(solution)/shard_map/forward/pallas_call | solution.py:337
  144.6 0.4 collective-permute-start.10
  145.0 0.0 collective-permute-done.11.gb.g1
  145.0 15.9 %heads_grad.1.gh_a = bf16[288,2048]{1,0:T(8,128)(2,1)} custom-call(bf16[144,8192]{1,0:T(8,128)(2,1)} %bitcast.30, bf16[144,8192]{1,0:T(8,128)(2,1)} %collective-permute-done.11.gb.g1, bf16[2048,8192]{1,0:T(8,128)(2,1)} %w_out.3, bf16[288,256]{1,0:T(8,128)(2,1)} %get-tuple-element.46.ka.refs_0_, f32[288,128]{1,0:T(8,128)} %get-tuple-element.78.cos.refs_1_.cb, ...), custom_call_target="tpu_custom_call" | custom-call | flops 9663676416 | bytes 33554432 | tf_op jit(solution)/shard_map/heads_grad/pallas_call | solution.py:175
  160.9 0.2 collective-permute-start.12
  161.0 1.7 collective-permute-start.13
  162.8 61.8 %backward.1 = (bf16[576,2048]{1,0:T(8,128)(2,1)}, bf16[576,256]{1,0:T(8,128)(2,1)}, bf16[576,256]{1,0:T(8,128)(2,1)}, bf16[144,8192]{1,0:T(8,128)(2,1)}, bf16[14...) custom-call(bf16[144,8192]{1,0:T(8,128)(2,1)} %collective-permute-done.9.ga.g2, ...), custom_call_target="tpu_custom_call" | custom-call | flops 43486543872 | bytes 67108864 | tf_op jit(solution)/shard_map/backward/pallas_call | solution.py:434
  224.6 0.1 collective-permute-start.18
  224.7 1.7 collective-permute-start.17
  226.5 0.1 collective-permute-start.16
  226.5 0.0 collective-permute-done.12.p1
  226.5 0.5 collective-permute-start.14
  227.0 0.3 collective-permute-start.15
  227.3 76.8 %weight_grads.1 = (f32[8192,2048]{1,0:T(8,128)}, f32[8192,256]{1,0:T(8,128)}, f32[8192,256]{1,0:T(8,128)}, f32[2048,8192]{1,0:T(8,128)}, bf16[144,8192]{1,0:T(8,128)(2,1)}) custom-call(bf16[288,8192]{1,0:T(8,128)(2,1)} %get-tuple-element.42.na, bf16[288,8192]{1,0:T(8,128)(2,1)} %get-tuple-element.49.nb, bf16[576,2048]{1,0:T(8,128)(2,1)} %get-tuple-element.61.dq, ...), custom_call_target="tpu_custom_call" | custom-call | flops 43486543872 | bytes 150994944 | tf_op jit(solution)/shard_map/weight_grads/pallas_call | solution.py:483
  304.1 0.0 collective-permute-done.17
  304.1 0.0 collective-permute-done.16
  304.1 0.7 add_add_fusion
  304.8 0.0 collective-permute-done.14.d1
  304.8 0.0 collective-permute-done.15.d2
  304.8 8.1 %norm_back.1 = bf16[144,8192]{1,0:T(8,128)(2,1)} custom-call(bf16[144,8192]{1,0:T(8,128)(2,1)} %get-tuple-element.70.d0, bf16[144,8192]{1,0:T(8,128)(2,1)} %collective-permute-done.14.d1, bf16[144,8192]{1,0:T(8,128)(2,1)} %collective-permute-done.15.d2, bf16[144,8192]{1,0:T(8,128)(2,1)} %bitcast.27, bf16[144,8192]{1,0:T(8,128)(2,1)} %bitcast.32, ...), custom_call_target="tpu_custom_call" | custom-call | flops 23592960 | bytes 14155776 | tf_op jit(solution)/shard_map/norm_back/pallas_call | solution.py:517
  (20 shorter events, 0.1 us)
Async XLA Ops:
  0.6 54.9 %collective-permute-start.2 = (bf16[144,8192]{1,0:T(8,128)(2,1)}, bf16[144,8192]{1,0:T(8,128)(2,1)}, u32[]{:S(2)}, u32[]{:S(2)}) collective-permute-start(bf16[144,8192]{1,0:T(8,128)(2,1)} %bitcast.22), channel_id=1, source_target_pairs={{0,2},{1,3},{2,0},{3,1},{4,6},{5,7},{6,4},{7,5}} | collective-permute-start | bytes 7077896 | tf_op jit(solution)/shard_map/ppermute | solution.py:532
  4.0 55.0 %collective-permute-start = (bf16[144,8192]{1,0:T(8,128)(2,1)}, bf16[144,8192]{1,0:T(8,128)(2,1)}, u32[]{:S(2)}, u32[]{:S(2)}) collective-permute-start(bf16[144,8192]{1,0:T(8,128)(2,1)} %bitcast.23), channel_id=1, source_target_pairs={{0,1},{1,0},{2,3},{3,2},{4,5},{5,4},{6,7},{7,6}} | collective-permute-start | bytes 7077896 | tf_op jit(solution)/shard_map/ppermute | solution.py:532
  4.0 53.0 %collective-permute-start.1 = (s32[3,48]{1,0:T(4,128)}, s32[3,48]{1,0:T(4,128)S(1)}, u32[]{:S(2)}, u32[]{:S(2)}) collective-permute-start(s32[3,48]{1,0:T(4,128)} %param.10), channel_id=1, source_target_pairs={{0,1},{1,0},{2,3},{3,2},{4,5},{5,4},{6,7},{7,6}} | collective-permute-start | bytes 1736 | tf_op jit(solution)/shard_map/ppermute | solution.py:532
  4.5 77.0 %collective-permute-start.4 = (s32[3,48]{1,0:T(4,128)}, s32[3,48]{1,0:T(4,128)S(1)}, u32[]{:S(2)}, u32[]{:S(2)}) collective-permute-start(s32[3,48]{1,0:T(4,128)} %param.10), channel_id=1, source_target_pairs={{0,2},{1,3},{2,0},{3,1},{4,6},{5,7},{6,4},{7,5}} | collective-permute-start | bytes 1736 | tf_op jit(solution)/shard_map/ppermute | solution.py:532
  4.5 77.0 %collective-permute-start.5 = (s32[3,48]{1,0:T(4,128)}, s32[3,48]{1,0:T(4,128)S(1)}, u32[]{:S(2)}, u32[]{:S(2)}) collective-permute-start(s32[3,48]{1,0:T(4,128)} %param.11), channel_id=1, source_target_pairs={{0,2},{1,3},{2,0},{3,1},{4,6},{5,7},{6,4},{7,5}} | collective-permute-start | bytes 1736 | tf_op jit(solution)/shard_map/ppermute | solution.py:532
  55.6 35.0 %collective-permute-start.3 = (bf16[144,8192]{1,0:T(8,128)(2,1)}, bf16[144,8192]{1,0:T(8,128)(2,1)}, u32[]{:S(2)}, u32[]{:S(2)}) collective-permute-start(bf16[144,8192]{1,0:T(8,128)(2,1)} %collective-permute-done.2.ha.h2), channel_id=1, source_target_pairs={{0,1},{1,0},{2,3},{3,2},{4,5},{5,4},{6,7},{7,6}} | collective-permute-start | bytes 7077896 | tf_op jit(solution)/shard_map/ppermute | solution.py:532
  59.0 23.0 %copy-start.2 = (s32[3,48]{1,0:T(4,128)S(1)}, s32[3,48]{1,0:T(4,128)}, u32[]{:S(2)}) copy-start(s32[3,48]{1,0:T(4,128)} %param.11) | copy-start | bytes 1732
  59.0 25.3 %copy-start.1 = (s32[3,48]{1,0:T(4,128)S(1)}, s32[3,48]{1,0:T(4,128)}, u32[]{:S(2)}) copy-start(s32[3,48]{1,0:T(4,128)} %param.10) | copy-start | bytes 1732
  81.5 2.8 collective-permute-start.6
  82.1 2.6 collective-permute-start.7
  82.1 62.9 %collective-permute-start.11 = (bf16[144,8192]{1,0:T(8,128)(2,1)}, bf16[144,8192]{1,0:T(8,128)(2,1)}, u32[]{:S(2)}, u32[]{:S(2)}) collective-permute-start(bf16[144,8192]{1,0:T(8,128)(2,1)} %bitcast.28), channel_id=1, source_target_pairs={{0,1},{1,0},{2,3},{3,2},{4,5},{5,4},{6,7},{7,6}} | collective-permute-start | bytes 7077896 | tf_op jit(solution)/shard_map/ppermute | solution.py:532
  82.6 62.1 %collective-permute-start.9 = (bf16[144,8192]{1,0:T(8,128)(2,1)}, bf16[144,8192]{1,0:T(8,128)(2,1)}, u32[]{:S(2)}, u32[]{:S(2)}) collective-permute-start(bf16[144,8192]{1,0:T(8,128)(2,1)} %bitcast.29), channel_id=1, source_target_pairs={{0,2},{1,3},{2,0},{3,1},{4,6},{5,7},{6,4},{7,5}} | collective-permute-start | bytes 7077896 | tf_op jit(solution)/shard_map/ppermute | solution.py:532
  84.3 2.8 collective-permute-start.8
  144.6 18.2 %collective-permute-start.10 = (bf16[144,8192]{1,0:T(8,128)(2,1)}, bf16[144,8192]{1,0:T(8,128)(2,1)}, u32[]{:S(2)}, u32[]{:S(2)}) collective-permute-start(bf16[144,8192]{1,0:T(8,128)(2,1)} %collective-permute-done.9.ga.g2), channel_id=1, source_target_pairs={{0,1},{1,0},{2,3},{3,2},{4,5},{5,4},{6,7},{7,6}} | collective-permute-start | bytes 7077896 | tf_op jit(solution)/shard_map/ppermute | solution.py:532
  160.9 65.6 %collective-permute-start.12 = (bf16[144,8192]{1,0:T(8,128)(2,1)}, bf16[144,8192]{1,0:T(8,128)(2,1)}, u32[]{:S(2)}, u32[]{:S(2)}) collective-permute-start(bf16[144,8192]{1,0:T(8,128)(2,1)} %get-tuple-element.65), channel_id=1, source_target_pairs={{0,1},{1,0},{2,3},{3,2},{4,5},{5,4},{6,7},{7,6}} | collective-permute-start | bytes 7077896 | tf_op jit(solution)/shard_map/ppermute | solution.py:532
  161.0 65.9 %collective-permute-start.13 = (bf16[144,8192]{1,0:T(8,128)(2,1)}, bf16[144,8192]{1,0:T(8,128)(2,1)}, u32[]{:S(2)}, u32[]{:S(2)}) collective-permute-start(bf16[144,8192]{1,0:T(8,128)(2,1)} %get-tuple-element.66), channel_id=1, source_target_pairs={{0,2},{1,3},{2,0},{3,1},{4,6},{5,7},{6,4},{7,5}} | collective-permute-start | bytes 7077896 | tf_op jit(solution)/shard_map/ppermute | solution.py:532
  224.6 79.4 %collective-permute-start.18 = (f32[1,8192]{1,0:T(1,128)}, f32[1,8192]{1,0:T(1,128)S(1)}, u32[]{:S(2)}, u32[]{:S(2)}) collective-permute-start(f32[1,8192]{1,0:T(1,128)} %get-tuple-element.73), channel_id=1, source_target_pairs={{0,3},{1,2},{2,1},{3,0},{4,7},{5,6},{6,5},{7,4}} | collective-permute-start | bytes 98312 | tf_op jit(solution)/shard_map/ppermute | solution.py:532
  224.7 79.4 %collective-permute-start.17 = (f32[1,8192]{1,0:T(1,128)}, f32[1,8192]{1,0:T(1,128)S(1)}, u32[]{:S(2)}, u32[]{:S(2)}) collective-permute-start(f32[1,8192]{1,0:T(1,128)} %get-tuple-element.73), channel_id=1, source_target_pairs={{0,2},{1,3},{2,0},{3,1},{4,6},{5,7},{6,4},{7,5}} | collective-permute-start | bytes 98312 | tf_op jit(solution)/shard_map/ppermute | solution.py:532
  226.5 77.6 %collective-permute-start.16 = (f32[1,8192]{1,0:T(1,128)}, f32[1,8192]{1,0:T(1,128)S(1)}, u32[]{:S(2)}, u32[]{:S(2)}) collective-permute-start(f32[1,8192]{1,0:T(1,128)} %get-tuple-element.73), channel_id=1, source_target_pairs={{0,1},{1,0},{2,3},{3,2},{4,5},{5,4},{6,7},{7,6}} | collective-permute-start | bytes 98312 | tf_op jit(solution)/shard_map/ppermute | solution.py:532
  226.5 78.3 %collective-permute-start.14 = (bf16[144,8192]{1,0:T(8,128)(2,1)}, bf16[144,8192]{1,0:T(8,128)(2,1)}, u32[]{:S(2)}, u32[]{:S(2)}) collective-permute-start(bf16[144,8192]{1,0:T(8,128)(2,1)} %get-tuple-element.71), channel_id=1, source_target_pairs={{0,1},{1,0},{2,3},{3,2},{4,5},{5,4},{6,7},{7,6}} | collective-permute-start | bytes 7077896 | tf_op jit(solution)/shard_map/ppermute | solution.py:532
  227.0 77.8 %collective-permute-start.15 = (bf16[144,8192]{1,0:T(8,128)(2,1)}, bf16[144,8192]{1,0:T(8,128)(2,1)}, u32[]{:S(2)}, u32[]{:S(2)}) collective-permute-start(bf16[144,8192]{1,0:T(8,128)(2,1)} %get-tuple-element.72), channel_id=1, source_target_pairs={{0,2},{1,3},{2,0},{3,1},{4,6},{5,7},{6,4},{7,5}} | collective-permute-start | bytes 7077896 | tf_op jit(solution)/shard_map/ppermute | solution.py:532
  227.3 76.8 %copy-start = (f32[1,8192]{1,0:T(1,128)S(1)}, f32[1,8192]{1,0:T(1,128)}, u32[]{:S(2)}) copy-start(f32[1,8192]{1,0:T(1,128)} %get-tuple-element.73) | copy-start | bytes 98308

commit v4 on v3

--- a/solution.py
+++ b/solution.py
@@ -41,8 +41,8 @@
     return jnp.where(lane % 2 == 0, pltpu.roll(x, x.shape[-1] - 1, x.ndim - 1), pltpu.roll(x, 1, x.ndim - 1))
 
 
-def project(step, ha, hb, gain, cos, sin, wq, wk, wv, n_out, inv_out, q_out, k_out, v_out, ns, ws, sem, wsem):
-    half, width = ha.shape
+def project(step, fetch, gain, cos, sin, wq, wk, wv, n_out, inv_out, q_out, k_out, v_out, ns, ws, sem, wsem):
+    tok, width = ns.shape
     nk = wk.shape[1]
     slots, _, blk = ws.shape
     q_steps = wq.shape[1] // blk
@@ -54,12 +54,9 @@
 
     @pl.when(step == 0)
     def _():
-        loads = [pltpu.make_async_copy(ha, ns.at[pl.ds(0, half)], sem.at[0]),
-                 pltpu.make_async_copy(hb, ns.at[pl.ds(half, half)], sem.at[1])]
-        for c in loads:
+        for c in fetch:
             c.start()
-        for c in loads:
-            c.wait()
+        fetch[0].wait()
         load_q(0).start()
         wide = 512
 
@@ -76,9 +73,10 @@
             inv_out[at, :] = jnp.broadcast_to(inv, (48, 128))
             return 0
 
-        chunks = 2 * half // 48
+        chunks = tok // 48
         lax.fori_loop(0, chunks // 2, rows, 0)
         load_q(1).start()
+        fetch[1].wait()
         lax.fori_loop(chunks // 2, chunks, rows, 0)
         load_q(2).start()
 
@@ -121,6 +119,13 @@
 
 def project_scratch(tok, width, blk):
     return [pltpu.VMEM((tok, width), BF16), pltpu.VMEM((3, width, blk), BF16), pltpu.SemaphoreType.DMA((5,)), pltpu.SemaphoreType.DMA((3,))]
+
+
+def qkv_kernel(ha, hb, *refs):
+    ns, sem = refs[-4], refs[-2]
+    half = ha.shape[0]
+    fetch = copies_of((ha, hb), (ns.at[pl.ds(0, half)], ns.at[pl.ds(half, half)]), sem)
+    project(pl.program_id(0), fetch, *refs)
 
 
 def qkv(ha, hb, gain, cos, sin, wq, wk, wv):
@@ -130,7 +135,7 @@
     blk = 2 * nk
     specs, shapes = project_out(tok, width, nq, nk)
     return pl.pallas_call(
-        lambda *refs: project(pl.program_id(0), *refs), name="qkv", grid=(nq // blk + 1,),
+        qkv_kernel, name="qkv", grid=(nq // blk + 1,),
         in_specs=[ANY, ANY, const_spec((1, width)), const_spec((tok, HEAD_DIM)), const_spec((tok, HEAD_DIM)), ANY, ANY, ANY],
         out_specs=specs, out_shape=shapes, scratch_shapes=project_scratch(tok, width, blk),
         compiler_params=params(62), cost_estimate=cost(2 * tok * width * (nq + 2 * nk), 2 * width * (nq + 2 * nk)),
@@ -243,22 +248,27 @@
         put_tokens(dq_out, row, rows, batch, at, dq)
 
 
+def other_core():
+    tp = lax.axis_index("tp")
+    return {"tp": tp + 1 - 2 * lax.rem(tp, 2)}
+
+
+def greet():
+    @pl.when(pl.program_id(0) == 0)
+    def _():
+        barrier = pltpu.get_barrier_semaphore()
+        pl.semaphore_signal(barrier, inc=1, device_id=other_core(), device_id_type=pl.DeviceIdType.MESH)
+        pl.semaphore_wait(barrier, 1)
+
+
 def chip_sum(first, steps, share, out, keep, box, got, send_sem, recv_sem):
-    now = pl.program_id(0)
-    step = now - first
-    tp = lax.axis_index("tp")
-    neighbour = {"tp": tp + 1 - 2 * lax.rem(tp, 2)}
+    step = pl.program_id(0) - first
+    neighbour = other_core()
 
     def copy(i):
         return pltpu.make_async_remote_copy(box.at[i % 2], got.at[i % 2], send_sem.at[i % 2], recv_sem.at[i % 2],
                                             device_id=neighbour, device_id_type=pl.DeviceIdType.MESH)
 
-    @pl.when(now == 0)
-    def _():
-        barrier = pltpu.get_barrier_semaphore()
-        pl.semaphore_signal(barrier, inc=1, device_id=neighbour, device_id_type=pl.DeviceIdType.MESH)
-        pl.semaphore_wait(barrier, 1)
-
     @pl.when(step > 0)
     def _():
         copy(step - 1).start()
@@ -279,6 +289,24 @@
     return [pltpu.VMEM((2, rows, blk), F32)] * 3 + [pltpu.SemaphoreType.DMA((2,))] * 2
 
 
+def start_all(copies):
+    for c in copies:
+        c.start()
+
+
+def wait_all(copies):
+    for c in copies:
+        c.wait()
+
+
+def copies_of(sources, targets, sem):
+    return [pltpu.make_async_copy(a, b, sem.at[i]) for i, (a, b) in enumerate(zip(sources, targets))]
+
+
+def like(*arrays):
+    return [pltpu.VMEM(x.shape, x.dtype) for x in arrays]
+
+
 def clip(i, n):
     return jnp.clip(i, 0, n - 1)
 
@@ -287,23 +315,46 @@
     return pltpu.CompilerParams(dimension_semantics=("arbitrary",), vmem_limit_bytes=62 << 20, collective_id=number, has_side_effects=True)
 
 
-def forward_kernel(batch, first, steps, ha, hb, gain, cos, sin, wq, wk, wv, qa, ka, va, down, across, w_out,
-                   n_out, inv_out, qb, kb, vb, o, p0, p1, s2, ns, ws, sem, wsem, wo, osem, *chip):
+def forward_kernel(batch, first, steps, h2, gain, cos, sin, wq, wk, wv, qa_in, ka_in, va_in, down, across, w_out,
+                   n_out, inv_out, qb_out, kb_out, vb_out, o_out, h3, p0, p1, s2,
+                   ns, ws, sem, wsem, wo, osem, qa, ka, va, qb, kb, vb, o, isem, esem, xsem, *chip):
     step = pl.program_id(0)
     slots, _, blk = wo.shape
     attend_at = first - batch
+    loads = copies_of((qa_in, ka_in, va_in), (qa, ka, va), isem)
+    saves = copies_of((qb, kb, vb, o), (qb_out, kb_out, vb_out, o_out), esem)
+
+    half = h2.shape[0]
+    fetch = [pltpu.make_async_copy(h2, ns.at[pl.ds(0, half)], sem.at[0])] + [
+        pltpu.make_async_remote_copy(h2, to, xsem.at[0, i], xsem.at[1, i], device_id=other_core(), device_id_type=pl.DeviceIdType.MESH)
+        for i, to in enumerate((ns.at[pl.ds(half, half)], h3))]
+    greet()
+
+    @pl.when(step == 1)
+    def _():
+        start_all(loads)
+        fetch[2].start()
 
     def load(i):
         return pltpu.make_async_copy(w_out.at[:, pl.ds(pl.multiple_of(i * blk, blk), blk)], wo.at[i % slots], osem.at[i % slots])
 
     @pl.when(step < attend_at)
     def _():
-        project(step, ha, hb, gain, cos, sin, wq, wk, wv, n_out, inv_out, qb, kb, vb, ns, ws, sem, wsem)
+        project(step, fetch[:2], gain, cos, sin, wq, wk, wv, n_out, inv_out, qb, kb, vb, ns, ws, sem, wsem)
 
     @pl.when(step == attend_at - 1)
     def _():
         for i in range(slots):
             load(i).start()
+
+    @pl.when(step == attend_at)
+    def _():
+        wait_all(loads)
+        start_all(saves[:3])
+
+    @pl.when(step == first)
+    def _():
+        saves[3].start()
 
     @pl.when((step >= attend_at) & (step < first))
     def _():
@@ -324,9 +375,14 @@
 
     chip_sum(first, steps, share, s2, *chip)
 
-
-def forward(batch, ha, hb, gain, cos, sin, wq, wk, wv, qa, ka, va, down, across, w_out):
-    half, width = ha.shape
+    @pl.when(step == first + steps)
+    def _():
+        wait_all(saves)
+        fetch[2].wait()
+
+
+def forward(batch, h2, gain, cos, sin, wq, wk, wv, qa, ka, va, down, across, w_out):
+    half, width = h2.shape
     tok = 2 * half
     nq, nk = wq.shape[1], wk.shape[1]
     wide, blk = 2 * nk, 1024
@@ -336,20 +392,29 @@
     late = pl.BlockSpec((half, blk), lambda i: (0, clip(i - first - 1, steps)))
     return pl.pallas_call(
         functools.partial(forward_kernel, batch, first, steps), name="forward", grid=(first + steps + 1,),
-        in_specs=[ANY, ANY] + [const_spec(x.shape) for x in (gain, cos, sin)] + [ANY] * 3
-        + [const_spec(x.shape) for x in (qa, ka, va, down, across)] + [ANY],
-        out_specs=specs + [const_spec((2 * tok, nq)), now, now, late],
-        out_shape=shapes + [jax.ShapeDtypeStruct((2 * tok, nq), BF16)] + [jax.ShapeDtypeStruct((half, width), BF16)] * 3,
+        in_specs=[ANY] + [const_spec(x.shape) for x in (gain, cos, sin)] + [ANY] * 3
+        + [ANY] * 3 + [const_spec(x.shape) for x in (down, across)] + [ANY],
+        out_specs=specs[:2] + [ANY] * 5 + [now, now, late],
+        out_shape=shapes + [jax.ShapeDtypeStruct((2 * tok, nq), BF16)] + [jax.ShapeDtypeStruct((half, width), BF16)] * 4,
         scratch_shapes=project_scratch(tok, width, wide) + [pltpu.VMEM((3, nq, blk), BF16), pltpu.SemaphoreType.DMA((3,))]
+        + like(qa, ka, va, qa, ka, va) + [pltpu.VMEM((2 * tok, nq), BF16), pltpu.SemaphoreType.DMA((3,)), pltpu.SemaphoreType.DMA((4,)), pltpu.SemaphoreType.DMA((2, 2))]
         + chip_sum_scratch(half, blk),
         compiler_params=comm_params(0), cost_estimate=cost(2 * tok * width * (3 * nq + 2 * nk), 4 * width * nq),
-    )(ha, hb, gain, cos, sin, wq, wk, wv, qa, ka, va, down, across, w_out)
-
-
-def backward_kernel(batch, heads_steps, steps, ga, gb, w_out, gh_a, qa, qb, ka, kb, va, vb, down, across, ca, cb, sa, sb,
-                    wq, wk, wv, h0, h1, h2, h3, inv_a, inv_b,
-                    dq, dk, dv, d0, d1, t2, gain, gs, gh_b, wo, ws, wks, wvs, sem, osem, wsem, *chip):
+    )(h2, gain, cos, sin, wq, wk, wv, qa, ka, va, down, across, w_out)
+
+
+def backward_kernel(batch, heads_steps, steps, ga, gb, w_out, down, across, wq, wk, wv, h0, h1, h2, h3, inv_a, inv_b, *refs):
+    kept_in, (dq_out, dk_out, dv_out, d0, d1, t2, gain), kept = refs[:11], refs[11:18], refs[18:29]
+    gh_a, qa, qb, ka, kb, va, vb, ca, cb, sa, sb = kept
+    grads, gs, gh_b, wo, ws, sem, osem, wsem, isem, esem = refs[29:39]
+    chip = refs[39:]
     step = pl.program_id(0)
+    loads = copies_of(kept_in, kept, isem)
+    nq, nk = wq.shape[1], wk.shape[1]
+    lanes = [pl.ds(0, nq), pl.ds(nq, nk), pl.ds(nq + nk, nk)]
+    dq, dk, dv = [grads.at[:, at] for at in lanes]
+    saves = copies_of((dq, dk, dv), (dq_out, dk_out, dv_out), esem)
+    greet()
     half = ga.shape[0]
     slots, blk = wo.shape[:2]
     w_slots, wide = ws.shape[:2]
@@ -360,8 +425,7 @@
 
     def load_w(i):
         at = pl.ds(pl.multiple_of(i * wide, wide), wide)
-        return [pltpu.make_async_copy(w.at[at], buf.at[i % w_slots], wsem.at[j, i % w_slots])
-                for j, (w, buf) in enumerate(((wq, ws), (wk, wks), (wv, wvs)))]
+        return [pltpu.make_async_copy(w.at[at], ws.at[i % w_slots, :, lanes[j]], wsem.at[j, i % w_slots]) for j, w in enumerate((wq, wk, wv))]
 
     def start_w(i):
         for c in load_w(i):
@@ -369,15 +433,24 @@
 
     @pl.when(step == 0)
     def _():
-        loads = [pltpu.make_async_copy(ga, gs.at[pl.ds(0, half)], sem.at[0]),
-                 pltpu.make_async_copy(gb, gs.at[pl.ds(half, half)], sem.at[1])]
-        for c in loads:
-            c.start()
+        fetch = copies_of((ga, gb), (gs.at[pl.ds(0, half)], gs.at[pl.ds(half, half)]), sem)
+        start_all(fetch)
         load(0).start()
-        for c in loads:
-            c.wait()
+        wait_all(fetch)
         for i in range(1, slots):
             load(i).start()
+
+    @pl.when(step == heads_steps // 2)
+    def _():
+        start_all(loads)
+
+    @pl.when(step == heads_steps)
+    def _():
+        wait_all(loads)
+
+    @pl.when(step == first)
+    def _():
+        start_all(saves)
 
     @pl.when((step > 0) & (step + slots - 1 < heads_steps))
     def _():
@@ -406,8 +479,7 @@
         i = step - first
         for c in load_w(i):
             c.wait()
-        i = i % w_slots
-        r = dot(dq[...], ws[i], NT) + dot(dk[...], wks[i], NT) + dot(dv[...], wvs[i], NT)
+        r = dot(grads[...], ws[i % w_slots], NT)
         parts = [r[j * half:(j + 1) * half] for j in range(4)]
         d0[...] = parts[0].astype(BF16)
         d1[...] = parts[1].astype(BF16)
@@ -420,6 +492,10 @@
 
     chip_sum(first, steps, share, t2, *chip)
 
+    @pl.when(step == first + steps)
+    def _():
+        wait_all(saves)
+
 
 def backward(batch, ga, gb, w_out, gh_a, qa, qb, ka, kb, va, vb, down, across, ca, cb, sa, sb, wq, wk, wv, h, inv_a, inv_b):
     half, width = ga.shape
@@ -430,23 +506,31 @@
     first = heads_steps + batch
     now = pl.BlockSpec((half, wide), lambda i: (0, clip(i - first, steps)))
     late = pl.BlockSpec((half, wide), lambda i: (0, clip(i - first - 1, steps)))
-    kept = (gh_a, qa, qb, ka, kb, va, vb, down, across, ca, cb, sa, sb)
+    kept = (gh_a, qa, qb, ka, kb, va, vb, ca, cb, sa, sb)
     return pl.pallas_call(
         functools.partial(backward_kernel, batch, heads_steps, steps), name="backward", grid=(first + steps + 1,),
-        in_specs=[ANY] * 3 + [const_spec(x.shape) for x in kept] + [ANY] * 3 + [now] * 4 + [const_spec(x.shape) for x in (inv_a, inv_b)],
-        out_specs=[const_spec((tok, n)) for n in (nq, nk, nk)] + [now, now, late, pl.BlockSpec((1, wide), lambda i: (0, clip(i - first, steps)))],
+        in_specs=[ANY] * 3 + [const_spec(x.shape) for x in (down, across)] + [ANY] * 3 + [now] * 4
+        + [const_spec(x.shape) for x in (inv_a, inv_b)] + [ANY] * len(kept),
+        out_specs=[ANY] * 3 + [now, now, late, pl.BlockSpec((1, wide), lambda i: (0, clip(i - first, steps)))],
         out_shape=[jax.ShapeDtypeStruct((tok, n), BF16) for n in (nq, nk, nk)] + [jax.ShapeDtypeStruct((half, width), BF16)] * 3
         + [jax.ShapeDtypeStruct((1, width), F32)],
-        scratch_shapes=[pltpu.VMEM((2 * half, width), BF16), pltpu.VMEM((2 * half, nq), BF16), pltpu.VMEM((4, blk, width), BF16),
-                        pltpu.VMEM((3, wide, nq), BF16), pltpu.VMEM((3, wide, nk), BF16), pltpu.VMEM((3, wide, nk), BF16),
-                        pltpu.SemaphoreType.DMA((2,)), pltpu.SemaphoreType.DMA((4,)), pltpu.SemaphoreType.DMA((3, 3))]
+        scratch_shapes=like(*kept) + [pltpu.VMEM((tok, nq + 2 * nk), BF16)]
+        + [pltpu.VMEM((2 * half, width), BF16), pltpu.VMEM((2 * half, nq), BF16), pltpu.VMEM((4, blk, width), BF16),
+           pltpu.VMEM((3, wide, nq + 2 * nk), BF16),
+           pltpu.SemaphoreType.DMA((2,)), pltpu.SemaphoreType.DMA((4,)), pltpu.SemaphoreType.DMA((3, 3)),
+           pltpu.SemaphoreType.DMA((len(kept),)), pltpu.SemaphoreType.DMA((3,))]
         + chip_sum_scratch(half, wide),
         compiler_params=comm_params(1), cost_estimate=cost(2 * tok * width * (2 * nq + 2 * nk), 4 * width * nq),
-    )(ga, gb, w_out, *kept, wq, wk, wv, *h, inv_a, inv_b)
-
-
-def weight_grads_kernel(steps, na, nb, dq, dk, dv, o, g0, g1, g2, g3, p0, p1, p2, h, gq, gk, gv, g_out, out, ot):
+    )(ga, gb, w_out, down, across, wq, wk, wv, *h, inv_a, inv_b, *kept)
+
+
+def weight_grads_kernel(steps, na, nb, dq, dk, dv, o_in, g0, g1, g2, g3, p0, p1, p2, h, gq, gk, gv, g_out, out, o, ot, sem):
     step = pl.program_id(0)
+    load = pltpu.make_async_copy(o_in, o, sem)
+
+    @pl.when(step == 1)
+    def _():
+        load.start()
 
     @pl.when(step < steps)
     def _():
@@ -456,6 +540,7 @@
 
     @pl.when(step == steps)
     def _():
+        load.wait()
         for c in range(0, o.shape[1], 256):
             ot[c:c + 256, :] = o[:, c:c + 256].T
 
@@ -483,43 +568,72 @@
     return pl.pallas_call(
         functools.partial(weight_grads_kernel, steps), name="weight_grads", grid=(2 * steps,),
         in_specs=[pl.BlockSpec((tok // 2, blk), lambda i: (0, early(i)))] * 2 + [const_spec((tok, nq))] + [const_spec((tok, nk))] * 2
-        + [const_spec((tok, nq))] + [rows] * 8,
+        + [ANY] + [rows] * 8,
         out_specs=[pl.BlockSpec((blk, n), lambda i: (early(i), 0)) for n in (nq, nk, nk)] + [pl.BlockSpec((nq, blk), lambda i: (0, late(i))), rows],
         out_shape=[jax.ShapeDtypeStruct((width, n), F32) for n in (nq, nk, nk)]
         + [jax.ShapeDtypeStruct((nq, width), F32), jax.ShapeDtypeStruct(h.shape, BF16)],
-        scratch_shapes=[pltpu.VMEM((nq, tok), BF16)],
+        scratch_shapes=[pltpu.VMEM((tok, nq), BF16), pltpu.VMEM((nq, tok), BF16), pltpu.SemaphoreType.DMA],
         compiler_params=params(62), cost_estimate=cost(4 * tok * width * (nq + nk), 8 * width * (nq + nk)),
     )(na, nb, dq, dk, dv, o, *g, *p, h)
 
 
-def norm_back_kernel(d0, d1, d2, h, g, inv, gain, grad, dg):
-    rows, width = h.shape
+def norm_back_kernel(d0, d1, d2, h, g, inv, gain, gg0, gg1, gg2, gg3, grad, grad_gain, *refs):
+    held, (out, dg, isem, esem) = refs[:5], refs[5:]
+    rows, width = dg.shape
+    count = out.shape[0] // rows
     wide = 1024
-    total = jnp.zeros((rows, wide), F32)
-    for c in range(0, width, wide):
-        at = slice(c, c + wide)
-        x = sum(d[:, at].astype(F32) for d in (d0, d1, d2)) * gain[:, at]
-        dg[:, at] = x
-        total = total + x * h[:, at].astype(F32)
-    s = inv[:, :1]
-    back = (s * s * s) * (jnp.sum(total, axis=-1, keepdims=True) / width)
-    s = jnp.broadcast_to(s, (rows, wide))
-    back = jnp.broadcast_to(back, (rows, wide))
-    for c in range(0, width, wide):
-        at = slice(c, c + wide)
-        grad[:, at] = (g[:, at].astype(F32) + (s * dg[:, at] - h[:, at].astype(F32) * back)).astype(BF16)
-
-
-def norm_back(d, h, g, inv, gain):
+
+    def at(i):
+        return pl.ds(pl.multiple_of(i * rows, rows), rows)
+
+    def loads(i):
+        return [pltpu.make_async_copy(a.at[at(i)], b.at[at(i)], isem.at[j, i]) for j, (a, b) in enumerate(zip((d0, d1, d2, h, g), held))]
+
+    def save(i):
+        return pltpu.make_async_copy(out.at[at(i)], grad.at[at(i)], esem.at[i])
+
+    @pl.loop(0, count)
+    def _(i):
+        start_all(loads(i))
+
+    grad_gain[...] = (gg0[...] + gg1[...]) + (gg2[...] + gg3[...])
+    x0, x1, x2, hs, gs = held
+
+    @pl.loop(0, count)
+    def _(i):
+        wait_all(loads(i))
+        total = jnp.zeros((rows, wide), F32)
+        for c in range(0, width, wide):
+            cut = slice(c, c + wide)
+            x = sum(d[at(i), cut].astype(F32) for d in (x0, x1, x2)) * gain[:, cut]
+            dg[:, cut] = x
+            total = total + x * hs[at(i), cut].astype(F32)
+        s = inv[at(i), :1]
+        back = (s * s * s) * (jnp.sum(total, axis=-1, keepdims=True) / width)
+        s = jnp.broadcast_to(s, (rows, wide))
+        back = jnp.broadcast_to(back, (rows, wide))
+        for c in range(0, width, wide):
+            cut = slice(c, c + wide)
+            out[at(i), cut] = (gs[at(i), cut].astype(F32) + (s * dg[:, cut] - hs[at(i), cut].astype(F32) * back)).astype(BF16)
+        save(i).start()
+
+    @pl.loop(0, count)
+    def _(i):
+        save(i).wait()
+
+
+def norm_back(d, h, g, inv, gain, gain_shares):
     tok, width = h.shape
-    blk = 48
-    spec = pl.BlockSpec((blk, width), lambda i: (i, 0))
+    rows = 16
+    count = tok // rows
+    whole = pl.BlockSpec(memory_space=pltpu.VMEM)
     return pl.pallas_call(
-        norm_back_kernel, name="norm_back", grid=(tok // blk,),
-        in_specs=[spec] * 5 + [pl.BlockSpec((blk, 128), lambda i: (i, 0)), const_spec((1, width))],
-        out_specs=spec, out_shape=jax.ShapeDtypeStruct((tok, width), BF16), scratch_shapes=[pltpu.VMEM((blk, width), F32)],
-        compiler_params=params(62), cost_estimate=cost(20 * tok * width, 12 * tok * width),
-    )(*d, h, g, inv, gain)
+        norm_back_kernel, name="norm_back", in_specs=[ANY] * 5 + [whole] * 6, out_specs=[ANY, whole],
+        out_shape=[jax.ShapeDtypeStruct((tok, width), BF16), jax.ShapeDtypeStruct((1, width), F32)],
+        scratch_shapes=[pltpu.VMEM((tok, width), BF16)] * 6
+        + [pltpu.VMEM((rows, width), F32), pltpu.SemaphoreType.DMA((5, count)), pltpu.SemaphoreType.DMA((count,))],
+        compiler_params=pltpu.CompilerParams(vmem_limit_bytes=62 << 20), cost_estimate=cost(20 * tok * width, 12 * tok * width),
+    )(*d, h, g, inv, gain, *gain_shares)
 
 
 def solution(mesh):
@@ -549,7 +663,6 @@
         h1 = send(h0, beside)
         g1 = send(g0, beside)
         g2 = send(g0, across)
-        h3 = send(h2, beside)
 
         lane = jnp.arange(HEAD_DIM)
         inv_freq = ROPE_BASE ** (-(lane // 2 * 2).astype(F32) / HEAD_DIM)
@@ -567,8 +680,8 @@
         both = jnp.stack([jnp.concatenate([doc_ids, doc1, doc2, doc3], axis=1), jnp.concatenate([positions, pos1, pos2, pos3], axis=1)], axis=1)
         down, over = jnp.swapaxes(both, 1, 2), jnp.tile(both, (1, 1, group))
         dha = heads_grad(g0, g1, w_out, ka, cb, sb, down, over)
-        nb, inv_b, qb, kb, vb, o, p0, p1, s2 = forward(
-            batch, h2, h3, gain, cb, sb, w_query, w_key, w_value, qa, ka, va, down, over, w_out)
+        nb, inv_b, qb, kb, vb, o, h3, p0, p1, s2 = forward(
+            batch, h2, gain, cb, sb, w_query, w_key, w_value, qa, ka, va, down, over, w_out)
         s2 = send(s2, across)
         g3 = send(after(g2, p0), beside)
         p1 = send(p1, beside)
@@ -580,8 +693,8 @@
         d1 = send(d1, beside)
         gg1, gg2, gg3 = send(gg, beside), send(gg, across), send(gg, diagonal)
         gq, gk, gv, g_out, attn_out = weight_grads(na, nb, dq, dk, dv, o, (g0, g1, g2, g3), (p0, p1, s2), h0)
-        grad_hidden = norm_back((after(d0, gk), d1, t2), h0, g0, inv_a, gain)
-        grad_gain = ((gg + gg1) + (gg2 + gg3)).reshape(width)
+        grad_hidden, gg = norm_back((after(d0, gk), d1, t2), h0, g0, inv_a[:tok], gain, (gg, gg1, gg2, gg3))
+        grad_gain = gg.reshape(width)
         attn_out, grad_hidden = attn_out.reshape(hidden.shape), grad_hidden.reshape(hidden.shape)
         return (attn_out, grad_hidden, grad_gain, gq, gk, gv, g_out)
 

time: 313 us -> 285 us (0.911)
  waiting for transfers between devices: 51.5 us -> 30 us
  Pallas kernels: 239 us -> 233 us
    ppermute x19 -> x18, waiting for transfers between devices: 51.5 us -> 30 us  [send(): return lax.ppermute(x, 'tp', pairs)]
    ppermute x19 -> x18, starting transfers between devices: 13.6 us -> 11.7 us  [send(): return lax.ppermute(x, 'tp', pairs)]
  transfers between devices with their start and end apart: 19 -> 18, of which waited for: 2 -> 3; matrix products, arithmetic and copies ran while one was open for 3% -> 3% of each run, Pallas kernels for 74% -> 79%
where the time goes in v4:
time: 285 us
  Pallas kernels  233 us (82%)
  waiting for transfers between devices  30 us (11%)
  starting transfers between devices  11.7 us (4%)
  other arithmetic  5.83 us (2%)
    pallas_call x1, Pallas kernels, weight_grads(): pl.pallas_call(functools.partial(weight_grads_kernel, steps), name='weigh...  76.2 us
    pallas_call x1, Pallas kernels, backward(): pl.pallas_call(functools.partial(backward_kernel, batch, heads_steps, ste...  59 us
    pallas_call x1, Pallas kernels, forward(): pl.pallas_call(functools.partial(forward_kernel, batch, first, steps), na...  52.3 us
    ppermute x18, waiting for transfers between devices, send(): return lax.ppermute(x, 'tp', pairs)  30 us
    pallas_call x1, Pallas kernels, qkv(): pl.pallas_call(qkv_kernel, name='qkv', grid=(nq // blk + 1,), in_specs=[A...  21.9 us
    pallas_call x1, Pallas kernels, heads_grad(): pl.pallas_call(functools.partial(heads_grad_kernel, steps), name='heads_g...  15.9 us
    ppermute x18, starting transfers between devices, send(): return lax.ppermute(x, 'tp', pairs)  11.7 us
    pallas_call x1, Pallas kernels, norm_back(): pl.pallas_call(norm_back_kernel, name='norm_back', in_specs=[ANY] * 5 + [...  7.97 us
  transfers between devices with their start and end apart: 18, of which 3 were waited for; matrix products, arithmetic and copies ran while one was open for 3% of the time, Pallas kernels for 79%

profile of v4, /device:TPU:0, one launch (start us, length us, event | category | flops | bytes accessed | tf_op | source)
XLA Modules:
  0.0 284.5 jit_solution(14614707258683876875)
XLA Ops:
  0.6 0.9 collective-permute-start
  1.5 0.0 collective-permute-start.1
  1.5 2.9 %collective-permute-start.3 = (s32[3,48]{1,0:T(4,128)}, s32[3,48]{1,0:T(4,128)S(1)}, u32[]{:S(2)}, u32[]{:S(2)}) collective-permute-start(s32[3,48]{1,0:T(4,128)} %param.10), channel_id=1, source_target_pairs={{0,2},{1,3},{2,0},{3,1},{4,6},{5,7},{6,4},{7,5}} | collective-permute-start | bytes 1736 | tf_op jit(solution)/shard_map/ppermute | solution.py:646
  4.5 0.0 collective-permute-start.2
  4.5 2.0 collective-permute-start.4
  6.5 1.3 reshape.116
  7.8 0.0 collective-permute-done.1
  7.8 0.7 add_convert_fusion
  8.5 0.1 convert_element_type.31
  8.6 1.3 fusion
  9.9 0.0 collective-permute-done.hb.h1
  9.9 21.9 %qkv.1 = (bf16[288,8192]{1,0:T(8,128)(2,1)}, f32[288,128]{1,0:T(8,128)}, bf16[288,2048]{1,0:T(8,128)(2,1)}, bf16[288,256]{1,0:T(8,128)(2,1)}, bf16[288,256]{1,0:T(8,128)(2,1)}) custom-call(bf16[144,8192]{1,0:T(8,128)(2,1)} %bitcast.24, bf16[144,8192]{1,0:T(8,128)(2,1)} %collective-permute-done.hb.h1, f32[1,8192]{1,0:T(1,128)} %bitcast.33, ...), custom_call_target="tpu_custom_call" | custom-call | flops 12079595520 | bytes 41943040 | tf_op jit(solution)/shard_map/qkv/pallas_call | solution.py:137
  31.9 25.8 %collective-permute-done.4 = s32[3,48]{1,0:T(4,128)S(1)} collective-permute-done((s32[3,48]{1,0:T(4,128)}, s32[3,48]{1,0:T(4,128)S(1)}, u32[]{:S(2)}, u32[]{:S(2)}) %collective-permute-start.4) | collective-permute-done | bytes 608 | tf_op jit(solution)/shard_map/ppermute | solution.py:646
  57.7 0.5 collective-permute-start.6
  58.2 0.0 collective-permute-start.10
  58.2 0.3 collective-permute-start.8
  58.6 0.3 collective-permute-done.5
  58.9 0.2 collective-permute-start.7
  59.1 0.1 add_bitcast_fusion.1
  59.1 0.2 copy.24
  59.3 3.8 %collective-permute-done.7 = s32[3,48]{1,0:T(4,128)S(1)} collective-permute-done((s32[3,48]{1,0:T(4,128)S(1)}, s32[3,48]{1,0:T(4,128)S(1)}, u32[]{:S(2)}, u32[]{:S(2)}) %collective-permute-start.7) | collective-permute-done | bytes 608 | tf_op jit(solution)/shard_map/ppermute | solution.py:646
  63.1 0.1 add_bitcast_fusion
  63.2 0.2 copy.23
  63.4 0.1 pad_add_fusion
  63.5 0.1 copy.25
  63.7 0.7 tile.10.across.refs_4_
  64.4 0.1 convert_element_type.34
  64.5 0.9 fusion.7.down.refs_3_
  65.4 1.3 fusion.1
  66.7 52.3 %forward.1 = (bf16[288,8192]{1,0:T(8,128)(2,1)}, f32[288,128]{1,0:T(8,128)}, bf16[288,2048]{1,0:T(8,128)(2,1)}, bf16[288,256]{1,0:T(8,128)(2,1)}, bf16[288,256]{...) custom-call(bf16[144,8192]{1,0:T(8,128)(2,1)} %collective-permute-do, ...), custom_call_target="tpu_custom_call" | custom-call | flops 31406948352 | bytes 67108864 | tf_op jit(solution)/shard_map/forward/pallas_call | solution.py:393
  119.0 0.0 collective-permute-done.8.ga.g2
  119.0 0.4 collective-permute-start.9
  119.4 0.6 slice.3.inv
  120.1 0.1 collective-permute-start.11
  120.2 0.3 collective-permute-start.12
  120.5 15.9 %heads_grad.1.refs_0_ = bf16[288,2048]{1,0:T(8,128)(2,1)} custom-call(bf16[144,8192]{1,0:T(8,128)(2,1)} %bitcast.30, bf16[144,8192]{1,0:T(8,128)(2,1)} %collective-permute-done.10.gb.g1, bf16[2048,8192]{1,0:T(8,128)(2,1)} %w_out.3, bf16[288,256]{1,0:T(8,128)(2,1)} %get-tuple-element.49.ka_in.refs_0_.refs_3_, ...), custom_call_target="tpu_custom_call" | custom-call | flops 9663676416 | bytes 33554432 | tf_op jit(solution)/shard_map/heads_grad/pallas_call | solution.py:180
  136.4 0.0 collective-permute-done.9.gb.g3
  136.4 59.0 %backward.1 = (bf16[576,2048]{1,0:T(8,128)(2,1)}, bf16[576,256]{1,0:T(8,128)(2,1)}, bf16[576,256]{1,0:T(8,128)(2,1)}, bf16[144,8192]{1,0:T(8,128)(2,1)}, bf16[14...) custom-call(bf16[144,8192]{1,0:T(8,128)(2,1)} %collective-permute-done.8.ga.g2, ...), custom_call_target="tpu_custom_call" | custom-call | flops 43486543872 | bytes 67108864 | tf_op jit(solution)/shard_map/backward/pallas_call | solution.py:510
  195.4 0.2 collective-permute-start.15
  195.6 1.7 collective-permute-start.16
  197.3 0.0 collective-permute-start.17
  197.3 0.4 collective-permute-start.13
  197.7 1.7 collective-permute-start.14
  199.4 76.2 %weight_grads.1 = (f32[8192,2048]{1,0:T(8,128)}, f32[8192,256]{1,0:T(8,128)}, f32[8192,256]{1,0:T(8,128)}, f32[2048,8192]{1,0:T(8,128)}, bf16[144,8192]{1,0:T(8,128)(2,1)}) custom-call(bf16[288,8192]{1,0:T(8,128)(2,1)} %get-tuple-element.45.na, bf16[288,8192]{1,0:T(8,128)(2,1)} %get-tuple-element.52.nb, bf16[576,2048]{1,0:T(8,128)(2,1)} %get-tuple-element.65.dq, ...), custom_call_target="tpu_custom_call" | custom-call | flops 43486543872 | bytes 150994944 | tf_op jit(solution)/shard_map/weight_grads/pallas_call | solution.py:568
  275.8 0.5 copy-done.1
  276.3 0.0 copy-done.2
  276.3 0.0 copy-done.3
  276.3 8.0 %norm_back.1 = (bf16[144,8192]{1,0:T(8,128)(2,1)}, f32[1,8192]{1,0:T(1,128)}) custom-call(bf16[144,8192]{1,0:T(8,128)(2,1)} %get-tuple-element.74.d0, bf16[144,8192]{1,0:T(8,128)(2,1)} %collective-permute-done.13.d1, bf16[144,8192]{1,0:T(8,128)(2,1)} %collective-permute-done.14.d2, bf16[144,8192]{1,0:T(8,128)(2,1)} %bitcast.27, bf16[144,8192]{1,0:T(8,128)(2,1)} %bitcast.32, ...), custom_call_target="tpu_custom_call" | custom-call | flops 23592960 | bytes 14155776 | tf_op jit(solution)/shard_map/norm_back/pallas_call | solution.py:630
  (24 shorter events, 0.1 us)
Async XLA Ops:
  0.6 9.3 %collective-permute-start = (bf16[144,8192]{1,0:T(8,128)(2,1)}, bf16[144,8192]{1,0:T(8,128)(2,1)}, u32[]{:S(2)}, u32[]{:S(2)}) collective-permute-start(bf16[144,8192]{1,0:T(8,128)(2,1)} %bitcast.22), channel_id=1, source_target_pairs={{0,1},{1,0},{2,3},{3,2},{4,5},{5,4},{6,7},{7,6}} | collective-permute-start | bytes 7077896 | tf_op jit(solution)/shard_map/ppermute | solution.py:646
  1.5 6.4 %collective-permute-start.1 = (s32[3,48]{1,0:T(4,128)}, s32[3,48]{1,0:T(4,128)S(1)}, u32[]{:S(2)}, u32[]{:S(2)}) collective-permute-start(s32[3,48]{1,0:T(4,128)} %param.10), channel_id=1, source_target_pairs={{0,1},{1,0},{2,3},{3,2},{4,5},{5,4},{6,7},{7,6}} | collective-permute-start | bytes 1736 | tf_op jit(solution)/shard_map/ppermute | solution.py:646
  1.5 30.4 %collective-permute-start.3 = (s32[3,48]{1,0:T(4,128)}, s32[3,48]{1,0:T(4,128)S(1)}, u32[]{:S(2)}, u32[]{:S(2)}) collective-permute-start(s32[3,48]{1,0:T(4,128)} %param.10), channel_id=1, source_target_pairs={{0,2},{1,3},{2,0},{3,1},{4,6},{5,7},{6,4},{7,5}} | collective-permute-start | bytes 1736 | tf_op jit(solution)/shard_map/ppermute | solution.py:646
  4.5 62.2 %collective-permute-start.2 = (bf16[144,8192]{1,0:T(8,128)(2,1)}, bf16[144,8192]{1,0:T(8,128)(2,1)}, u32[]{:S(2)}, u32[]{:S(2)}) collective-permute-start(bf16[144,8192]{1,0:T(8,128)(2,1)} %bitcast.23), channel_id=1, source_target_pairs={{0,2},{1,3},{2,0},{3,1},{4,6},{5,7},{6,4},{7,5}} | collective-permute-start | bytes 7077896 | tf_op jit(solution)/shard_map/ppermute | solution.py:646
  4.5 53.2 %collective-permute-start.4 = (s32[3,48]{1,0:T(4,128)}, s32[3,48]{1,0:T(4,128)S(1)}, u32[]{:S(2)}, u32[]{:S(2)}) collective-permute-start(s32[3,48]{1,0:T(4,128)} %param.11), channel_id=1, source_target_pairs={{0,2},{1,3},{2,0},{3,1},{4,6},{5,7},{6,4},{7,5}} | collective-permute-start | bytes 1736 | tf_op jit(solution)/shard_map/ppermute | solution.py:646
  9.9 47.8 %copy-start.5 = (s32[3,48]{1,0:T(4,128)S(1)}, s32[3,48]{1,0:T(4,128)}, u32[]{:S(2)}) copy-start(s32[3,48]{1,0:T(4,128)} %param.11) | copy-start | bytes 1732
  9.9 49.1 %copy-start.4 = (s32[3,48]{1,0:T(4,128)S(1)}, s32[3,48]{1,0:T(4,128)}, u32[]{:S(2)}) copy-start(s32[3,48]{1,0:T(4,128)} %param.10) | copy-start | bytes 1732
  57.7 1.2 collective-permute-start.5
  57.7 1.6 collective-permute-start.6
  58.2 62.3 %collective-permute-start.10 = (bf16[144,8192]{1,0:T(8,128)(2,1)}, bf16[144,8192]{1,0:T(8,128)(2,1)}, u32[]{:S(2)}, u32[]{:S(2)}) collective-permute-start(bf16[144,8192]{1,0:T(8,128)(2,1)} %bitcast.28), channel_id=1, source_target_pairs={{0,1},{1,0},{2,3},{3,2},{4,5},{5,4},{6,7},{7,6}} | collective-permute-start | bytes 7077896 | tf_op jit(solution)/shard_map/ppermute | solution.py:646
  58.2 60.8 %collective-permute-start.8 = (bf16[144,8192]{1,0:T(8,128)(2,1)}, bf16[144,8192]{1,0:T(8,128)(2,1)}, u32[]{:S(2)}, u32[]{:S(2)}) collective-permute-start(bf16[144,8192]{1,0:T(8,128)(2,1)} %bitcast.29), channel_id=1, source_target_pairs={{0,2},{1,3},{2,0},{3,1},{4,6},{5,7},{6,4},{7,5}} | collective-permute-start | bytes 7077896 | tf_op jit(solution)/shard_map/ppermute | solution.py:646
  58.9 4.2 %collective-permute-start.7 = (s32[3,48]{1,0:T(4,128)S(1)}, s32[3,48]{1,0:T(4,128)S(1)}, u32[]{:S(2)}, u32[]{:S(2)}) collective-permute-start(s32[3,48]{1,0:T(4,128)S(1)} %collective-permute-done.4), channel_id=1, source_target_pairs={{0,1},{1,0},{2,3},{3,2},{4,5},{5,4},{6,7},{7,6}} | collective-permute-start | bytes 1736 | tf_op jit(solution)/shard_map/ppermute | solution.py:646
  66.7 52.7 %copy-start = (f32[288,128]{1,0:T(8,128)S(1)}, f32[288,128]{1,0:T(8,128)}, u32[]{:S(2)}) copy-start(f32[288,128]{1,0:T(8,128)} %get-tuple-element.56.inv_a) | copy-start | bytes 442372
  119.0 17.3 %collective-permute-start.9 = (bf16[144,8192]{1,0:T(8,128)(2,1)}, bf16[144,8192]{1,0:T(8,128)(2,1)}, u32[]{:S(2)}, u32[]{:S(2)}) collective-permute-start(bf16[144,8192]{1,0:T(8,128)(2,1)} %collective-permute-done.8.ga.g2), channel_id=1, source_target_pairs={{0,1},{1,0},{2,3},{3,2},{4,5},{5,4},{6,7},{7,6}} | collective-permute-start | bytes 7077896 | tf_op jit(solution)/shard_map/ppermute | solution.py:646
  120.1 77.3 %collective-permute-start.11 = (bf16[144,8192]{1,0:T(8,128)(2,1)}, bf16[144,8192]{1,0:T(8,128)(2,1)}, u32[]{:S(2)}, u32[]{:S(2)}) collective-permute-start(bf16[144,8192]{1,0:T(8,128)(2,1)} %get-tuple-element.69), channel_id=1, source_target_pairs={{0,1},{1,0},{2,3},{3,2},{4,5},{5,4},{6,7},{7,6}} | collective-permute-start | bytes 7077896 | tf_op jit(solution)/shard_map/ppermute | solution.py:646
  120.2 77.5 %collective-permute-start.12 = (bf16[144,8192]{1,0:T(8,128)(2,1)}, bf16[144,8192]{1,0:T(8,128)(2,1)}, u32[]{:S(2)}, u32[]{:S(2)}) collective-permute-start(bf16[144,8192]{1,0:T(8,128)(2,1)} %get-tuple-element.70), channel_id=1, source_target_pairs={{0,2},{1,3},{2,0},{3,1},{4,6},{5,7},{6,4},{7,5}} | collective-permute-start | bytes 7077896 | tf_op jit(solution)/shard_map/ppermute | solution.py:646
  195.4 80.3 %collective-permute-start.15 = (f32[1,8192]{1,0:T(1,128)}, f32[1,8192]{1,0:T(1,128)S(1)}, u32[]{:S(2)}, u32[]{:S(2)}) collective-permute-start(f32[1,8192]{1,0:T(1,128)} %get-tuple-element.77.gg0), channel_id=1, source_target_pairs={{0,1},{1,0},{2,3},{3,2},{4,5},{5,4},{6,7},{7,6}} | collective-permute-start | bytes 98312 | tf_op jit(solution)/shard_map/ppermute | solution.py:646
  195.6 80.1 %collective-permute-start.16 = (f32[1,8192]{1,0:T(1,128)}, f32[1,8192]{1,0:T(1,128)S(1)}, u32[]{:S(2)}, u32[]{:S(2)}) collective-permute-start(f32[1,8192]{1,0:T(1,128)} %get-tuple-element.77.gg0), channel_id=1, source_target_pairs={{0,2},{1,3},{2,0},{3,1},{4,6},{5,7},{6,4},{7,5}} | collective-permute-start | bytes 98312 | tf_op jit(solution)/shard_map/ppermute | solution.py:646
  197.3 78.4 %collective-permute-start.17 = (f32[1,8192]{1,0:T(1,128)}, f32[1,8192]{1,0:T(1,128)S(1)}, u32[]{:S(2)}, u32[]{:S(2)}) collective-permute-start(f32[1,8192]{1,0:T(1,128)} %get-tuple-element.77.gg0), channel_id=1, source_target_pairs={{0,3},{1,2},{2,1},{3,0},{4,7},{5,6},{6,5},{7,4}} | collective-permute-start | bytes 98312 | tf_op jit(solution)/shard_map/ppermute | solution.py:646
  197.3 78.4 %collective-permute-start.13 = (bf16[144,8192]{1,0:T(8,128)(2,1)}, bf16[144,8192]{1,0:T(8,128)(2,1)}, u32[]{:S(2)}, u32[]{:S(2)}) collective-permute-start(bf16[144,8192]{1,0:T(8,128)(2,1)} %get-tuple-element.75), channel_id=1, source_target_pairs={{0,1},{1,0},{2,3},{3,2},{4,5},{5,4},{6,7},{7,6}} | collective-permute-start | bytes 7077896 | tf_op jit(solution)/shard_map/ppermute | solution.py:646
  197.7 78.0 %collective-permute-start.14 = (bf16[144,8192]{1,0:T(8,128)(2,1)}, bf16[144,8192]{1,0:T(8,128)(2,1)}, u32[]{:S(2)}, u32[]{:S(2)}) collective-permute-start(bf16[144,8192]{1,0:T(8,128)(2,1)} %get-tuple-element.76), channel_id=1, source_target_pairs={{0,2},{1,3},{2,0},{3,1},{4,6},{5,7},{6,4},{7,5}} | collective-permute-start | bytes 7077896 | tf_op jit(solution)/shard_map/ppermute | solution.py:646
  275.7 0.6 copy-start.1
  275.7 0.6 copy-start.2
  275.7 0.6 copy-start.3

commit v5 on v4

--- a/solution.py
+++ b/solution.py
@@ -261,7 +261,7 @@
         pl.semaphore_wait(barrier, 1)
 
 
-def chip_sum(first, steps, share, out, keep, box, got, send_sem, recv_sem):
+def chip_sum(first, steps, share, outs, keep, box, got, send_sem, recv_sem):
     step = pl.program_id(0) - first
     neighbour = other_core()
 
@@ -275,14 +275,20 @@
 
     @pl.when((step >= 0) & (step < steps))
     def _():
-        counterpart, diagonal = share()
-        keep[step % 2] = counterpart
-        box[step % 2] = diagonal
+        at = 0
+        for mine, theirs in share():
+            keep[step % 2, at:at + mine.shape[0]] = mine
+            box[step % 2, at:at + mine.shape[0]] = theirs
+            at += mine.shape[0]
 
     @pl.when(step > 0)
     def _():
         copy(step - 1).wait()
-        out[...] = (keep[(step - 1) % 2] + got[(step - 1) % 2]).astype(BF16)
+        at = 0
+        for out in outs:
+            cut = slice(at, at + out.shape[0])
+            out[...] = (keep[(step - 1) % 2, cut] + got[(step - 1) % 2, cut]).astype(out.dtype)
+            at += out.shape[0]
 
 
 def chip_sum_scratch(rows, blk):
@@ -371,9 +377,9 @@
         rows = p0.shape[0]
         p0[...] = r[:rows].astype(BF16)
         p1[...] = r[rows:2 * rows].astype(BF16)
-        return r[2 * rows:3 * rows], r[3 * rows:]
-
-    chip_sum(first, steps, share, s2, *chip)
+        return [(r[2 * rows:3 * rows], r[3 * rows:])]
+
+    chip_sum(first, steps, share, [s2], *chip)
 
     @pl.when(step == first + steps)
     def _():
@@ -487,10 +493,10 @@
         for j, (part, h) in enumerate(zip(parts, (h0, h1, h2, h3))):
             inv = (inv_a, inv_b)[j // 2][(j % 2) * half:(j % 2 + 1) * half, :1]
             total = total + jnp.sum(part * (h[...].astype(F32) * inv), axis=0, keepdims=True)
-        gain[...] = total
-        return parts[2], parts[3]
-
-    chip_sum(first, steps, share, t2, *chip)
+        total = jnp.broadcast_to(total, gain.shape)
+        return [(parts[2], parts[3]), (total, total)]
+
+    chip_sum(first, steps, share, [t2, gain], *chip)
 
     @pl.when(step == first + steps)
     def _():
@@ -511,15 +517,15 @@
         functools.partial(backward_kernel, batch, heads_steps, steps), name="backward", grid=(first + steps + 1,),
         in_specs=[ANY] * 3 + [const_spec(x.shape) for x in (down, across)] + [ANY] * 3 + [now] * 4
         + [const_spec(x.shape) for x in (inv_a, inv_b)] + [ANY] * len(kept),
-        out_specs=[ANY] * 3 + [now, now, late, pl.BlockSpec((1, wide), lambda i: (0, clip(i - first, steps)))],
+        out_specs=[ANY] * 3 + [now, now, late, pl.BlockSpec((8, wide), lambda i: (0, clip(i - first - 1, steps)))],
         out_shape=[jax.ShapeDtypeStruct((tok, n), BF16) for n in (nq, nk, nk)] + [jax.ShapeDtypeStruct((half, width), BF16)] * 3
-        + [jax.ShapeDtypeStruct((1, width), F32)],
+        + [jax.ShapeDtypeStruct((8, width), F32)],
         scratch_shapes=like(*kept) + [pltpu.VMEM((tok, nq + 2 * nk), BF16)]
         + [pltpu.VMEM((2 * half, width), BF16), pltpu.VMEM((2 * half, nq), BF16), pltpu.VMEM((4, blk, width), BF16),
            pltpu.VMEM((3, wide, nq + 2 * nk), BF16),
            pltpu.SemaphoreType.DMA((2,)), pltpu.SemaphoreType.DMA((4,)), pltpu.SemaphoreType.DMA((3, 3)),
            pltpu.SemaphoreType.DMA((len(kept),)), pltpu.SemaphoreType.DMA((3,))]
-        + chip_sum_scratch(half, wide),
+        + chip_sum_scratch(half + 8, wide),
         compiler_params=comm_params(1), cost_estimate=cost(2 * tok * width * (2 * nq + 2 * nk), 4 * width * nq),
     )(ga, gb, w_out, down, across, wq, wk, wv, *h, inv_a, inv_b, *kept)
 
@@ -573,35 +579,35 @@
         out_shape=[jax.ShapeDtypeStruct((width, n), F32) for n in (nq, nk, nk)]
         + [jax.ShapeDtypeStruct((nq, width), F32), jax.ShapeDtypeStruct(h.shape, BF16)],
         scratch_shapes=[pltpu.VMEM((tok, nq), BF16), pltpu.VMEM((nq, tok), BF16), pltpu.SemaphoreType.DMA],
-        compiler_params=params(62), cost_estimate=cost(4 * tok * width * (nq + nk), 8 * width * (nq + nk)),
+        compiler_params=params(56), cost_estimate=cost(4 * tok * width * (nq + nk), 8 * width * (nq + nk)),
     )(na, nb, dq, dk, dv, o, *g, *p, h)
 
 
-def norm_back_kernel(d0, d1, d2, h, g, inv, gain, gg0, gg1, gg2, gg3, grad, grad_gain, *refs):
-    held, (out, dg, isem, esem) = refs[:5], refs[5:]
+def norm_back_kernel(d0, d1, d2, h, g, inv, gain, gg0, gg1, grad, grad_gain, *refs):
+    held, out, dg, isem, esem = refs
     rows, width = dg.shape
     count = out.shape[0] // rows
-    wide = 1024
+    wide = 512
 
     def at(i):
         return pl.ds(pl.multiple_of(i * rows, rows), rows)
 
-    def loads(i):
-        return [pltpu.make_async_copy(a.at[at(i)], b.at[at(i)], isem.at[j, i]) for j, (a, b) in enumerate(zip((d0, d1, d2, h, g), held))]
+    def load(i):
+        return pltpu.make_async_copy(d2.at[at(i)], held.at[at(i)], isem.at[i])
 
     def save(i):
         return pltpu.make_async_copy(out.at[at(i)], grad.at[at(i)], esem.at[i])
 
     @pl.loop(0, count)
     def _(i):
-        start_all(loads(i))
-
-    grad_gain[...] = (gg0[...] + gg1[...]) + (gg2[...] + gg3[...])
-    x0, x1, x2, hs, gs = held
+        load(i).start()
+
+    grad_gain[...] = gg0[0:1] + gg1[0:1]
+    x0, x1, x2, hs, gs = d0, d1, held, h, g
 
     @pl.loop(0, count)
     def _(i):
-        wait_all(loads(i))
+        load(i).wait()
         total = jnp.zeros((rows, wide), F32)
         for c in range(0, width, wide):
             cut = slice(c, c + wide)
@@ -624,15 +630,15 @@
 
 def norm_back(d, h, g, inv, gain, gain_shares):
     tok, width = h.shape
-    rows = 16
+    rows = 48
     count = tok // rows
     whole = pl.BlockSpec(memory_space=pltpu.VMEM)
     return pl.pallas_call(
-        norm_back_kernel, name="norm_back", in_specs=[ANY] * 5 + [whole] * 6, out_specs=[ANY, whole],
+        norm_back_kernel, name="norm_back", in_specs=[whole] * 2 + [ANY] + [whole] * 6, out_specs=[ANY, whole],
         out_shape=[jax.ShapeDtypeStruct((tok, width), BF16), jax.ShapeDtypeStruct((1, width), F32)],
-        scratch_shapes=[pltpu.VMEM((tok, width), BF16)] * 6
-        + [pltpu.VMEM((rows, width), F32), pltpu.SemaphoreType.DMA((5, count)), pltpu.SemaphoreType.DMA((count,))],
-        compiler_params=pltpu.CompilerParams(vmem_limit_bytes=62 << 20), cost_estimate=cost(20 * tok * width, 12 * tok * width),
+        scratch_shapes=[pltpu.VMEM((tok, width), BF16)] * 2
+        + [pltpu.VMEM((rows, width), F32), pltpu.SemaphoreType.DMA((count,)), pltpu.SemaphoreType.DMA((count,))],
+        compiler_params=pltpu.CompilerParams(vmem_limit_bytes=20 << 20), cost_estimate=cost(20 * tok * width, 12 * tok * width),
     )(*d, h, g, inv, gain, *gain_shares)
 
 
@@ -640,7 +646,6 @@
     tp_size = mesh.shape['tp']
     beside = [(i, i ^ 1) for i in range(tp_size)]
     across = [(i, i ^ 2) for i in range(tp_size)]
-    diagonal = [(i, i ^ 3) for i in range(tp_size)]
 
     def send(x, pairs):
         return lax.ppermute(x, 'tp', pairs)
@@ -691,9 +696,9 @@
         t2, d1, gg, dq = lax.optimization_barrier((t2, d1, gg, dq))
         t2 = send(t2, across)
         d1 = send(d1, beside)
-        gg1, gg2, gg3 = send(gg, beside), send(gg, across), send(gg, diagonal)
+        gg2 = send(gg, across)
         gq, gk, gv, g_out, attn_out = weight_grads(na, nb, dq, dk, dv, o, (g0, g1, g2, g3), (p0, p1, s2), h0)
-        grad_hidden, gg = norm_back((after(d0, gk), d1, t2), h0, g0, inv_a[:tok], gain, (gg, gg1, gg2, gg3))
+        grad_hidden, gg = norm_back((after(d0, gk), d1, t2), h0, g0, inv_a[:tok], gain, (gg, gg2))
         grad_gain = gg.reshape(width)
         attn_out, grad_hidden = attn_out.reshape(hidden.shape), grad_hidden.reshape(hidden.shape)
         return (attn_out, grad_hidden, grad_gain, gq, gk, gv, g_out)

time: 285 us -> 281 us (0.986)
    ppermute x18 -> x16, starting transfers between devices: 11.7 us -> 9.93 us  [send(): return lax.ppermute(x, 'tp', pairs)]
    ppermute x18 -> x16, waiting for transfers between devices: 30 us -> 29.9 us  [send(): return lax.ppermute(x, 'tp', pairs)]
  transfers between devices with their start and end apart: 18 -> 16, of which waited for: 3 -> 3; matrix products, arithmetic and copies ran while one was open for 3% -> 3% of each run, Pallas kernels for 79% -> 80%
where the time goes in v5:
time: 281 us
  Pallas kernels  233 us (83%)
  waiting for transfers between devices  29.9 us (11%)
  starting transfers between devices  9.93 us (4%)
  other arithmetic  5.82 us (2%)
    pallas_call x1, Pallas kernels, weight_grads(): pl.pallas_call(functools.partial(weight_grads_kernel, steps), name='weigh...  76.4 us
    pallas_call x1, Pallas kernels, backward(): pl.pallas_call(functools.partial(backward_kernel, batch, heads_steps, ste...  59 us
    pallas_call x1, Pallas kernels, forward(): pl.pallas_call(functools.partial(forward_kernel, batch, first, steps), na...  52.2 us
    ppermute x16, waiting for transfers between devices, send(): return lax.ppermute(x, 'tp', pairs)  29.9 us
    pallas_call x1, Pallas kernels, qkv(): pl.pallas_call(qkv_kernel, name='qkv', grid=(nq // blk + 1,), in_specs=[A...  22 us
    pallas_call x1, Pallas kernels, heads_grad(): pl.pallas_call(functools.partial(heads_grad_kernel, steps), name='heads_g...  15.8 us
    ppermute x16, starting transfers between devices, send(): return lax.ppermute(x, 'tp', pairs)  9.93 us
    pallas_call x1, Pallas kernels, norm_back(): pl.pallas_call(norm_back_kernel, name='norm_back', in_specs=[whole] * 2 +...  7.09 us
  transfers between devices with their start and end apart: 16, of which 3 were waited for; matrix products, arithmetic and copies ran while one was open for 3% of the time, Pallas kernels for 80%

profile of v5, /device:TPU:0, one launch (start us, length us, event | category | flops | bytes accessed | tf_op | source)
XLA Modules:
  0.0 280.7 jit_solution(18311624871784250811)
XLA Ops:
  0.6 0.9 collective-permute-start
  1.5 0.0 collective-permute-start.1
  1.5 2.9 %collective-permute-start.3 = (s32[3,48]{1,0:T(4,128)}, s32[3,48]{1,0:T(4,128)S(1)}, u32[]{:S(2)}, u32[]{:S(2)}) collective-permute-start(s32[3,48]{1,0:T(4,128)} %param.10), channel_id=1, source_target_pairs={{0,2},{1,3},{2,0},{3,1},{4,6},{5,7},{6,4},{7,5}} | collective-permute-start | bytes 1736 | tf_op jit(solution)/shard_map/ppermute | solution.py:651
  4.5 0.0 collective-permute-start.2
  4.5 2.0 collective-permute-start.4
  6.5 1.3 reshape.116
  7.8 0.0 collective-permute-done.1
  7.9 0.7 add_convert_fusion
  8.5 0.1 convert_element_type.31
  8.6 1.3 fusion
  9.9 0.0 collective-permute-done.hb.h1
  9.9 22.0 %qkv.1 = (bf16[288,8192]{1,0:T(8,128)(2,1)}, f32[288,128]{1,0:T(8,128)}, bf16[288,2048]{1,0:T(8,128)(2,1)}, bf16[288,256]{1,0:T(8,128)(2,1)}, bf16[288,256]{1,0:T(8,128)(2,1)}) custom-call(bf16[144,8192]{1,0:T(8,128)(2,1)} %bitcast.24, bf16[144,8192]{1,0:T(8,128)(2,1)} %collective-permute-done.hb.h1, f32[1,8192]{1,0:T(1,128)} %bitcast.33, ...), custom_call_target="tpu_custom_call" | custom-call | flops 12079595520 | bytes 41943040 | tf_op jit(solution)/shard_map/qkv/pallas_call | solution.py:137
  31.9 0.0 collective-permute-done.3
  31.9 25.8 %collective-permute-done.4 = s32[3,48]{1,0:T(4,128)S(1)} collective-permute-done((s32[3,48]{1,0:T(4,128)}, s32[3,48]{1,0:T(4,128)S(1)}, u32[]{:S(2)}, u32[]{:S(2)}) %collective-permute-start.4) | collective-permute-done | bytes 608 | tf_op jit(solution)/shard_map/ppermute | solution.py:651
  57.7 0.5 collective-permute-start.6
  58.2 0.0 collective-permute-start.10
  58.2 0.3 collective-permute-start.8
  58.6 0.3 collective-permute-done.5
  58.9 0.2 collective-permute-start.7
  59.1 0.1 add_bitcast_fusion.1
  59.1 0.2 copy.24
  59.3 3.8 %collective-permute-done.7 = s32[3,48]{1,0:T(4,128)S(1)} collective-permute-done((s32[3,48]{1,0:T(4,128)S(1)}, s32[3,48]{1,0:T(4,128)S(1)}, u32[]{:S(2)}, u32[]{:S(2)}) %collective-permute-start.7) | collective-permute-done | bytes 608 | tf_op jit(solution)/shard_map/ppermute | solution.py:651
  63.1 0.1 add_bitcast_fusion
  63.2 0.2 copy.23
  63.4 0.1 pad_add_fusion
  63.5 0.1 copy.25
  63.7 0.7 tile.10.across.refs_4_
  64.4 0.1 convert_element_type.34
  64.5 0.9 fusion.7.down.refs_3_
  65.4 1.3 fusion.1
  66.7 52.2 %forward.1 = (bf16[288,8192]{1,0:T(8,128)(2,1)}, f32[288,128]{1,0:T(8,128)}, bf16[288,2048]{1,0:T(8,128)(2,1)}, bf16[288,256]{1,0:T(8,128)(2,1)}, bf16[288,256]{...) custom-call(bf16[144,8192]{1,0:T(8,128)(2,1)} %collective-permute-do, ...), custom_call_target="tpu_custom_call" | custom-call | flops 31406948352 | bytes 67108864 | tf_op jit(solution)/shard_map/forward/pallas_call | solution.py:399
  118.9 0.0 collective-permute-done.8.ga.g2
  118.9 0.4 collective-permute-start.9
  119.3 0.2 collective-permute-start.11
  119.5 0.3 collective-permute-start.12
  119.8 15.8 %heads_grad.1.refs_0_ = bf16[288,2048]{1,0:T(8,128)(2,1)} custom-call(bf16[144,8192]{1,0:T(8,128)(2,1)} %bitcast.30, bf16[144,8192]{1,0:T(8,128)(2,1)} %collective-permute-done.10.gb.g1, bf16[2048,8192]{1,0:T(8,128)(2,1)} %w_out.3, bf16[288,256]{1,0:T(8,128)(2,1)} %get-tuple-element.49.ka_in.refs_0_.refs_3_, ...), custom_call_target="tpu_custom_call" | custom-call | flops 9663676416 | bytes 33554432 | tf_op jit(solution)/shard_map/heads_grad/pallas_call | solution.py:180
  135.7 0.0 collective-permute-done.9.gb.g3
  135.7 59.0 %backward.1 = (bf16[576,2048]{1,0:T(8,128)(2,1)}, bf16[576,256]{1,0:T(8,128)(2,1)}, bf16[576,256]{1,0:T(8,128)(2,1)}, bf16[144,8192]{1,0:T(8,128)(2,1)}, bf16[14...) custom-call(bf16[144,8192]{1,0:T(8,128)(2,1)} %collective-permute-done.8.ga.g2, ...), custom_call_target="tpu_custom_call" | custom-call | flops 43486543872 | bytes 67108864 | tf_op jit(solution)/shard_map/backward/pallas_call | solution.py:516
  194.7 0.2 collective-permute-start.13
  194.9 1.7 collective-permute-start.14
  196.6 0.3 collective-permute-start.15
  196.9 0.0 collective-permute-done.12.p2
  196.9 0.0 copy-start.1
  197.0 0.0 copy-start.3
  197.0 76.4 %weight_grads.1 = (f32[8192,2048]{1,0:T(8,128)}, f32[8192,256]{1,0:T(8,128)}, f32[8192,256]{1,0:T(8,128)}, f32[2048,8192]{1,0:T(8,128)}, bf16[144,8192]{1,0:T(8,128)(2,1)}) custom-call(bf16[288,8192]{1,0:T(8,128)(2,1)} %get-tuple-element.45.na, bf16[288,8192]{1,0:T(8,128)(2,1)} %get-tuple-element.52.nb, bf16[576,2048]{1,0:T(8,128)(2,1)} %get-tuple-element.65.dq, ...), custom_call_target="tpu_custom_call" | custom-call | flops 43486543872 | bytes 150994944 | tf_op jit(solution)/shard_map/weight_grads/pallas_call | solution.py:574
  273.4 0.0 collective-permute-done.15.gg1
  273.4 0.0 collective-permute-done.14.d2
  273.5 7.1 %norm_back.1 = (bf16[144,8192]{1,0:T(8,128)(2,1)}, f32[1,8192]{1,0:T(1,128)}) custom-call(bf16[144,8192]{1,0:T(8,128)(2,1)S(1)} %copy-done.2, bf16[144,8192]{1,0:T(8,128)(2,1)} %collective-permute-done.13.d1, bf16[144,8192]{1,0:T(8,128)(2,1)} %collective-permute-done.14.d2, bf16[144,8192]{1,0:T(8,128)(2,1)S(1)} %bitcast.27, bf16[144,8192]{1,0:T(8,128)(2,1)S(1)} %bitcast.32, ...), custom_call_target="tpu_custom_call" | custom-call | flops 23592960 | bytes 14155776 | tf_op jit(solution)/shard_map/norm_back/pallas_call | solution.py:636
  (24 shorter events, 0.1 us)
Async XLA Ops:
  0.6 9.3 %collective-permute-start = (bf16[144,8192]{1,0:T(8,128)(2,1)}, bf16[144,8192]{1,0:T(8,128)(2,1)}, u32[]{:S(2)}, u32[]{:S(2)}) collective-permute-start(bf16[144,8192]{1,0:T(8,128)(2,1)} %bitcast.22), channel_id=1, source_target_pairs={{0,1},{1,0},{2,3},{3,2},{4,5},{5,4},{6,7},{7,6}} | collective-permute-start | bytes 7077896 | tf_op jit(solution)/shard_map/ppermute | solution.py:651
  1.5 6.4 %collective-permute-start.1 = (s32[3,48]{1,0:T(4,128)}, s32[3,48]{1,0:T(4,128)S(1)}, u32[]{:S(2)}, u32[]{:S(2)}) collective-permute-start(s32[3,48]{1,0:T(4,128)} %param.10), channel_id=1, source_target_pairs={{0,1},{1,0},{2,3},{3,2},{4,5},{5,4},{6,7},{7,6}} | collective-permute-start | bytes 1736 | tf_op jit(solution)/shard_map/ppermute | solution.py:651
  1.5 30.4 %collective-permute-start.3 = (s32[3,48]{1,0:T(4,128)}, s32[3,48]{1,0:T(4,128)S(1)}, u32[]{:S(2)}, u32[]{:S(2)}) collective-permute-start(s32[3,48]{1,0:T(4,128)} %param.10), channel_id=1, source_target_pairs={{0,2},{1,3},{2,0},{3,1},{4,6},{5,7},{6,4},{7,5}} | collective-permute-start | bytes 1736 | tf_op jit(solution)/shard_map/ppermute | solution.py:651
  4.5 62.2 %collective-permute-start.2 = (bf16[144,8192]{1,0:T(8,128)(2,1)}, bf16[144,8192]{1,0:T(8,128)(2,1)}, u32[]{:S(2)}, u32[]{:S(2)}) collective-permute-start(bf16[144,8192]{1,0:T(8,128)(2,1)} %bitcast.23), channel_id=1, source_target_pairs={{0,2},{1,3},{2,0},{3,1},{4,6},{5,7},{6,4},{7,5}} | collective-permute-start | bytes 7077896 | tf_op jit(solution)/shard_map/ppermute | solution.py:651
  4.5 53.2 %collective-permute-start.4 = (s32[3,48]{1,0:T(4,128)}, s32[3,48]{1,0:T(4,128)S(1)}, u32[]{:S(2)}, u32[]{:S(2)}) collective-permute-start(s32[3,48]{1,0:T(4,128)} %param.11), channel_id=1, source_target_pairs={{0,2},{1,3},{2,0},{3,1},{4,6},{5,7},{6,4},{7,5}} | collective-permute-start | bytes 1736 | tf_op jit(solution)/shard_map/ppermute | solution.py:651
  9.9 47.8 %copy-start.7 = (s32[3,48]{1,0:T(4,128)S(1)}, s32[3,48]{1,0:T(4,128)}, u32[]{:S(2)}) copy-start(s32[3,48]{1,0:T(4,128)} %param.11) | copy-start | bytes 1732
  9.9 49.1 %copy-start.6 = (s32[3,48]{1,0:T(4,128)S(1)}, s32[3,48]{1,0:T(4,128)}, u32[]{:S(2)}) copy-start(s32[3,48]{1,0:T(4,128)} %param.10) | copy-start | bytes 1732
  57.7 1.2 collective-permute-start.5
  57.7 1.6 collective-permute-start.6
  58.2 61.6 %collective-permute-start.10 = (bf16[144,8192]{1,0:T(8,128)(2,1)}, bf16[144,8192]{1,0:T(8,128)(2,1)}, u32[]{:S(2)}, u32[]{:S(2)}) collective-permute-start(bf16[144,8192]{1,0:T(8,128)(2,1)} %bitcast.28), channel_id=1, source_target_pairs={{0,1},{1,0},{2,3},{3,2},{4,5},{5,4},{6,7},{7,6}} | collective-permute-start | bytes 7077896 | tf_op jit(solution)/shard_map/ppermute | solution.py:651
  58.2 60.7 %collective-permute-start.8 = (bf16[144,8192]{1,0:T(8,128)(2,1)}, bf16[144,8192]{1,0:T(8,128)(2,1)}, u32[]{:S(2)}, u32[]{:S(2)}) collective-permute-start(bf16[144,8192]{1,0:T(8,128)(2,1)} %bitcast.29), channel_id=1, source_target_pairs={{0,2},{1,3},{2,0},{3,1},{4,6},{5,7},{6,4},{7,5}} | collective-permute-start | bytes 7077896 | tf_op jit(solution)/shard_map/ppermute | solution.py:651
  58.9 4.2 %collective-permute-start.7 = (s32[3,48]{1,0:T(4,128)S(1)}, s32[3,48]{1,0:T(4,128)S(1)}, u32[]{:S(2)}, u32[]{:S(2)}) collective-permute-start(s32[3,48]{1,0:T(4,128)S(1)} %collective-permute-done.4), channel_id=1, source_target_pairs={{0,1},{1,0},{2,3},{3,2},{4,5},{5,4},{6,7},{7,6}} | collective-permute-start | bytes 1736 | tf_op jit(solution)/shard_map/ppermute | solution.py:651
  66.7 52.7 %copy-start.5 = (f32[288,128]{1,0:T(8,128)S(1)}, f32[288,128]{1,0:T(8,128)}, u32[]{:S(2)}) copy-start(f32[288,128]{1,0:T(8,128)} %get-tuple-element.56.inv_a) | copy-start | bytes 442372
  118.9 16.7 %collective-permute-start.9 = (bf16[144,8192]{1,0:T(8,128)(2,1)}, bf16[144,8192]{1,0:T(8,128)(2,1)}, u32[]{:S(2)}, u32[]{:S(2)}) collective-permute-start(bf16[144,8192]{1,0:T(8,128)(2,1)} %collective-permute-done.8.ga.g2), channel_id=1, source_target_pairs={{0,1},{1,0},{2,3},{3,2},{4,5},{5,4},{6,7},{7,6}} | collective-permute-start | bytes 7077896 | tf_op jit(solution)/shard_map/ppermute | solution.py:651
  119.3 77.6 %collective-permute-start.11 = (bf16[144,8192]{1,0:T(8,128)(2,1)}, bf16[144,8192]{1,0:T(8,128)(2,1)}, u32[]{:S(2)}, u32[]{:S(2)}) collective-permute-start(bf16[144,8192]{1,0:T(8,128)(2,1)} %get-tuple-element.69), channel_id=1, source_target_pairs={{0,1},{1,0},{2,3},{3,2},{4,5},{5,4},{6,7},{7,6}} | collective-permute-start | bytes 7077896 | tf_op jit(solution)/shard_map/ppermute | solution.py:651
  119.5 77.4 %collective-permute-start.12 = (bf16[144,8192]{1,0:T(8,128)(2,1)}, bf16[144,8192]{1,0:T(8,128)(2,1)}, u32[]{:S(2)}, u32[]{:S(2)}) collective-permute-start(bf16[144,8192]{1,0:T(8,128)(2,1)} %get-tuple-element.70), channel_id=1, source_target_pairs={{0,2},{1,3},{2,0},{3,1},{4,6},{5,7},{6,4},{7,5}} | collective-permute-start | bytes 7077896 | tf_op jit(solution)/shard_map/ppermute | solution.py:651
  194.7 78.7 %collective-permute-start.13 = (bf16[144,8192]{1,0:T(8,128)(2,1)}, bf16[144,8192]{1,0:T(8,128)(2,1)}, u32[]{:S(2)}, u32[]{:S(2)}) collective-permute-start(bf16[144,8192]{1,0:T(8,128)(2,1)} %get-tuple-element.75), channel_id=1, source_target_pairs={{0,1},{1,0},{2,3},{3,2},{4,5},{5,4},{6,7},{7,6}} | collective-permute-start | bytes 7077896 | tf_op jit(solution)/shard_map/ppermute | solution.py:651
  194.9 78.5 %collective-permute-start.14 = (bf16[144,8192]{1,0:T(8,128)(2,1)}, bf16[144,8192]{1,0:T(8,128)(2,1)}, u32[]{:S(2)}, u32[]{:S(2)}) collective-permute-start(bf16[144,8192]{1,0:T(8,128)(2,1)} %get-tuple-element.76), channel_id=1, source_target_pairs={{0,2},{1,3},{2,0},{3,1},{4,6},{5,7},{6,4},{7,5}} | collective-permute-start | bytes 7077896 | tf_op jit(solution)/shard_map/ppermute | solution.py:651
  196.6 76.8 %collective-permute-start.15 = (f32[8,8192]{1,0:T(8,128)}, f32[8,8192]{1,0:T(8,128)S(1)}, u32[]{:S(2)}, u32[]{:S(2)}) collective-permute-start(f32[8,8192]{1,0:T(8,128)} %get-tuple-element.77.gg0), channel_id=1, source_target_pairs={{0,2},{1,3},{2,0},{3,1},{4,6},{5,7},{6,4},{7,5}} | collective-permute-start | bytes 786440 | tf_op jit(solution)/shard_map/ppermute | solution.py:651
  196.9 76.5 %copy-start = (bf16[3,48,8192]{2,1,0:T(8,128)(2,1)S(1)}, bf16[3,48,8192]{2,1,0:T(8,128)(2,1)}, u32[]{:S(2)}) copy-start(bf16[3,48,8192]{2,1,0:T(8,128)(2,1)} %param.9) | copy-start | bytes 7077892
  196.9 76.5 %copy-start.1 = (bf16[3,48,8192]{2,1,0:T(8,128)(2,1)S(1)}, bf16[3,48,8192]{2,1,0:T(8,128)(2,1)}, u32[]{:S(2)}) copy-start(bf16[3,48,8192]{2,1,0:T(8,128)(2,1)} %param.17) | copy-start | bytes 7077892
  196.9 76.5 %copy-start.2 = (bf16[144,8192]{1,0:T(8,128)(2,1)S(1)}, bf16[144,8192]{1,0:T(8,128)(2,1)}, u32[]{:S(2)}) copy-start(bf16[144,8192]{1,0:T(8,128)(2,1)} %get-tuple-element.74.d0) | copy-start | bytes 7077892
  197.0 76.5 %copy-start.3 = (f32[8192]{0:T(1024)S(1)}, f32[8192]{0:T(1024)}, u32[]{:S(2)}) copy-start(f32[8192]{0:T(1024)} %reshape.116) | copy-start | bytes 98308
  197.0 76.5 %copy-start.4 = (f32[8,8192]{1,0:T(8,128)S(1)}, f32[8,8192]{1,0:T(8,128)}, u32[]{:S(2)}) copy-start(f32[8,8192]{1,0:T(8,128)} %get-tuple-element.77.gg0) | copy-start | bytes 786436
